TPU v7x, 256 devices: a whole 4x4x8 slice. The times are simulated.
256 devices in a mesh: samp: 64 (over z_hi, x, y), cls: 4 (over z_lo, core).
Axes of the slice: x: 4, y: 4, z: 8 (z_hi: 4, z_lo: 2; z = z_hi * 2 + z_lo), core: 2. Of those that a mesh axis runs over, the one named last changes fastest.
Arguments:
- samples: bfloat16 [8192, 32768], P('samp'), may hold values from -0.09375 to 0.09375
- labels: int32 [8192], P('samp'), may hold values from 0 to 511
- weight: bfloat16 [32768, 512], P('samp', 'cls'), may hold values from -6 to 6
- dual: float32 [8192, 512], P('samp', 'cls'), may hold values from 0 to 1
- block_inverse: float32 [512, 16, 16], P('samp'), may hold values from -0.4 to 1.2, as said below
Outputs:
- new_weight: float32 [32768, 512], P('samp', 'cls')
- new_dual: float32 [8192, 512], P('samp', 'cls')
- class_gap: float32 [512], P('cls')
- top_margin: float32 [8192], P('samp')
Inputs may be any that keep to these rules, and one draw needn't show every extreme that they name: `block_inverse`: each [16, 16] matrix has a positive diagonal.
All inputs are finite; a program needn't handle non-finite values.
Results may differ from a plain program's by a relative error of at most 0.00045.
Values may be sent and summed in bfloat16 or wider, within the bound.
No kernel may reach another device: no remote copies, remote signals or barrier semaphores. Data moves between devices by JAX's collectives and lax.ppermute only.
A program may use at most 128 MiB of HBM per device.

v0:
```python
import jax
import jax.numpy as jnp
from jax import lax
from jax.sharding import PartitionSpec as P

BLOCK = 16
PASSES = 2


coupling = 0.5


def from_everyone(value, axis):
    copies = jnp.broadcast_to(value, (lax.axis_size(axis), *value.shape))
    return lax.all_to_all(copies, axis, split_axis=0, concat_axis=0, tiled=True)


def taken_together(value, axis):
    everything = from_everyone(value, axis)
    return jnp.sum(everything, axis=0)


def over_copies(value, axis):
    everything = from_everyone(value, axis)
    return jnp.max(everything, axis=0)


def dual_passes(gram, start, sign, dual, inverse):
    rows = start.shape[0]
    blocks = rows // BLOCK

    def visit(turn, carry):
        alpha, change = carry
        index = (turn % blocks).astype(jnp.int32)
        low = index * BLOCK
        gram_rows = lax.dynamic_slice_in_dim(gram, low, BLOCK, 0)
        start_rows = lax.dynamic_slice_in_dim(start, low, BLOCK, 0)
        sign_rows = lax.dynamic_slice_in_dim(sign, low, BLOCK, 0)
        dual_rows = lax.dynamic_slice_in_dim(dual, low, BLOCK, 0)
        alpha_rows = lax.dynamic_slice_in_dim(alpha, low, BLOCK, 0)
        matrix = lax.dynamic_index_in_dim(inverse, index, 0, keepdims=False)
        margin = start_rows + coupling * jnp.dot(gram_rows, change, precision=lax.Precision.HIGHEST)
        ascent = jnp.dot(matrix, 1.0 - sign_rows * margin, precision=lax.Precision.HIGHEST)
        alpha_rows = jnp.clip(alpha_rows + ascent, 0.0, 1.0)
        change_rows = sign_rows * (alpha_rows - dual_rows)
        alpha = lax.dynamic_update_slice_in_dim(alpha, alpha_rows, low, 0)
        change = lax.dynamic_update_slice_in_dim(change, change_rows, low, 0)
        return (alpha, change)

    alpha, change = lax.fori_loop(0, PASSES * blocks, visit, (dual, jnp.zeros_like(dual)))
    margin = start + coupling * jnp.dot(gram, change, precision=lax.Precision.HIGHEST)
    return (alpha, margin, change)


def body(samples, labels, weight, dual, block_inverse):
    rows, features = samples.shape
    width = weight.shape[1]
    class_ids = lax.axis_index("cls") * width + jnp.arange(width, dtype=jnp.int32)
    sign = jnp.where(labels[:, None] == class_ids[None, :], 1.0, -1.0).astype(jnp.float32)
    start = jnp.dot(
        samples,
        lax.all_gather(weight, "samp", axis=0, tiled=True),
        preferred_element_type=jnp.float32,
    )
    gram = lax.dot_general(
        samples, samples, (((1,), (1,)), ((), ())), preferred_element_type=jnp.float32
    )
    scaled = sign * start
    terms = jnp.maximum(0.0, 1.0 - scaled) + dual * (scaled - 1.0)
    class_gap = taken_together(jnp.sum(terms, axis=0), "samp") / (rows * lax.axis_size("samp"))
    alpha, margin, change = dual_passes(gram, start, sign, dual, block_inverse)
    top_margin = over_copies(jnp.max(margin, axis=1), "cls")
    steps = change.astype(jnp.bfloat16)
    regrouped = lax.all_to_all(samples, "samp", split_axis=1, concat_axis=0, tiled=True)
    every_step = lax.all_gather(steps, "samp", axis=0, tiled=True)
    delta = lax.dot_general(
        regrouped, every_step, (((0,), (0,)), ((), ())), preferred_element_type=jnp.float32
    )
    new_weight = weight.astype(jnp.float32) + coupling * delta
    return (new_weight, alpha, class_gap, top_margin)


def solution(mesh):
    placed = (P("samp", None), P("samp"), P("samp", "cls"), P("samp", "cls"), P("samp", None, None))
    return jax.shard_map(
        body,
        mesh=mesh,
        in_specs=placed,
        out_specs=(P("samp", "cls"), P("samp", "cls"), P("cls"), P("samp")),
        check_vma=False,
    )
```

profile of v0, /device:TPU:2, one launch (start us, length us, event | category | flops | bytes accessed | tf_op | source)
XLA Modules:
  0.0 397.1 jit_solution(15759915740206989065)
XLA Ops:
  7.9 11.9 %copy.26 = bf16[128,32768]{0,1:T(8,128)(2,1)} copy(bf16[128,32768]{1,0:T(8,128)(2,1)} %param.7) | data formatting | bytes 16777216 | tf_op args[0]
  19.8 15.0 %all-to-all-start = ((bf16[128,64,512]{0,2,1:T(8,128)(2,1)}), bf16[128,64,512]{0,2,1:T(8,128)(2,1)}, u32[]{:S(2)}, u32[]{:S(2)}) async-start(bf16[128,64,512]{0,2,1:T(8,128)(2,1)} %bitcast.29), calls=%async_computation | async-start | bytes 16777216 | tf_op jit(solution)/shard_map/all_to_all | solution.py:74
  34.9 8.1 %fusion.13 = f32[128,128]{1,0:T(8,128)S(1)} fusion(bf16[128,32768]{1,0:T(8,128)(2,1)} %param.7), kind=kOutput, calls=%fused_computation.23 | convolution fusion | flops 1073741824 | bytes 8454144 | tf_op jit(solution)/shard_map/dot_general | solution.py:65
  43.1 234.0 %all-gather.3.cloned.1.call-done = bf16[32768,128]{1,0:T(8,128)(2,1)} async-done(((bf16[512,128]{1,0:T(8,128)(2,1)}), bf16[32768,128]{1,0:T(8,128)(2,1)}) %all-gather.3.cloned.1.call-update) | async-done | bytes 8388624 | tf_op jit(solution)/shard_map/all_gather | solution.py:62
  277.1 8.1 %add_reduce_fusion = (f32[128]{0:T(128)S(1)}, f32[128,128]{1,0:T(8,128)S(1)}, f32[128,128]{1,0:T(8,128)S(1)}) fusion(f32[128,128]{1,0:T(8,128)S(1)} %copy-done.1, s32[128]{0:T(128)S(1)} %iota_add_fusion, s32[128]{0:T(128)S(1)} %copy-done.3, bf16[128,32768]{1,0:T(8,128)(2,1)} %param.7, bf16[32768,128]{1,0:T(8,128)(2,1)} %all-gather.3.cloned.1.call-done), kind=kOutput, calls=%fused_computation.19 | convolution fusion | flops 1073889152 | bytes 16975360 | tf_op jit(solution)/shard_map/dot_general | solution.py:60
  285.2 16.8 %while.17 = (s32[]{:T(128)}, f32[128,128]{1,0:T(8,128)S(1)}, f32[128,128]{1,0:T(8,128)S(1)}, f32[8,16,16]{2,1,0:T(8,128)}, f32[128,128]{1,0:T(8,128)S(1)}, /*ind...) while((s32[]{:T(128)}, f32[128,128]{1,0:T(8,128)S(1)}, ...), condition=%wide.region_1.2_spmd, body=%wide.region_0.1_spmd.sunk | while | flops 3555343 | bytes 173339 | solution.py:50
  285.4 0.8 fusion.35
  286.5 0.8 fusion.35
  287.5 0.8 fusion.35
  288.6 0.8 fusion.35
  289.6 0.8 fusion.35
  290.7 0.8 fusion.35
  291.7 0.8 fusion.35
  292.8 0.8 fusion.35
  294.9 0.8 fusion.35
  297.0 0.8 fusion.35
  298.0 0.8 fusion.35
  300.1 0.8 fusion.35
  303.0 6.1 %all_to_all.31 = f32[4,1,128]{2,1,0:T(1,128)S(1)} all-to-all(f32[4,1,128]{2,1,0:T(1,128)S(1)} %broadcast_in_dim.19), channel_id=1, replica_groups=mesh['samp'=64,'cls'=4] {'cls'}, dimensions={0} | all-to-all | bytes 4096 | tf_op jit(solution)/shard_map/all_to_all | solution.py:15
  309.7 14.2 %all-to-all-start.1 = ((f32[64,1,128]{2,1,0:T(1,128)}), f32[64,1,128]{2,1,0:T(1,128)S(1)}, u32[]{:S(2)}, u32[]{:S(2)}) async-start(f32[64,1,128]{2,1,0:T(1,128)} %broadcast_in_dim.18), calls=%async_computation.1 | async-start | bytes 65536 | tf_op jit(solution)/shard_map/all_to_all | solution.py:15
  324.1 12.0 %copy.27 = bf16[64,128,512]{2,1,0:T(8,128)(2,1)} copy(bf16[64,128,512]{1,2,0:T(8,128)(2,1)} %bitcast.2) | data formatting | bytes 16777216 | tf_op jit(solution)/shard_map/all_to_all | solution.py:74
  337.1 47.0 %all-gather.5.cloned.1.call-done = bf16[8192,128]{1,0:T(8,128)(2,1)} async-done(((bf16[128,128]{1,0:T(8,128)(2,1)}), bf16[8192,128]{1,0:T(8,128)(2,1)}) %all-gather.5.cloned.1.call-update) | async-done | bytes 2097168 | tf_op jit(solution)/shard_map/all_gather | solution.py:75
  384.1 5.3 %fusion.10 = f32[512,128]{0,1:T(8,128)S(1)} fusion(bf16[8192,128]{1,0:T(8,128)(2,1)} %all-gather.5.cloned.1.call-done, bf16[8192,512]{1,0:T(8,128)(2,1)} %bitcast.28, bf16[512,128]{0,1:T(8,128)(2,1)S(1)} %copy.25), kind=kOutput, calls=%fused_computation.15 | convolution fusion | flops 1073938432 | bytes 10878976 | tf_op jit(solution)/shard_map/dot_general | solution.py:76
  389.5 0.8 copy.31
  (61 shorter events, 9.8 us)
Async XLA Ops:
  7.2 269.9 %all-gather.3.cloned.1.call-start = ((), (), s32[]{:S(2)}) async-start(), calls=%async_computation.3 | async-start | bytes 8519680 | tf_op jit(solution)/shard_map/all_gather | solution.py:62
  19.8 15.0 %copy-start.1 = (f32[128,128]{1,0:T(8,128)S(1)}, f32[128,128]{1,0:T(8,128)}, u32[]{:S(2)}) copy-start(f32[128,128]{1,0:T(8,128)} %param.10) | copy-start | bytes 196612
  19.8 283.1 %all-to-all-start = ((bf16[128,64,512]{0,2,1:T(8,128)(2,1)}), bf16[128,64,512]{0,2,1:T(8,128)(2,1)}, u32[]{:S(2)}, u32[]{:S(2)}) async-start(bf16[128,64,512]{0,2,1:T(8,128)(2,1)} %bitcast.29), calls=%async_computation | async-start | bytes 16777216 | tf_op jit(solution)/shard_map/all_to_all | solution.py:74
  34.8 349.3 %all-gather.5.cloned.1.call-start = ((), (), s32[]{:S(2)}) async-start(), calls=%async_computation.4 | async-start | bytes 2129920 | tf_op jit(solution)/shard_map/all_gather | solution.py:75
  34.9 242.2 %copy-start.3 = (s32[128]{0:T(128)S(1)}, s32[128]{0:T(128)}, u32[]{:S(2)}) copy-start(s32[128]{0:T(128)} %param.8) | copy-start | bytes 1540
  43.0 280.9 %copy-start = (bf16[512,128]{1,0:T(8,128)(2,1)S(1)}, bf16[512,128]{1,0:T(8,128)(2,1)}, u32[]{:S(2)}) copy-start(bf16[512,128]{1,0:T(8,128)(2,1)} %param.9) | copy-start | bytes 393220
  302.0 34.0 %copy-start.2 = (f32[128,128]{1,0:T(8,128)}, f32[128,128]{1,0:T(8,128)S(1)}, u32[]{:S(2)}) copy-start(f32[128,128]{1,0:T(8,128)S(1)} %get-tuple-element.223) | copy-start | bytes 196612
  309.7 26.9 %all-to-all-start.1 = ((f32[64,1,128]{2,1,0:T(1,128)}), f32[64,1,128]{2,1,0:T(1,128)S(1)}, u32[]{:S(2)}, u32[]{:S(2)}) async-start(f32[64,1,128]{2,1,0:T(1,128)} %broadcast_in_dim.18), calls=%async_computation.1 | async-start | bytes 65536 | tf_op jit(solution)/shard_map/all_to_all | solution.py:15
Sparse Core Ops, SparseCore 0:
  11.3 265.7 all-gather.2
  302.8 81.2 all-gather.4
where the time goes:
time: 399 us; the launch traced here: 397 us
  waiting for transfers between devices  282 us (71%)
  matrix products  38 us (10%)
  starting transfers between devices  29.3 us (7%)
  local copies, waits for them, and re-layouts  25.5 us (6%)
  between operations  14.2 us (4%)
  blocking collectives  6.12 us (2%)
    all_gather x1, waiting for transfers between devices, body(): lax.all_gather(weight, 'samp', axis=0, tiled=True)  234 us
    all_gather x1, waiting for transfers between devices, body(): every_step = lax.all_gather(steps, 'samp', axis=0, tiled=True)  47 us
    all_to_all x1, starting transfers between devices, body(): lax.all_to_all(samples, 'samp', split_axis=1, concat_axis=0, tiled=True)  15 us
    all_to_all x1, starting transfers between devices, from_everyone(): return lax.all_to_all(copies, axis, split_axis=0, concat_axis=0, tiled=True)  14.2 us
    dot_general x16, matrix products, visit(): jnp.dot(matrix, 1.0 - sign_rows * margin, precision=lax.Precision.HIGHEST)  13.4 us
    unnamed x12, local copies, waits for them, and re-layouts  12.9 us
    all_to_all x1, local copies, waits for them, and re-layouts, body(): lax.all_to_all(samples, 'samp', split_axis=1, concat_axis=0, tiled=True)  12 us
    dot_general x1, matrix products, body(): jnp.dot(samples, lax.all_gather(weight, 'samp', axis=0, tiled=True), pref...  8.12 us
  transfers between devices with their start and end apart: 4, of which 2 were waited for; matrix products, arithmetic and copies ran while one was open for 15% of the time, Pallas kernels for 0%

commit v1 on v0

v1 whole, which is shorter than its diff:
```python
import functools

import jax
import jax.numpy as jnp
from jax import lax
from jax.experimental import pallas as pl
from jax.experimental.pallas import tpu as pltpu
from jax.sharding import Mesh, PartitionSpec as P


BLOCK = 16
PASSES = 2
COUPLING = 0.5

ZH, X, Y, ZL, CORE = "zh", "x", "y", "zl", "core"
PLANE = (X, Y)
SAMP = (ZH, X, Y)
CLS = (ZL, CORE)
GAP_ROWS = 8
ORDER = (0, 2, 1, 3)
F32, BF16 = jnp.float32, jnp.bfloat16
SMALL = pltpu.CompilerParams(vmem_limit_bytes=16 * 2**20)


def shifted(value, axis, by):
    size = lax.axis_size(axis)
    return lax.ppermute(value, axis, [(i, (i + by) % size) for i in range(size)])


def pack_kernel(where, rows_ref, out_ref):
    width = out_ref.shape[2]
    for place in range(out_ref.shape[0]):
        out_ref[place] = rows_ref[:, place * width:(place + 1) * width]


def pack(samples, where, planes, members, quarters):
    rows, features = samples.shape
    part = rows // quarters
    width = features // (planes * members)
    return pl.pallas_call(
        pack_kernel,
        grid_spec=pltpu.PrefetchScalarGridSpec(
            num_scalar_prefetch=1,
            grid=(planes,),
            in_specs=[pl.BlockSpec((part, features // planes), lambda k, where: (where[0], lax.rem(where[1] + (planes - k), planes)))],
            out_specs=pl.BlockSpec((members, part, width), lambda k, where: (0, 0, k)),
        ),
        out_shape=jax.ShapeDtypeStruct((members, part, planes * width), samples.dtype),
        name="pack",
    )(where, samples)


def exact_dot(a, b):
    return jnp.dot(a, b, precision=lax.Precision.HIGHEST, preferred_element_type=F32)


def three_pieces(value):
    first = value.astype(BF16)
    rest = value - first.astype(F32)
    second = rest.astype(BF16)
    third = (rest - second.astype(F32)).astype(BF16)
    return first, second, third


def passes_kernel(where, start_ref, gram_ref, labels_ref, dual_ref, inverse_ref,
                  alpha_ref, steps_ref, top_ref, sign_ref, margin_ref, change_ref):
    rows, width = start_ref.shape
    class_ids = where[0] * width + lax.broadcasted_iota(jnp.int32, (rows, width), 1)
    sign = jnp.where(labels_ref[...] == class_ids, 1.0, -1.0).astype(F32)
    sign_ref[...] = sign
    start = start_ref[...]
    margin_ref[...] = start
    alpha_ref[...] = dual_ref[...]
    change_ref[...] = jnp.zeros((rows, width), F32)
    scaled = sign * start
    gap = jnp.sum(jnp.maximum(0.0, 1.0 - scaled) + dual_ref[...] * (scaled - 1.0), axis=0, keepdims=True)
    for turn in range(PASSES * (rows // BLOCK)):
        b = turn % (rows // BLOCK)
        at = slice(b * BLOCK, (b + 1) * BLOCK)
        signs = sign_ref[at]
        ascent = exact_dot(inverse_ref[b], 1.0 - signs * margin_ref[at])
        alpha = jnp.clip(alpha_ref[at] + ascent, 0.0, 1.0)
        change = signs * (alpha - dual_ref[at])
        moved = change - change_ref[at]
        alpha_ref[at] = alpha
        change_ref[at] = change
        margin_ref[...] += COUPLING * exact_dot(gram_ref[:, at], moved)
    top_ref[...] = jnp.max(margin_ref[...], axis=1, keepdims=True)
    payload = change_ref[...].astype(BF16)
    tail = tail_of(gap)
    for place in range(steps_ref.shape[0]):
        steps_ref[place, :rows] = payload
        steps_ref[place, rows:] = tail


def passes(where, start, gram, labels, dual, inverse, members):
    rows, width = start.shape
    whole = pl.BlockSpec(memory_space=pltpu.VMEM)
    return pl.pallas_call(
        passes_kernel,
        in_specs=[pl.BlockSpec(memory_space=pltpu.SMEM)] + [whole] * 5,
        out_specs=[whole] * 3,
        out_shape=[
            jax.ShapeDtypeStruct((rows, width), F32),
            jax.ShapeDtypeStruct((members, rows + GAP_ROWS, width), BF16),
            jax.ShapeDtypeStruct((rows, 1), F32),
        ],
        scratch_shapes=[pltpu.VMEM((rows, width), F32)] * 3,
        compiler_params=SMALL,
        name="passes",
    )(where, start, gram, labels, dual, inverse)


def tail_of(gap):
    first, second, third = three_pieces(gap)
    row = lax.broadcasted_iota(jnp.int32, (GAP_ROWS, gap.shape[1]), 0)
    zero = jnp.zeros((GAP_ROWS, gap.shape[1]), F32)
    return jnp.where(row == 0, first.astype(F32), jnp.where(row == 1, second.astype(F32), jnp.where(row == 2, third.astype(F32), zero))).astype(BF16)


def from_tail(tail):
    tail = tail.astype(F32)
    return (tail[0:1] + tail[1:2]) + tail[2:3]


def product(turned_ref, quarter_refs):
    total, d, low = None, 0, 0
    for ref in quarter_refs:
        high = low + ref.shape[0]
        term = jnp.dot(turned_ref[d, :, low:high], ref[...], preferred_element_type=F32)
        total = term if total is None else total + term
        d, low = (d + 1, 0) if high == turned_ref.shape[2] else (d, high)
    return total.T


def first_delta_kernel(where, *refs):
    *held, steps_ref, sent_ref, turned_ref, gap_ref = refs
    members, _, width = steps_ref.shape
    quarters = turned_ref.shape[0]
    part = turned_ref.shape[2] // members
    rows = quarters * part
    for d in range(quarters):
        low = pl.multiple_of(lax.bitwise_xor(where[0], d) * part, part)
        picked = jnp.concatenate([steps_ref[g, pl.ds(low, part), :] for g in range(members)], axis=0)
        turned_ref[d] = picked.astype(F32).T.astype(BF16)
    gap = jnp.zeros((1, width), F32)
    for g in range(members):
        gap += from_tail(steps_ref[g, rows:, :])
    gap_ref[...] = gap
    delta = product(turned_ref, held)
    depth = delta.shape[0]
    sent_ref[:depth] = delta.astype(BF16)
    sent_ref[depth:] = tail_of(gap)


def next_delta_kernel(where, *refs):
    *held, turned_ref, gap_ref, sent_ref = refs
    delta = product(turned_ref, held)
    depth = delta.shape[0]
    sent_ref[:depth] = delta.astype(BF16)
    sent_ref[depth:] = tail_of(gap_ref[...])


def own_delta_kernel(where, *refs):
    *held, turned_ref, sum_ref = refs
    sum_ref[...] = product(turned_ref, held)


def finish_kernel(count, weight_ref, own_ref, gap_ref, *refs):
    *came, new_ref, class_gap_ref = refs
    depth = own_ref.shape[0]
    total, gap = own_ref[...], gap_ref[...]
    for ref in came:
        total += ref[:depth].astype(F32)
        gap += from_tail(ref[depth:])
    new_ref[...] = weight_ref[...].astype(F32) + COUPLING * total
    class_gap_ref[...] = gap / count


def finish(weight, own, gap, came, count):
    depth, width = weight.shape
    whole = pl.BlockSpec(memory_space=pltpu.VMEM)
    return pl.pallas_call(
        functools.partial(finish_kernel, count),
        in_specs=[whole] * (3 + len(came)),
        out_specs=[whole] * 2,
        out_shape=[jax.ShapeDtypeStruct((depth, width), F32), jax.ShapeDtypeStruct((1, width), F32)],
        compiler_params=SMALL,
        name="finish",
    )(weight, own, gap, *came)


def column_specs(quarters, planes, k):
    return [pl.BlockSpec((held.shape[0], held.shape[1] // planes), lambda *_: (0, k)) for held in quarters]


def whole_spec(shape):
    return pl.BlockSpec(shape, lambda *_: (0,) * len(shape))


def first_delta(where, quarters, steps, planes, k):
    total, features = quarters[0].shape
    width = steps.shape[2]
    shapes = [
        jax.ShapeDtypeStruct((features // planes + GAP_ROWS, width), BF16),
        jax.ShapeDtypeStruct((len(ORDER), width, total), BF16),
        jax.ShapeDtypeStruct((1, width), F32),
    ]
    return pl.pallas_call(
        first_delta_kernel,
        grid_spec=pltpu.PrefetchScalarGridSpec(
            num_scalar_prefetch=1,
            grid=(1,),
            in_specs=column_specs(quarters, planes, k) + [whole_spec(steps.shape)],
            out_specs=[whole_spec(shape.shape) for shape in shapes],
        ),
        out_shape=shapes,
        compiler_params=SMALL,
        name="delta_first",
    )(where, *quarters, steps)


def next_delta(where, quarters, turned, gap, planes, k):
    shape = jax.ShapeDtypeStruct((quarters[0].shape[1] // planes + GAP_ROWS, gap.shape[1]), BF16)
    return pl.pallas_call(
        next_delta_kernel,
        grid_spec=pltpu.PrefetchScalarGridSpec(
            num_scalar_prefetch=1,
            grid=(1,),
            in_specs=column_specs(quarters, planes, k) + [whole_spec(turned.shape), whole_spec(gap.shape)],
            out_specs=whole_spec(shape.shape),
        ),
        out_shape=shape,
        compiler_params=SMALL,
        name="delta_next",
    )(where, *quarters, turned, gap)


def own_delta(where, quarters, turned, planes):
    shape = jax.ShapeDtypeStruct((quarters[0].shape[1] // planes, turned.shape[1]), F32)
    return pl.pallas_call(
        own_delta_kernel,
        grid_spec=pltpu.PrefetchScalarGridSpec(
            num_scalar_prefetch=1,
            grid=(1,),
            in_specs=column_specs(quarters, planes, 0) + [whole_spec(turned.shape)],
            out_specs=whole_spec(shape.shape),
        ),
        out_shape=shape,
        compiler_params=SMALL,
        name="delta_own",
    )(where, *quarters, turned)


def gathered_kernel(where, parts_ref, out_ref):
    members = parts_ref.shape[0]
    width = out_ref.shape[2]
    total = parts_ref[0]
    for g in range(1, members):
        total += parts_ref[g]
    for i, d in enumerate(ORDER):
        out_ref[lax.bitwise_xor(where[0], d)] = total[:, i * width:(i + 1) * width]


def gathered(where, parts):
    _, part, total = parts.shape
    return pl.pallas_call(
        gathered_kernel,
        in_specs=[pl.BlockSpec(memory_space=pltpu.SMEM), pl.BlockSpec(memory_space=pltpu.VMEM)],
        out_specs=pl.BlockSpec(memory_space=pltpu.VMEM),
        out_shape=jax.ShapeDtypeStruct((len(ORDER), part, total // len(ORDER)), F32),
        compiler_params=SMALL,
        name="gathered",
    )(where, parts)


def round_of_ascent(samples, labels, weight, dual, inverse):
    rows = samples.shape[0]
    depth, width = weight.shape
    planes = lax.axis_size(ZH)
    members = lax.axis_size(X) * lax.axis_size(Y)
    quarters = lax.axis_size(ZL) * lax.axis_size(CORE)
    part = rows // quarters
    mine = lax.axis_index(CLS).astype(jnp.int32)
    where = jnp.stack([mine, lax.axis_index(ZH).astype(jnp.int32)])

    packed = pack(samples, where, planes, members, quarters)
    quarter = lax.all_to_all(packed, PLANE, split_axis=0, concat_axis=0, tiled=True)
    near = [weight]
    for k in range(1, planes):
        near.append(shifted(weight, ZH, k))
    pairs = [jnp.concatenate([piece, shifted(piece, ZL, 1)], axis=1) for piece in near]
    by_pair = jnp.concatenate(pairs, axis=0)
    by_all = jnp.concatenate([by_pair, shifted(by_pair, CORE, 1)], axis=1)
    gram = lax.dot_general(samples, samples, (((1,), (1,)), ((), ())), preferred_element_type=F32)

    flat = quarter.reshape(members * part, planes * depth)
    half = members * part // 2
    beside_a = shifted(flat[:half], ZL, 1)
    partial = jnp.dot(flat, by_all, preferred_element_type=F32)
    partial = lax.all_to_all(partial.reshape(members, part, quarters * width), PLANE, split_axis=0, concat_axis=0, tiled=True)
    across = shifted(flat, CORE, 1)
    diagonal_a = shifted(beside_a, CORE, 1)
    pieces = gathered(where, partial)
    start = lax.all_to_all(pieces, CLS, split_axis=0, concat_axis=0, tiled=True).reshape(rows, width)
    beside_b = shifted(flat[half:], ZL, 1)

    alpha, steps, top = passes(where, start, gram, labels[:, None], dual, inverse, members)
    steps = lax.all_to_all(steps, PLANE, split_axis=0, concat_axis=0, tiled=True)
    diagonal_b = shifted(beside_b, CORE, 1)

    top = top[:, 0]
    other = shifted(top, CORE, 1)
    top = jnp.maximum(top, other)
    other = shifted(top, ZL, 1)
    top = jnp.maximum(top, other)

    held = [flat, across, beside_a, beside_b, diagonal_a, diagonal_b]
    far = planes // 2
    sent, turned, gap = first_delta(where, held, steps, planes, far)
    came = [shifted(sent, ZH, planes - far)]
    for k in range(1, planes):
        if k != far:
            sent = next_delta(where, held, turned, gap, planes, k)
            came.append(shifted(sent, ZH, planes - k))
    own = own_delta(where, held, turned, planes)
    new_weight, gap = finish(weight, own, gap, came, rows * planes * members)
    return new_weight, alpha, gap[0], top


def solution(mesh):
    fine = Mesh(mesh.devices.reshape(4, 4, 4, 2, 2), (ZH, X, Y, ZL, CORE))
    return jax.shard_map(
        round_of_ascent,
        mesh=fine,
        in_specs=(P(SAMP, None), P(SAMP), P(SAMP, CLS), P(SAMP, CLS), P(SAMP, None, None)),
        out_specs=(P(SAMP, CLS), P(SAMP, CLS), P(CLS), P(SAMP)),
        check_vma=False,
    )
```

time: 399 us -> 158 us (0.40)
  waiting for transfers between devices: 282 us -> 48.7 us
  Pallas kernels: 0 us -> 26.4 us
  matrix products: 38 us -> 11.7 us
  local copies, waits for them, and re-layouts: 25.5 us -> 3.63 us
  between operations: 14.2 us -> 0.81 us
  starting transfers between devices: 29.3 us -> 41.8 us
  blocking collectives: 6.12 us -> 18.3 us
    all_gather x2 -> x0, waiting for transfers between devices: 281 us -> none  [the longest x1 234 us: body(): lax.all_gather(weight, 'samp', axis=0, tiled=True)]
    ppermute x0 -> x18, waiting for transfers between devices: none -> 33.4 us  [shifted(): lax.ppermute(value, axis, [(i, (i + by) % size) for i in range(size)])]
    pallas_call x0 -> x8, Pallas kernels: none -> 26.4 us  [the longest x1 6.77 us: passes(): pl.pallas_call(passes_kernel, in_specs=[pl.BlockSpec(memory_space=pltpu.S...]
    dot_general x36 -> x2, matrix products: 38 us -> 11.7 us  [the longest x1 8.09 us: round_of_ascent(): lax.dot_general(samples, samples, (((1,), (1,)), ((), ())), preferred_ele...]
    ppermute x0 -> x18, starting transfers between devices: none -> 23.5 us  [shifted(): lax.ppermute(value, axis, [(i, (i + by) % size) for i in range(size)])]
    all_to_all x2 -> x3, waiting for transfers between devices: 0.01 us -> 15.3 us  [the longest x1 15.3 us: round_of_ascent(): lax.all_to_all(partial.reshape(members, part, quarters * width), PLANE, s...]
    all_to_all x1, blocking collectives: 6.12 us -> 18.3 us  [round_of_ascent(): lax.all_to_all(steps, PLANE, split_axis=0, concat_axis=0, tiled=True)]
    all_to_all x1 -> x0, local copies, waits for them, and re-layouts: 12 us -> none  [body(): lax.all_to_all(samples, 'samp', split_axis=1, concat_axis=0, tiled=True)]
  transfers between devices with their start and end apart: 4 -> 21, of which waited for: 2 -> 10; matrix products, arithmetic and copies ran while one was open for 15% -> 11% of each run, Pallas kernels for 0% -> 9%
where the time goes in v1:
time: 158 us; the launch traced here: 156 us
  waiting for transfers between devices  48.7 us (31%)
  starting transfers between devices  41.8 us (26%)
  Pallas kernels  26.4 us (17%)
  blocking collectives  18.3 us (12%)
  matrix products  11.7 us (7%)
  other arithmetic  4.33 us (3%)
  local copies, waits for them, and re-layouts  3.63 us (2%)
    ppermute x18, waiting for transfers between devices, shifted(): lax.ppermute(value, axis, [(i, (i + by) % size) for i in range(size)])  33.4 us
    ppermute x18, starting transfers between devices, shifted(): lax.ppermute(value, axis, [(i, (i + by) % size) for i in range(size)])  23.5 us
    all_to_all x1, blocking collectives, round_of_ascent(): lax.all_to_all(steps, PLANE, split_axis=0, concat_axis=0, tiled=True)  18.3 us
    all_to_all x1, waiting for transfers between devices, round_of_ascent(): lax.all_to_all(partial.reshape(members, part, quarters * width), PLANE, s...  15.3 us
    dot_general x1, matrix products, round_of_ascent(): lax.dot_general(samples, samples, (((1,), (1,)), ((), ())), preferred_ele...  8.09 us
    all_to_all x1, starting transfers between devices, round_of_ascent(): lax.all_to_all(packed, PLANE, split_axis=0, concat_axis=0, tiled=True)  7.61 us
    all_to_all x1, starting transfers between devices, round_of_ascent(): lax.all_to_all(partial.reshape(members, part, quarters * width), PLANE, s...  7.36 us
    pallas_call x1, Pallas kernels, passes(): pl.pallas_call(passes_kernel, in_specs=[pl.BlockSpec(memory_space=pltpu.S...  6.77 us
  transfers between devices with their start and end apart: 21, of which 10 were waited for; matrix products, arithmetic and copies ran while one was open for 11% of the time, Pallas kernels for 9%

profile of v1, /device:TPU:2, one launch (start us, length us, event | category | flops | bytes accessed | tf_op | source)
XLA Modules:
  0.0 155.7 jit_solution(7999770771599559306)
XLA Ops:
  1.2 4.5 %pack.1 = bf16[16,32,2048]{2,1,0:T(8,128)(2,1)} custom-call(s32[2]{0:T(128)} %pad_add_fusion.where, bf16[128,32768]{1,0:T(8,128)(2,1)} %rows_ref.1), custom_call_target="tpu_custom_call" | custom-call | tf_op jit(solution)/shard_map/pack/pallas_call | solution.py:40
  5.8 7.6 %all-to-all-start = ((bf16[16,32,2048]{2,1,0:T(8,128)(2,1)}), bf16[16,32,2048]{2,1,0:T(8,128)(2,1)S(1)}, u32[]{:S(2)}, u32[]{:S(2)}) async-start(bf16[16,32,2048]{2,1,0:T(8,128)(2,1)} %pack.1), calls=%async_computation | async-start | bytes 4194304 | tf_op jit(solution)/shard_map/all_to_all | solution.py:288
  13.4 7.3 %collective-permute-start.8 = (bf16[512,128]{1,0:T(8,128)(2,1)S(1)}, bf16[512,128]{1,0:T(8,128)(2,1)S(1)}, u32[]{:S(2)}, u32[]{:S(2)}) collective-permute-start(bf16[512,128]{1,0:T(8,128)(2,1)S(1)} %copy-done.2), channel_id=1, source_target_pairs={{0,128},{64,192},{128,0},{192,64},{1,129},{65,193},{129,1},{193,65... | collective-permute-start | bytes 393224 | tf_op jit(solution)/shard_map/ppermute | solution.py:27
  22.1 2.7 %collective-permute-start.10 = (bf16[512,128]{1,0:T(8,128)(2,1)S(1)}, bf16[512,128]{1,0:T(8,128)(2,1)S(1)}, u32[]{:S(2)}, u32[]{:S(2)}) collective-permute-start(bf16[512,128]{1,0:T(8,128)(2,1)S(1)} %copy-done.2), channel_id=1, source_target_pairs={{0,192},{64,0},{128,64},{192,128},{1,193},{65,1},{129,65},{193,129... | collective-permute-start | bytes 393224 | tf_op jit(solution)/shard_map/ppermute | solution.py:27
  28.0 4.1 %collective-permute-done.6 = bf16[512,128]{1,0:T(8,128)(2,1)S(1)} collective-permute-done((bf16[512,128]{1,0:T(8,128)(2,1)S(1)}, bf16[512,128]{1,0:T(8,128)(2,1)S(1)}, u32[]{:S(2)}, u32[]{:S(2)}) %collective-permute-start.6) | collective-permute-done | bytes 131104 | tf_op jit(solution)/shard_map/ppermute | solution.py:27
  34.2 2.6 %collective-permute-done.5 = bf16[512,128]{1,0:T(8,128)(2,1)S(1)} collective-permute-done((bf16[512,128]{1,0:T(8,128)(2,1)S(1)}, bf16[512,128]{1,0:T(8,128)(2,1)S(1)}, u32[]{:S(2)}, u32[]{:S(2)}) %collective-permute-start.5) | collective-permute-done | bytes 131104 | tf_op jit(solution)/shard_map/ppermute | solution.py:27
  36.8 2.8 %collective-permute-done.9 = bf16[512,128]{1,0:T(8,128)(2,1)S(1)} collective-permute-done((bf16[512,128]{1,0:T(8,128)(2,1)S(1)}, bf16[512,128]{1,0:T(8,128)(2,1)S(1)}, u32[]{:S(2)}, u32[]{:S(2)}) %collective-permute-start.9) | collective-permute-done | bytes 131104 | tf_op jit(solution)/shard_map/ppermute | solution.py:27
  39.6 2.8 %collective-permute-done.7 = bf16[512,128]{1,0:T(8,128)(2,1)S(1)} collective-permute-done((bf16[512,128]{1,0:T(8,128)(2,1)S(1)}, bf16[512,128]{1,0:T(8,128)(2,1)S(1)}, u32[]{:S(2)}, u32[]{:S(2)}) %collective-permute-start.7) | collective-permute-done | bytes 131104 | tf_op jit(solution)/shard_map/ppermute | solution.py:27
  47.2 1.8 %collective-permute-start.2 = (bf16[256,2048]{1,0:T(8,128)(2,1)}, bf16[256,2048]{1,0:T(8,128)(2,1)}, u32[]{:S(2)}, u32[]{:S(2)}) collective-permute-start(bf16[256,2048]{1,0:T(8,128)(2,1)} %bitcast.4), channel_id=1, source_target_pairs={{0,2},{2,0},{1,3},{3,1},{4,6},{6,4},{5,7},{7,5},{8,10},{10,8},{9,1... | collective-permute-start | bytes 3145736 | tf_op jit(solution)/shard_map/ppermute | solution.py:27
  49.1 3.6 %fusion = f32[16,32,512]{2,1,0:T(8,128)} fusion(bf16[16,32,2048]{2,1,0:T(8,128)(2,1)S(1)} %all-to-all-done, bf16[2048,256]{1,0:T(8,128)(2,1)} %collective-permute-done.12, bf16[512,128]{1,0:T(8,128)(2,1)} %copy-done.11, bf16[512,128]{1,0:T(8,128)(2,1)} %copy-done.7, bf16[512,128]{1,0:T(8,128)(2,1)} %copy-done.9, ...), kind=kOutput, calls=%fused_computation.1 | convolution fusion | flops 1092616192 | bytes 5242880 | tf_op jit(solution)/shard_map/dot_general | solution.py:300
  52.7 7.4 %all-to-all-start.1 = ((f32[16,32,512]{2,1,0:T(8,128)}), f32[16,32,512]{2,1,0:T(8,128)}, u32[]{:S(2)}, u32[]{:S(2)}) async-start(f32[16,32,512]{2,1,0:T(8,128)} %fusion), calls=%async_computation.1 | async-start | bytes 2097152 | tf_op jit(solution)/shard_map/all_to_all | solution.py:301
  60.1 15.3 %all-to-all-done.1.parts_ref = f32[16,32,512]{2,1,0:T(8,128)} async-done(((f32[16,32,512]{2,1,0:T(8,128)}), f32[16,32,512]{2,1,0:T(8,128)}, u32[]{:S(2)}, u32[]{:S(2)}) %all-to-all-start.1) | async-done | bytes 1048608 | tf_op jit(solution)/shard_map/all_to_all | solution.py:301
  75.3 1.9 %gathered.1 = f32[4,32,128]{2,1,0:T(8,128)} custom-call(s32[2]{0:T(128)S(1)} %copy-done.6, f32[16,32,512]{2,1,0:T(8,128)} %all-to-all-done.1.parts_ref), custom_call_target="tpu_custom_call" | custom-call | tf_op jit(solution)/shard_map/gathered/pallas_call | solution.py:267
  77.3 3.3 %all-to-all-start.2 = ((f32[4,32,128]{2,1,0:T(8,128)}), f32[4,32,128]{2,1,0:T(8,128)S(1)}, u32[]{:S(2)}, u32[]{:S(2)}) async-start(f32[4,32,128]{2,1,0:T(8,128)} %gathered.1), calls=%async_computation.2 | async-start | bytes 131072 | tf_op jit(solution)/shard_map/all_to_all | solution.py:305
  81.1 14.6 %collective-permute-done.2.refs_3_ = bf16[256,2048]{1,0:T(8,128)(2,1)} collective-permute-done((bf16[256,2048]{1,0:T(8,128)(2,1)}, bf16[256,2048]{1,0:T(8,128)(2,1)}, u32[]{:S(2)}, u32[]{:S(2)}) %collective-permute-start.2) | collective-permute-done | bytes 1048608 | tf_op jit(solution)/shard_map/ppermute | solution.py:27
  95.8 8.1 %fusion.19.gram_ref = f32[128,128]{1,0:T(8,128)S(1)} fusion(bf16[128,32768]{1,0:T(8,128)(2,1)} %rows_ref.1), kind=kOutput, calls=%fused_computation.22 | convolution fusion | flops 1073741824 | bytes 8454144 | tf_op jit(solution)/shard_map/dot_general | solution.py:295
  104.8 6.8 %passes.1 = (f32[128,128]{1,0:T(8,128)}, bf16[16,136,128]{2,1,0:T(8,128)(2,1)S(1)}, f32[128,1]{1,0:T(8,128)S(1)}) custom-call(s32[2]{0:T(128)S(1)} %copy-done.6, f32[128,128]{1,0:T(8,128)S(1)} %bitcast.19, f32[128,128]{1,0:T(8,128)S(1)} %fusion.19.gram_ref, s32[128,1]{1,0:T(8,128)S(1)} %copy.10.labels_ref, f32[128,128]{1,0:T(8,128)S(1)} %copy-done.3, ...), custom_call_target="tpu_custom_call" | custom-call | tf_op jit(solution)/shard_map/passes/pallas_call | solution.py:99
  111.6 18.3 %all_to_all.20.refs_6_ = bf16[16,136,128]{2,1,0:T(8,128)(2,1)S(1)} all-to-all(bf16[16,136,128]{2,1,0:T(8,128)(2,1)S(1)} %get-tuple-element.12), channel_id=1, replica_groups=mesh['zh'=4,'x'=4,'y'=4,'zl'=2,'core'=2] {'x','y'}, dimensions={0} | all-to-all | bytes 1114112 | tf_op jit(solution)/shard_map/all_to_all | solution.py:309
  129.9 3.1 %delta_first.1 = (bf16[520,128]{1,0:T(8,128)(2,1)}, bf16[4,128,512]{2,1,0:T(8,128)(2,1)S(1)}, f32[1,128]{1,0:T(1,128)S(1)}) custom-call(s32[2]{0:T(128)S(1)} %copy-done.6, bf16[512,2048]{1,0:T(8,128)(2,1)S(1)} %bitcast.15, bf16[512,2048]{1,0:T(8,128)(2,1)} %collective-permute-done.refs_1_, bf16[256,2048]{1,0:T(8,128)(2,1)S(1)} %collective-permute-done.1.refs_2_, ...), custom_call_target="tpu_custom_call" | custom-call | tf_op jit(solution)/shard_map/delta_first/pallas_call | solution.py:209
  133.0 3.0 %delta_next.2 = bf16[520,128]{1,0:T(8,128)(2,1)} custom-call(s32[2]{0:T(128)S(1)} %copy-done.6, bf16[512,2048]{1,0:T(8,128)(2,1)S(1)} %bitcast.16, bf16[512,2048]{1,0:T(8,128)(2,1)} %collective-permute-done.refs_1_, bf16[256,2048]{1,0:T(8,128)(2,1)S(1)} %collective-permute-done.1.refs_2_, bf16[256,2048]{1,0:T(8,128)(2,1)} %collective-permute-done.2.refs_3_, ...), custom_call_target="tpu_custom_call" | custom-call | tf_op jit(solution)/shard_map/delta_next/pallas_call | solution.py:225
  136.7 3.0 %delta_next.3 = bf16[520,128]{1,0:T(8,128)(2,1)} custom-call(s32[2]{0:T(128)S(1)} %copy-done.6, bf16[512,2048]{1,0:T(8,128)(2,1)S(1)} %bitcast.17, bf16[512,2048]{1,0:T(8,128)(2,1)} %collective-permute-done.refs_1_, bf16[256,2048]{1,0:T(8,128)(2,1)S(1)} %collective-permute-done.1.refs_2_, bf16[256,2048]{1,0:T(8,128)(2,1)} %collective-permute-done.2.refs_3_, ...), custom_call_target="tpu_custom_call" | custom-call | tf_op jit(solution)/shard_map/delta_next/pallas_call | solution.py:225
  139.7 2.3 %collective-permute-start.15 = (bf16[520,128]{1,0:T(8,128)(2,1)}, bf16[520,128]{1,0:T(8,128)(2,1)S(1)}, u32[]{:S(2)}, u32[]{:S(2)}) collective-permute-start(bf16[520,128]{1,0:T(8,128)(2,1)} %delta_next.3), channel_id=1, source_target_pairs={{0,64},{64,128},{128,192},{192,0},{1,65},{65,129},{129,193},{193,1... | collective-permute-start | bytes 399368 | tf_op jit(solution)/shard_map/ppermute | solution.py:27
  146.4 1.9 %collective-permute-start.17 = (f32[128]{0:T(128)S(1)}, f32[128]{0:T(128)S(1)}, u32[]{:S(2)}, u32[]{:S(2)}) collective-permute-start(f32[128]{0:T(128)S(1)} %max.6), channel_id=1, source_target_pairs={{0,2},{2,0},{1,3},{3,1},{4,6},{6,4},{5,7},{7,5},{8,10},{10,8},{9,1... | collective-permute-start | bytes 1544 | tf_op jit(solution)/shard_map/ppermute | solution.py:27
  151.6 2.4 %delta_own.1.own_ref = f32[512,128]{1,0:T(8,128)S(1)} custom-call(s32[2]{0:T(128)S(1)} %copy-done.6, bf16[512,2048]{1,0:T(8,128)(2,1)S(1)} %bitcast.18, bf16[512,2048]{1,0:T(8,128)(2,1)} %collective-permute-done.refs_1_, bf16[256,2048]{1,0:T(8,128)(2,1)S(1)} %collective-permute-done.1.refs_2_, bf16[256,2048]{1,0:T(8,128)(2,1)} %collective-permute-done.2.refs_3_, ...), custom_call_target="tpu_custom_call" | custom-call | tf_op jit(solution)/shard_map/delta_own/pallas_call | solution.py:241
  (62 shorter events, 23.7 us)
Async XLA Ops:
  5.8 39.6 %all-to-all-start = ((bf16[16,32,2048]{2,1,0:T(8,128)(2,1)}), bf16[16,32,2048]{2,1,0:T(8,128)(2,1)S(1)}, u32[]{:S(2)}, u32[]{:S(2)}) async-start(bf16[16,32,2048]{2,1,0:T(8,128)(2,1)} %pack.1), calls=%async_computation | async-start | bytes 4194304 | tf_op jit(solution)/shard_map/all_to_all | solution.py:288
  13.4 14.1 %collective-permute-start.8 = (bf16[512,128]{1,0:T(8,128)(2,1)S(1)}, bf16[512,128]{1,0:T(8,128)(2,1)S(1)}, u32[]{:S(2)}, u32[]{:S(2)}) collective-permute-start(bf16[512,128]{1,0:T(8,128)(2,1)S(1)} %copy-done.2), channel_id=1, source_target_pairs={{0,128},{64,192},{128,0},{192,64},{1,129},{65,193},{129,1},{193,65... | collective-permute-start | bytes 393224 | tf_op jit(solution)/shard_map/ppermute | solution.py:27
  20.7 11.5 %collective-permute-start.6 = (bf16[512,128]{1,0:T(8,128)(2,1)S(1)}, bf16[512,128]{1,0:T(8,128)(2,1)S(1)}, u32[]{:S(2)}, u32[]{:S(2)}) collective-permute-start(bf16[512,128]{1,0:T(8,128)(2,1)S(1)} %copy-done.2), channel_id=1, source_target_pairs={{0,64},{64,128},{128,192},{192,0},{1,65},{65,129},{129,193},{193,1... | collective-permute-start | bytes 393224 | tf_op jit(solution)/shard_map/ppermute | solution.py:27
  22.1 10.7 %collective-permute-start.10 = (bf16[512,128]{1,0:T(8,128)(2,1)S(1)}, bf16[512,128]{1,0:T(8,128)(2,1)S(1)}, u32[]{:S(2)}, u32[]{:S(2)}) collective-permute-start(bf16[512,128]{1,0:T(8,128)(2,1)S(1)} %copy-done.2), channel_id=1, source_target_pairs={{0,192},{64,0},{128,64},{192,128},{1,193},{65,1},{129,65},{193,129... | collective-permute-start | bytes 393224 | tf_op jit(solution)/shard_map/ppermute | solution.py:27
  24.8 12.0 %collective-permute-start.5 = (bf16[512,128]{1,0:T(8,128)(2,1)S(1)}, bf16[512,128]{1,0:T(8,128)(2,1)S(1)}, u32[]{:S(2)}, u32[]{:S(2)}) collective-permute-start(bf16[512,128]{1,0:T(8,128)(2,1)S(1)} %copy-done.2), channel_id=1, source_target_pairs={{0,2},{2,0},{1,3},{3,1},{4,6},{6,4},{5,7},{7,5},{8,10},{10,8},{9,1... | collective-permute-start | bytes 393224 | tf_op jit(solution)/shard_map/ppermute | solution.py:27
  27.5 12.1 %collective-permute-start.9 = (bf16[512,128]{1,0:T(8,128)(2,1)S(1)}, bf16[512,128]{1,0:T(8,128)(2,1)S(1)}, u32[]{:S(2)}, u32[]{:S(2)}) collective-permute-start(bf16[512,128]{1,0:T(8,128)(2,1)S(1)} %collective-permute-done.8), channel_id=1, source_target_pairs={{0,2},{2,0},{1,3},{3,1},{4,6},{6,4},{5,7},{7,5},{8,10},{10,8},{9,1... | collective-permute-start | bytes 393224 | tf_op jit(solution)/shard_map/ppermute | solution.py:27
  32.2 10.2 %collective-permute-start.7 = (bf16[512,128]{1,0:T(8,128)(2,1)S(1)}, bf16[512,128]{1,0:T(8,128)(2,1)S(1)}, u32[]{:S(2)}, u32[]{:S(2)}) collective-permute-start(bf16[512,128]{1,0:T(8,128)(2,1)S(1)} %collective-permute-done.6), channel_id=1, source_target_pairs={{0,2},{2,0},{1,3},{3,1},{4,6},{6,4},{5,7},{7,5},{8,10},{10,8},{9,1... | collective-permute-start | bytes 393224 | tf_op jit(solution)/shard_map/ppermute | solution.py:27
  32.8 11.4 %collective-permute-start.11 = (bf16[512,128]{1,0:T(8,128)(2,1)S(1)}, bf16[512,128]{1,0:T(8,128)(2,1)S(1)}, u32[]{:S(2)}, u32[]{:S(2)}) collective-permute-start(bf16[512,128]{1,0:T(8,128)(2,1)S(1)} %collective-permute-done.10), channel_id=1, source_target_pairs={{0,2},{2,0},{1,3},{3,1},{4,6},{6,4},{5,7},{7,5},{8,10},{10,8},{9,1... | collective-permute-start | bytes 393224 | tf_op jit(solution)/shard_map/ppermute | solution.py:27
  45.3 3.7 %collective-permute-start.12 = (bf16[2048,256]{1,0:T(8,128)(2,1)}, bf16[2048,256]{1,0:T(8,128)(2,1)}, u32[]{:S(2)}, u32[]{:S(2)}) collective-permute-start(bf16[2048,256]{1,0:T(8,128)(2,1)} %maximum_maximum_fusion), channel_id=1, source_target_pairs={{0,1},{1,0},{2,3},{3,2},{4,5},{5,4},{6,7},{7,6},{8,9},{9,8},{10,11... | collective-permute-start | bytes 3145736 | tf_op jit(solution)/shard_map/ppermute | solution.py:27
  47.0 33.6 %collective-permute-start.1 = (bf16[256,2048]{1,0:T(8,128)(2,1)}, bf16[256,2048]{1,0:T(8,128)(2,1)S(1)}, u32[]{:S(2)}, u32[]{:S(2)}) collective-permute-start(bf16[256,2048]{1,0:T(8,128)(2,1)} %bitcast.3), channel_id=1, source_target_pairs={{0,2},{2,0},{1,3},{3,1},{4,6},{6,4},{5,7},{7,5},{8,10},{10,8},{9,1... | collective-permute-start | bytes 3145736 | tf_op jit(solution)/shard_map/ppermute | solution.py:27
  47.2 48.5 %collective-permute-start.2 = (bf16[256,2048]{1,0:T(8,128)(2,1)}, bf16[256,2048]{1,0:T(8,128)(2,1)}, u32[]{:S(2)}, u32[]{:S(2)}) collective-permute-start(bf16[256,2048]{1,0:T(8,128)(2,1)} %bitcast.4), channel_id=1, source_target_pairs={{0,2},{2,0},{1,3},{3,1},{4,6},{6,4},{5,7},{7,5},{8,10},{10,8},{9,1... | collective-permute-start | bytes 3145736 | tf_op jit(solution)/shard_map/ppermute | solution.py:27
  52.7 22.6 %copy-start.6 = (s32[2]{0:T(128)S(1)}, s32[2]{0:T(128)}, u32[]{:S(2)}) copy-start(s32[2]{0:T(128)} %pad_add_fusion.where) | copy-start | bytes 28
  52.7 22.6 %all-to-all-start.1 = ((f32[16,32,512]{2,1,0:T(8,128)}), f32[16,32,512]{2,1,0:T(8,128)}, u32[]{:S(2)}, u32[]{:S(2)}) async-start(f32[16,32,512]{2,1,0:T(8,128)} %fusion), calls=%async_computation.1 | async-start | bytes 2097152 | tf_op jit(solution)/shard_map/all_to_all | solution.py:301
  60.0 69.9 %collective-permute-start = (bf16[512,2048]{1,0:T(8,128)(2,1)S(1)}, bf16[512,2048]{1,0:T(8,128)(2,1)}, u32[]{:S(2)}, u32[]{:S(2)}) collective-permute-start(bf16[512,2048]{1,0:T(8,128)(2,1)S(1)} %bitcast.14), channel_id=1, source_target_pairs={{0,1},{1,0},{2,3},{3,2},{4,5},{5,4},{6,7},{7,6},{8,9},{9,8},{10,11... | collective-permute-start | bytes 6291464 | tf_op jit(solution)/shard_map/ppermute | solution.py:27
  77.3 26.7 %all-to-all-start.2 = ((f32[4,32,128]{2,1,0:T(8,128)}), f32[4,32,128]{2,1,0:T(8,128)S(1)}, u32[]{:S(2)}, u32[]{:S(2)}) async-start(f32[4,32,128]{2,1,0:T(8,128)} %gathered.1), calls=%async_computation.2 | async-start | bytes 131072 | tf_op jit(solution)/shard_map/all_to_all | solution.py:305
  80.5 23.3 %copy-start.12 = (s32[128]{0:T(128)S(1)}, s32[128]{0:T(128)}, u32[]{:S(2)}) copy-start(s32[128]{0:T(128)} %param.6) | copy-start | bytes 1540
  80.6 23.4 %copy-start.3 = (f32[128,128]{1,0:T(8,128)S(1)}, f32[128,128]{1,0:T(8,128)}, u32[]{:S(2)}) copy-start(f32[128,128]{1,0:T(8,128)} %dual_ref.1) | copy-start | bytes 196612
  80.6 49.3 %collective-permute-start.3 = (bf16[256,2048]{1,0:T(8,128)(2,1)S(1)}, bf16[256,2048]{1,0:T(8,128)(2,1)}, u32[]{:S(2)}, u32[]{:S(2)}) collective-permute-start(bf16[256,2048]{1,0:T(8,128)(2,1)S(1)} %collective-permute-done.1.refs_2_), channel_id=1, source_target_pairs={{0,1},{1,0},{2,3},{3,2},{4,5},{5,4},{6,7},{7,6},{8,9},{9,8},{10,11... | collective-permute-start | bytes 3145736 | tf_op jit(solution)/shard_map/ppermute | solution.py:27
  95.7 34.2 %collective-permute-start.4 = (bf16[256,2048]{1,0:T(8,128)(2,1)}, bf16[256,2048]{1,0:T(8,128)(2,1)}, u32[]{:S(2)}, u32[]{:S(2)}) collective-permute-start(bf16[256,2048]{1,0:T(8,128)(2,1)} %collective-permute-done.2.refs_3_), channel_id=1, source_target_pairs={{0,1},{1,0},{2,3},{3,2},{4,5},{5,4},{6,7},{7,6},{8,9},{9,8},{10,11... | collective-permute-start | bytes 3145736 | tf_op jit(solution)/shard_map/ppermute | solution.py:27
  136.0 17.9 %collective-permute-start.14 = (bf16[520,128]{1,0:T(8,128)(2,1)}, bf16[520,128]{1,0:T(8,128)(2,1)S(1)}, u32[]{:S(2)}, u32[]{:S(2)}) collective-permute-start(bf16[520,128]{1,0:T(8,128)(2,1)} %delta_next.2), channel_id=1, source_target_pairs={{0,192},{64,0},{128,64},{192,128},{1,193},{65,1},{129,65},{193,129... | collective-permute-start | bytes 399368 | tf_op jit(solution)/shard_map/ppermute | solution.py:27
  139.7 14.3 %collective-permute-start.15 = (bf16[520,128]{1,0:T(8,128)(2,1)}, bf16[520,128]{1,0:T(8,128)(2,1)S(1)}, u32[]{:S(2)}, u32[]{:S(2)}) collective-permute-start(bf16[520,128]{1,0:T(8,128)(2,1)} %delta_next.3), channel_id=1, source_target_pairs={{0,64},{64,128},{128,192},{192,0},{1,65},{65,129},{129,193},{193,1... | collective-permute-start | bytes 399368 | tf_op jit(solution)/shard_map/ppermute | solution.py:27
  142.0 12.0 %collective-permute-start.13 = (bf16[520,128]{1,0:T(8,128)(2,1)}, bf16[520,128]{1,0:T(8,128)(2,1)}, u32[]{:S(2)}, u32[]{:S(2)}) collective-permute-start(bf16[520,128]{1,0:T(8,128)(2,1)} %get-tuple-element.15), channel_id=1, source_target_pairs={{0,128},{64,192},{128,0},{192,64},{1,129},{65,193},{129,1},{193,65... | collective-permute-start | bytes 399368 | tf_op jit(solution)/shard_map/ppermute | solution.py:27
  144.5 1.3 collective-permute-start.16
  146.4 3.6 %collective-permute-start.17 = (f32[128]{0:T(128)S(1)}, f32[128]{0:T(128)S(1)}, u32[]{:S(2)}, u32[]{:S(2)}) collective-permute-start(f32[128]{0:T(128)S(1)} %max.6), channel_id=1, source_target_pairs={{0,2},{2,0},{1,3},{3,1},{4,6},{6,4},{5,7},{7,5},{8,10},{10,8},{9,1... | collective-permute-start | bytes 1544 | tf_op jit(solution)/shard_map/ppermute | solution.py:27
  (10 other events, 70.2 us)

commit v2 on v1

v2 whole, which is shorter than its diff:
```python
import functools

import jax
import jax.numpy as jnp
from jax import lax
from jax.experimental import pallas as pl
from jax.experimental.pallas import tpu as pltpu
from jax.sharding import Mesh, PartitionSpec as P


BLOCK = 16
PASSES = 2
COUPLING = 0.5

ZH, X, Y, ZL, CORE = "zh", "x", "y", "zl", "core"
PLANE = (X, Y)
SAMP = (ZH, X, Y)
CLS = (ZL, CORE)
GAP_ROWS = 8
EARLY = 10
ORDER = (0, 2, 1, 3)
F32, BF16 = jnp.float32, jnp.bfloat16
IN_VMEM = pl.BlockSpec(memory_space=pltpu.VMEM)
IN_SMEM = pl.BlockSpec(memory_space=pltpu.SMEM)
IN_HBM = pl.BlockSpec(memory_space=pltpu.HBM)
LEFT = (0, 0, 1, 1, 0, 2)
RIGHT = (0, 1, 0, 1, 2, 0)
SMALL = pltpu.CompilerParams(vmem_limit_bytes=16 * 2**20)
FULL = pltpu.CompilerParams(vmem_limit_bytes=60 * 1024 * 1024)


def shifted(value, axis, by):
    size = lax.axis_size(axis)
    return lax.ppermute(value, axis, [(i, (i + by) % size) for i in range(size)])


def pack_kernel(where, rows_hbm, out_hbm, held_ref, in_sems, out_sems):
    members, part, total = out_hbm.shape
    planes = in_sems.shape[0]
    width = total // planes
    span = members * width
    row = pl.multiple_of(where[0] * part, part)
    loads = []
    for k in range(planes):
        low = pl.multiple_of(lax.rem(where[1] + (planes - k), planes) * span, span)
        loads.append(pltpu.make_async_copy(rows_hbm.at[pl.ds(row, part), pl.ds(low, span)], held_ref.at[k], in_sems.at[k]))
    for load in loads:
        load.start()
    stores = []
    for k in range(planes):
        loads[k].wait()
        for place in range(members):
            store = pltpu.make_async_copy(
                held_ref.at[k, :, pl.ds(place * width, width)],
                out_hbm.at[place, :, pl.ds(k * width, width)],
                out_sems.at[k * members + place],
            )
            store.start()
            stores.append(store)
    for store in stores:
        store.wait()


def pack(samples, where, planes, members, quarters):
    rows, features = samples.shape
    part = rows // quarters
    return pl.pallas_call(
        pack_kernel,
        in_specs=[IN_SMEM, IN_HBM],
        out_specs=IN_HBM,
        out_shape=jax.ShapeDtypeStruct((members, part, features // members), samples.dtype),
        scratch_shapes=[
            pltpu.VMEM((planes, part, features // planes), samples.dtype),
            pltpu.SemaphoreType.DMA((planes,)),
            pltpu.SemaphoreType.DMA((planes * members,)),
        ],
        compiler_params=FULL,
        name="pack",
    )(where, samples)


def three_pieces(value):
    first = value.astype(BF16)
    rest = value - first.astype(F32)
    second = rest.astype(BF16)
    third = (rest - second.astype(F32)).astype(BF16)
    return first, second, third


def prepare_kernel(gram_ref, inverse_ref, expanded_ref, wide_ref):
    rows = gram_ref.shape[0]
    _, size, _ = inverse_ref.shape
    lanes = expanded_ref.shape[3]
    b = pl.program_id(0)
    low = pl.multiple_of(b * size, size)
    high = pl.multiple_of(lax.rem(b + 1, pl.num_programs(0)) * size, size)
    spot = lax.broadcasted_iota(jnp.int32, (rows, size), 0) == low + lax.broadcasted_iota(jnp.int32, (rows, size), 1)
    picks = jnp.where(spot, 1.0, 0.0).astype(BF16)
    sides = [jnp.dot(piece, picks, preferred_element_type=F32) for piece in three_pieces(COUPLING * gram_ref[...])]
    exact = jnp.dot(gram_ref[pl.ds(high, size)], jnp.where(spot, 1.0, 0.0), precision=lax.Precision.HIGHEST, preferred_element_type=F32)
    for k in range(size):
        expanded_ref[0, k] = jnp.broadcast_to(inverse_ref[0, :, k:k + 1], (size, lanes))
        expanded_ref[0, size + k] = COUPLING * jnp.broadcast_to(exact[:, k:k + 1], (size, lanes))
    wide_ref[0] = jnp.concatenate([sides[p].astype(BF16) for p in LEFT], axis=1)


def prepare(gram, inverse, lanes):
    rows = gram.shape[0]
    blocks, size, _ = inverse.shape
    return pl.pallas_call(
        prepare_kernel,
        grid=(blocks,),
        in_specs=[pl.BlockSpec((rows, rows), lambda b: (0, 0)), pl.BlockSpec((1, size, size), lambda b: (b, 0, 0))],
        out_specs=[
            pl.BlockSpec((1, 2 * size, size, lanes), lambda b: (b, 0, 0, 0)),
            pl.BlockSpec((1, rows, len(LEFT) * size), lambda b: (b, 0, 0)),
        ],
        out_shape=[
            jax.ShapeDtypeStruct((blocks, 2 * size, size, lanes), F32),
            jax.ShapeDtypeStruct((blocks, rows, len(LEFT) * size), BF16),
        ],
        compiler_params=FULL,
        name="prepare",
    )(gram, inverse)


def rows_product(expanded, value):
    size = value.shape[0]
    sums = []
    for k in range(size):
        term = expanded[k] * jnp.broadcast_to(value[k:k + 1], value.shape)
        if k < 4:
            sums.append(term)
        else:
            sums[k % 4] += term
    return (sums[0] + sums[1]) + (sums[2] + sums[3])


def passes_kernel(where, start_hbm, labels_hbm, dual_hbm, expanded_hbm, wide_hbm, alpha_hbm, steps_hbm, top_hbm,
                  margin_ref, labels_ref, dual_ref, expanded_ref, wide_ref, alpha_ref, start_ref, sign_ref, change_ref, payload_ref, top_ref, sems):
    rows, width = margin_ref.shape
    blocks = rows // BLOCK
    copies = [
        pltpu.make_async_copy(start_hbm, start_ref, sems.at[0]),
        pltpu.make_async_copy(labels_hbm, labels_ref, sems.at[1]),
        pltpu.make_async_copy(dual_hbm, dual_ref, sems.at[2]),
    ]
    parts = [
        [pltpu.make_async_copy(expanded_hbm.at[b], expanded_ref.at[b], sems.at[3 + b]),
         pltpu.make_async_copy(wide_hbm.at[b], wide_ref.at[b], sems.at[3 + blocks + b])]
        for b in range(blocks)
    ]
    for copy in copies + [part for pair in parts for part in pair]:
        copy.start()
    change_ref[...] = jnp.zeros((rows, width), F32)
    for copy in copies:
        copy.wait()
    class_ids = where[0] * width + lax.broadcasted_iota(jnp.int32, (rows, width), 1)
    sign_ref[...] = jnp.where(labels_ref[...] == class_ids, 1.0, -1.0).astype(F32)
    margin_ref[...] = start_ref[...]
    alpha_ref[...] = dual_ref[...]
    margin = start_ref[:BLOCK]
    for turn in range(PASSES * blocks):
        b = turn % blocks
        at = slice(b * BLOCK, (b + 1) * BLOCK)
        n = (b + 1) % blocks
        if turn < blocks:
            for copy in parts[b]:
                copy.wait()
        signs = sign_ref[at]
        ascent = rows_product(expanded_ref[b, :BLOCK], 1.0 - signs * margin)
        alpha = jnp.clip(alpha_ref[at] + ascent, 0.0, 1.0)
        change = signs * (alpha - dual_ref[at])
        moved = change - change_ref[at]
        alpha_ref[at] = alpha
        change_ref[at] = change
        margin = margin_ref[n * BLOCK:(n + 1) * BLOCK] + rows_product(expanded_ref[b, BLOCK:], moved)
        pieces = three_pieces(moved)
        tall = jnp.concatenate([pieces[p] for p in RIGHT], axis=0)
        margin_ref[...] += jnp.dot(wide_ref[b], tall, preferred_element_type=F32)
    scaled = sign_ref[...] * start_ref[...]
    gap = jnp.sum(jnp.maximum(0.0, 1.0 - scaled) + dual_ref[...] * (scaled - 1.0), axis=0, keepdims=True)
    payload_ref[:rows] = change_ref[...].astype(BF16)
    payload_ref[rows:] = tail_of(gap)
    outs = [pltpu.make_async_copy(payload_ref, steps_hbm.at[place], sems.at[place]) for place in range(steps_hbm.shape[0])]
    for copy in outs:
        copy.start()
    top_ref[...] = jnp.max(margin_ref[...].T, axis=0, keepdims=True)
    after = steps_hbm.shape[0]
    outs += [pltpu.make_async_copy(alpha_ref, alpha_hbm, sems.at[after]), pltpu.make_async_copy(top_ref, top_hbm, sems.at[after + 1])]
    for copy in outs[after:]:
        copy.start()
    for copy in outs:
        copy.wait()


def passes(where, start, labels, dual, ready, members):
    rows, width = start.shape
    square = pltpu.VMEM((rows, width), F32)
    return pl.pallas_call(
        passes_kernel,
        in_specs=[IN_SMEM] + [IN_HBM] * 5,
        out_specs=[IN_HBM] * 3,
        out_shape=[
            jax.ShapeDtypeStruct((rows, width), F32),
            jax.ShapeDtypeStruct((members, rows + GAP_ROWS, width), BF16),
            jax.ShapeDtypeStruct((1, rows), F32),
        ],
        scratch_shapes=[
            square,
            pltpu.VMEM(labels.shape, labels.dtype),
            square,
            pltpu.VMEM(ready[0].shape, ready[0].dtype),
            pltpu.VMEM(ready[1].shape, ready[1].dtype),
            square,
            square,
            square,
            square,
            pltpu.VMEM((rows + GAP_ROWS, width), BF16),
            pltpu.VMEM((1, rows), F32),
            pltpu.SemaphoreType.DMA((3 + 2 * (rows // BLOCK),)),
        ],
        compiler_params=FULL,
        name="passes",
    )(where, start, labels, dual, *ready)


def tail_of(gap):
    first, second, third = three_pieces(gap)
    row = lax.broadcasted_iota(jnp.int32, (GAP_ROWS, gap.shape[1]), 0)
    zero = jnp.zeros((GAP_ROWS, gap.shape[1]), F32)
    return jnp.where(row == 0, first.astype(F32), jnp.where(row == 1, second.astype(F32), jnp.where(row == 2, third.astype(F32), zero))).astype(BF16)


def from_tail(tail):
    tail = tail.astype(F32)
    return (tail[0:1] + tail[1:2]) + tail[2:3]


def fetches(held_refs, block_ref, sems, k):
    depth = block_ref.shape[1]
    copies, low = [], 0
    for i, ref in enumerate(held_refs):
        rows = ref.shape[0]
        copies.append(pltpu.make_async_copy(ref.at[:, pl.ds(k * depth, depth)], block_ref.at[pl.ds(low, rows)], sems.at[i]))
        low += rows
    for copy in copies:
        copy.start()
    return copies


def lanes_of(rows):
    return -(-rows // 128) * 128


def product(turned_ref, block_ref, copies, heights):
    total, low, at = None, 0, 0
    for copy, rows in zip(copies, heights):
        copy.wait()
        term = jnp.dot(turned_ref[:, at:at + rows], block_ref[low:low + rows], preferred_element_type=F32)
        total = term if total is None else total + term
        low += rows
        at += lanes_of(rows)
    return total.T


def first_delta_kernel(k, where, *refs):
    *held, steps_ref, sent_ref, turned_ref, gap_ref, block_ref, sems = refs
    copies = fetches(held, block_ref, sems, k)
    members, tall, width = steps_ref.shape
    rows = tall - GAP_ROWS
    part = rows // len(ORDER)
    d, first, at = 0, 0, 0
    for ref in held:
        count = ref.shape[0] // part
        low = pl.multiple_of(lax.bitwise_xor(where[0], d) * part, part)
        picked = jnp.concatenate([steps_ref[g, pl.ds(low, part), :] for g in range(first, first + count)], axis=0)
        turned_ref[:, at:at + count * part] = picked.astype(F32).T.astype(BF16)
        at += lanes_of(count * part)
        d, first = (d + 1, 0) if first + count == members else (d, first + count)
    gap = jnp.zeros((1, width), F32)
    for g in range(members):
        gap += from_tail(steps_ref[g, rows:, :])
    gap_ref[...] = gap
    delta = product(turned_ref, block_ref, copies, [ref.shape[0] for ref in held])
    depth = delta.shape[0]
    sent_ref[:depth] = delta.astype(BF16)
    sent_ref[depth:] = tail_of(gap)


def next_delta_kernel(k, *refs):
    *held, turned_ref, gap_ref, sent_ref, block_ref, sems = refs
    copies = fetches(held, block_ref, sems, k)
    delta = product(turned_ref, block_ref, copies, [ref.shape[0] for ref in held])
    depth = delta.shape[0]
    sent_ref[:depth] = delta.astype(BF16)
    sent_ref[depth:] = tail_of(gap_ref[...])


def own_delta_kernel(*refs):
    *held, turned_ref, sum_ref, block_ref, sems = refs
    copies = fetches(held, block_ref, sems, 0)
    sum_ref[...] = product(turned_ref, block_ref, copies, [ref.shape[0] for ref in held])


def finish_kernel(count, weight_ref, own_ref, gap_ref, *refs):
    *came, new_ref, class_gap_ref = refs
    depth = own_ref.shape[0]
    total, gap = own_ref[...], gap_ref[...]
    for ref in came:
        total += ref[:depth].astype(F32)
        gap += from_tail(ref[depth:])
    new_ref[...] = weight_ref[...].astype(F32) + COUPLING * total
    class_gap_ref[...] = gap / count


def finish(weight, own, gap, came, count):
    depth, width = weight.shape
    whole = pl.BlockSpec(memory_space=pltpu.VMEM)
    return pl.pallas_call(
        functools.partial(finish_kernel, count),
        in_specs=[whole] * (3 + len(came)),
        out_specs=[whole] * 2,
        out_shape=[jax.ShapeDtypeStruct((depth, width), F32), jax.ShapeDtypeStruct((1, width), F32)],
        compiler_params=SMALL,
        name="finish",
    )(weight, own, gap, *came)


def block_scratch(quarters, planes):
    rows = sum(held.shape[0] for held in quarters)
    return [pltpu.VMEM((rows, quarters[0].shape[1] // planes), BF16), pltpu.SemaphoreType.DMA((len(quarters),))]


def first_delta(where, quarters, steps, planes, k):
    features = quarters[0].shape[1]
    width = steps.shape[2]
    return pl.pallas_call(
        functools.partial(first_delta_kernel, k),
        in_specs=[IN_SMEM] + [IN_HBM] * len(quarters) + [IN_VMEM],
        out_specs=[IN_VMEM] * 3,
        out_shape=[
            jax.ShapeDtypeStruct((features // planes + GAP_ROWS, width), BF16),
            jax.ShapeDtypeStruct((width, sum(lanes_of(held.shape[0]) for held in quarters)), BF16),
            jax.ShapeDtypeStruct((1, width), F32),
        ],
        scratch_shapes=block_scratch(quarters, planes),
        compiler_params=SMALL,
        name="delta_first",
    )(where, *quarters, steps)


def next_delta(quarters, turned, gap, planes, k):
    return pl.pallas_call(
        functools.partial(next_delta_kernel, k),
        in_specs=[IN_HBM] * len(quarters) + [IN_VMEM] * 2,
        out_specs=IN_VMEM,
        out_shape=jax.ShapeDtypeStruct((quarters[0].shape[1] // planes + GAP_ROWS, gap.shape[1]), BF16),
        scratch_shapes=block_scratch(quarters, planes),
        compiler_params=SMALL,
        name="delta_next",
    )(*quarters, turned, gap)


def own_delta(quarters, turned, planes):
    return pl.pallas_call(
        own_delta_kernel,
        in_specs=[IN_HBM] * len(quarters) + [IN_VMEM],
        out_specs=IN_VMEM,
        out_shape=jax.ShapeDtypeStruct((quarters[0].shape[1] // planes, turned.shape[0]), F32),
        scratch_shapes=block_scratch(quarters, planes),
        compiler_params=SMALL,
        name="delta_own",
    )(*quarters, turned)


def gathered_kernel(where, parts_ref, out_ref):
    members = parts_ref.shape[0]
    width = out_ref.shape[2]
    total = parts_ref[0]
    for g in range(1, members):
        total += parts_ref[g]
    for i, d in enumerate(ORDER):
        out_ref[lax.bitwise_xor(where[0], d)] = total[:, i * width:(i + 1) * width]


def gathered(where, parts):
    _, part, total = parts.shape
    return pl.pallas_call(
        gathered_kernel,
        in_specs=[pl.BlockSpec(memory_space=pltpu.SMEM), pl.BlockSpec(memory_space=pltpu.VMEM)],
        out_specs=pl.BlockSpec(memory_space=pltpu.VMEM),
        out_shape=jax.ShapeDtypeStruct((len(ORDER), part, total // len(ORDER)), F32),
        compiler_params=FULL,
        name="gathered",
    )(where, parts)


def round_of_ascent(samples, labels, weight, dual, inverse):
    rows = samples.shape[0]
    depth, width = weight.shape
    planes = lax.axis_size(ZH)
    members = lax.axis_size(X) * lax.axis_size(Y)
    quarters = lax.axis_size(ZL) * lax.axis_size(CORE)
    part = rows // quarters
    mine = lax.axis_index(CLS).astype(jnp.int32)
    where = jnp.stack([mine, lax.axis_index(ZH).astype(jnp.int32)])

    packed = pack(samples, where, planes, members, quarters)
    quarter = lax.all_to_all(packed, PLANE, split_axis=0, concat_axis=0, tiled=True)
    near, lines = [weight], []
    for k in range(1, planes):
        near.append(shifted(weight, ZH, k))
    for k in range(planes):
        lines.append(shifted(near[k], ZL, 1))
    by_pair = jnp.concatenate([jnp.concatenate(pair, axis=1) for pair in zip(near, lines)], axis=0)
    by_all = jnp.concatenate([by_pair, shifted(by_pair, CORE, 1)], axis=1)
    gram = lax.dot_general(samples, samples, (((1,), (1,)), ((), ())), preferred_element_type=F32)

    flat = quarter.reshape(members * part, planes * depth)
    early = members * EARLY // 16 * part
    beside_a = shifted(flat[:early], ZL, 1)
    partial = jnp.dot(flat, by_all, preferred_element_type=F32)
    partial = lax.all_to_all(partial.reshape(members, part, quarters * width), PLANE, split_axis=0, concat_axis=0, tiled=True)
    across = shifted(flat, CORE, 1)
    diagonal_a = shifted(beside_a, CORE, 1)
    partial, late = lax.optimization_barrier((partial, flat))
    pieces = gathered(where, partial)
    start = lax.all_to_all(pieces, CLS, split_axis=0, concat_axis=0, tiled=True).reshape(rows, width)
    beside_b = shifted(late[early:], ZL, 1)

    ready = prepare(gram, inverse, width)
    alpha, steps, top = passes(where, start, labels[:, None], dual, ready, members)
    steps = lax.all_to_all(steps, PLANE, split_axis=0, concat_axis=0, tiled=True)
    diagonal_b = shifted(beside_b, CORE, 1)

    top = top[0]
    other = shifted(top, CORE, 1)
    top = jnp.maximum(top, other)
    other = shifted(top, ZL, 1)
    top = jnp.maximum(top, other)

    held = [flat, across, beside_a, beside_b, diagonal_a, diagonal_b]
    far = planes // 2
    sent, turned, gap = first_delta(where, held, steps, planes, far)
    came = [shifted(sent, ZH, planes - far)]
    for k in range(1, planes):
        if k != far:
            sent = next_delta(held, turned, gap, planes, k)
            came.append(shifted(sent, ZH, planes - k))
    own = own_delta(held, turned, planes)
    new_weight, gap = finish(weight, own, gap, came, rows * planes * members)
    return new_weight, alpha, gap[0], top


def solution(mesh):
    fine = Mesh(mesh.devices.reshape(4, 4, 4, 2, 2), (ZH, X, Y, ZL, CORE))
    return jax.shard_map(
        round_of_ascent,
        mesh=fine,
        in_specs=(P(SAMP, None), P(SAMP), P(SAMP, CLS), P(SAMP, CLS), P(SAMP, None, None)),
        out_specs=(P(SAMP, CLS), P(SAMP, CLS), P(CLS), P(SAMP)),
        check_vma=False,
    )
```

time: 158 us -> 171 us (1.082)
  waiting for transfers between devices: 48.7 us -> 77.6 us
  blocking collectives: 18.3 us -> 0 us
  starting transfers between devices: 41.8 us -> 49.4 us
  other arithmetic: 4.33 us -> 1.22 us
    ppermute x18, waiting for transfers between devices: 33.4 us -> 53.1 us  [shifted(): lax.ppermute(value, axis, [(i, (i + by) % size) for i in range(size)])]
    all_to_all x1 -> x0, blocking collectives: 18.3 us -> none  [round_of_ascent(): lax.all_to_all(steps, PLANE, split_axis=0, concat_axis=0, tiled=True)]
    all_to_all x0 -> x1, waiting for transfers between devices: none -> 10.3 us  [round_of_ascent(): lax.all_to_all(steps, PLANE, split_axis=0, concat_axis=0, tiled=True)]
    all_to_all x0 -> x1, starting transfers between devices: none -> 7.24 us  [round_of_ascent(): lax.all_to_all(steps, PLANE, split_axis=0, concat_axis=0, tiled=True)]
    unnamed x26 -> x8, local copies, waits for them, and re-layouts: 1.92 us -> 0.02 us
    pallas_call x6 -> x7, Pallas kernels: 22.8 us -> 23 us  [the longest x1 5.83 us: prepare(): pl.pallas_call(prepare_kernel, grid=(blocks,), in_specs=[pl.BlockSpec((ro...]
  transfers between devices with their start and end apart: 21 -> 22, of which waited for: 10 -> 11; matrix products, arithmetic and copies ran while one was open for 11% -> 7% of each run, Pallas kernels for 9% -> 13%
where the time goes in v2:
time: 171 us; the launch traced here: 170 us
  waiting for transfers between devices  77.6 us (45%)
  starting transfers between devices  49.4 us (29%)
  Pallas kernels  25.8 us (15%)
  matrix products  12.2 us (7%)
  local copies, waits for them, and re-layouts  2.94 us (2%)
    ppermute x18, waiting for transfers between devices, shifted(): lax.ppermute(value, axis, [(i, (i + by) % size) for i in range(size)])  53.1 us
    ppermute x18, starting transfers between devices, shifted(): lax.ppermute(value, axis, [(i, (i + by) % size) for i in range(size)])  23.4 us
    all_to_all x1, waiting for transfers between devices, round_of_ascent(): lax.all_to_all(partial.reshape(members, part, quarters * width), PLANE, s...  14.2 us
    all_to_all x1, waiting for transfers between devices, round_of_ascent(): lax.all_to_all(steps, PLANE, split_axis=0, concat_axis=0, tiled=True)  10.3 us
    dot_general x1, matrix products, round_of_ascent(): lax.dot_general(samples, samples, (((1,), (1,)), ((), ())), preferred_ele...  8.71 us
    all_to_all x1, starting transfers between devices, round_of_ascent(): lax.all_to_all(packed, PLANE, split_axis=0, concat_axis=0, tiled=True)  7.62 us
    all_to_all x1, starting transfers between devices, round_of_ascent(): lax.all_to_all(steps, PLANE, split_axis=0, concat_axis=0, tiled=True)  7.24 us
    all_to_all x1, starting transfers between devices, round_of_ascent(): lax.all_to_all(partial.reshape(members, part, quarters * width), PLANE, s...  7.23 us
  transfers between devices with their start and end apart: 22, of which 11 were waited for; matrix products, arithmetic and copies ran while one was open for 7% of the time, Pallas kernels for 13%

profile of v2, /device:TPU:2, one launch (start us, length us, event | category | flops | bytes accessed | tf_op | source)
XLA Modules:
  0.0 169.9 jit_solution(4236415990959917571)
XLA Ops:
  1.2 3.7 %pack.1 = bf16[16,32,2048]{2,1,0:T(8,128)(2,1)} custom-call(s32[2]{0:T(128)} %pad_add_fusion.where, bf16[128,32768]{1,0:T(8,128)(2,1)} %rows_hbm.1), custom_call_target="tpu_custom_call" | custom-call | tf_op jit(solution)/shard_map/pack/pallas_call | solution.py:67
  4.9 7.6 %all-to-all-start = ((bf16[16,32,2048]{2,1,0:T(8,128)(2,1)}), bf16[16,32,2048]{2,1,0:T(8,128)(2,1)S(1)}, u32[]{:S(2)}, u32[]{:S(2)}) async-start(bf16[16,32,2048]{2,1,0:T(8,128)(2,1)} %pack.1), calls=%async_computation | async-start | bytes 4194304 | tf_op jit(solution)/shard_map/all_to_all | solution.py:410
  12.5 3.3 %collective-permute-start.3 = (bf16[512,128]{1,0:T(8,128)(2,1)S(1)}, bf16[512,128]{1,0:T(8,128)(2,1)S(1)}, u32[]{:S(2)}, u32[]{:S(2)}) collective-permute-start(bf16[512,128]{1,0:T(8,128)(2,1)S(1)} %copy-done), channel_id=1, source_target_pairs={{0,64},{64,128},{128,192},{192,0},{1,65},{65,129},{129,193},{193,1... | collective-permute-start | bytes 393224 | tf_op jit(solution)/shard_map/ppermute | solution.py:34
  15.9 5.4 %collective-permute-start.5 = (bf16[512,128]{1,0:T(8,128)(2,1)S(1)}, bf16[512,128]{1,0:T(8,128)(2,1)S(1)}, u32[]{:S(2)}, u32[]{:S(2)}) collective-permute-start(bf16[512,128]{1,0:T(8,128)(2,1)S(1)} %copy-done), channel_id=1, source_target_pairs={{0,128},{64,192},{128,0},{192,64},{1,129},{65,193},{129,1},{193,65... | collective-permute-start | bytes 393224 | tf_op jit(solution)/shard_map/ppermute | solution.py:34
  21.3 2.7 %collective-permute-start.7 = (bf16[512,128]{1,0:T(8,128)(2,1)S(1)}, bf16[512,128]{1,0:T(8,128)(2,1)S(1)}, u32[]{:S(2)}, u32[]{:S(2)}) collective-permute-start(bf16[512,128]{1,0:T(8,128)(2,1)S(1)} %copy-done), channel_id=1, source_target_pairs={{0,192},{64,0},{128,64},{192,128},{1,193},{65,1},{129,65},{193,129... | collective-permute-start | bytes 393224 | tf_op jit(solution)/shard_map/ppermute | solution.py:34
  26.9 6.4 %collective-permute-done.5 = bf16[512,128]{1,0:T(8,128)(2,1)S(1)} collective-permute-done((bf16[512,128]{1,0:T(8,128)(2,1)S(1)}, bf16[512,128]{1,0:T(8,128)(2,1)S(1)}, u32[]{:S(2)}, u32[]{:S(2)}) %collective-permute-start.5) | collective-permute-done | bytes 131104 | tf_op jit(solution)/shard_map/ppermute | solution.py:34
  36.7 2.8 %collective-permute-done.4 = bf16[512,128]{1,0:T(8,128)(2,1)S(1)} collective-permute-done((bf16[512,128]{1,0:T(8,128)(2,1)S(1)}, bf16[512,128]{1,0:T(8,128)(2,1)S(1)}, u32[]{:S(2)}, u32[]{:S(2)}) %collective-permute-start.4) | collective-permute-done | bytes 131104 | tf_op jit(solution)/shard_map/ppermute | solution.py:34
  39.5 2.8 %collective-permute-done.6 = bf16[512,128]{1,0:T(8,128)(2,1)S(1)} collective-permute-done((bf16[512,128]{1,0:T(8,128)(2,1)S(1)}, bf16[512,128]{1,0:T(8,128)(2,1)S(1)}, u32[]{:S(2)}, u32[]{:S(2)}) %collective-permute-start.6) | collective-permute-done | bytes 131104 | tf_op jit(solution)/shard_map/ppermute | solution.py:34
  44.4 2.8 %collective-permute-done.9 = bf16[2048,256]{1,0:T(8,128)(2,1)} collective-permute-done((bf16[2048,256]{1,0:T(8,128)(2,1)S(1)}, bf16[2048,256]{1,0:T(8,128)(2,1)}, u32[]{:S(2)}, u32[]{:S(2)}) %collective-permute-start.9) | collective-permute-done | bytes 1048608 | tf_op jit(solution)/shard_map/ppermute | solution.py:34
  47.1 3.5 %fusion = f32[16,32,512]{2,1,0:T(8,128)} fusion(bf16[16,32,2048]{2,1,0:T(8,128)(2,1)S(1)} %all-to-all-done, bf16[2048,256]{1,0:T(8,128)(2,1)} %collective-permute-done.9, bf16[512,128]{1,0:T(8,128)(2,1)S(1)} %collective-permute-done.8, bf16[512,128]{1,0:T(8,128)(2,1)S(1)} %collective-permute-done.7, bf16[512,128]{1,0:T(8,128)(2,1)S(1)} %collective-permute-done.6, ...), kind=kOutput, calls=%fused_computation.1 | convolution fusion | flops 1092616192 | bytes 5242880 | tf_op jit(solution)/shard_map/dot_general | solution.py:423
  50.6 7.2 %all-to-all-start.1 = ((f32[16,32,512]{2,1,0:T(8,128)}), f32[16,32,512]{2,1,0:T(8,128)}, u32[]{:S(2)}, u32[]{:S(2)}) async-start(f32[16,32,512]{2,1,0:T(8,128)} %fusion), calls=%async_computation.1 | async-start | bytes 2097152 | tf_op jit(solution)/shard_map/all_to_all | solution.py:424
  59.0 14.2 %all-to-all-done.1.parts_ref = f32[16,32,512]{2,1,0:T(8,128)} async-done(((f32[16,32,512]{2,1,0:T(8,128)}), f32[16,32,512]{2,1,0:T(8,128)}, u32[]{:S(2)}, u32[]{:S(2)}) %all-to-all-start.1) | async-done | bytes 1048608 | tf_op jit(solution)/shard_map/all_to_all | solution.py:424
  76.2 3.9 %all-to-all-start.2 = ((f32[4,32,128]{2,1,0:T(8,128)}), f32[4,32,128]{2,1,0:T(8,128)}, u32[]{:S(2)}, u32[]{:S(2)}) async-start(f32[4,32,128]{2,1,0:T(8,128)} %gathered.1), calls=%async_computation.2 | async-start | bytes 131072 | tf_op jit(solution)/shard_map/all_to_all | solution.py:429
  80.1 10.8 %collective-permute-done.1.refs_2_ = bf16[320,2048]{1,0:T(8,128)(2,1)S(1)} collective-permute-done((bf16[320,2048]{1,0:T(8,128)(2,1)}, bf16[320,2048]{1,0:T(8,128)(2,1)S(1)}, u32[]{:S(2)}, u32[]{:S(2)}) %collective-permute-start.1) | collective-permute-done | bytes 1310752 | tf_op jit(solution)/shard_map/ppermute | solution.py:34
  90.9 15.9 %collective-permute-done.10.refs_3_ = bf16[192,2048]{1,0:T(8,128)(2,1)} collective-permute-done((bf16[192,2048]{1,0:T(8,128)(2,1)}, bf16[192,2048]{1,0:T(8,128)(2,1)}, u32[]{:S(2)}, u32[]{:S(2)}) %collective-permute-start.10) | collective-permute-done | bytes 786464 | tf_op jit(solution)/shard_map/ppermute | solution.py:34
  106.8 8.7 %fusion.18.gram_ref = f32[128,128]{1,0:T(8,128)} fusion(bf16[128,32768]{1,0:T(8,128)(2,1)} %rows_hbm.1), kind=kOutput, calls=%fused_computation.22 | convolution fusion | flops 1073741824 | bytes 8454144 | tf_op jit(solution)/shard_map/dot_general | solution.py:418
  116.3 5.8 %prepare.1 = (f32[8,32,16,128]{3,2,1,0:T(8,128)}, bf16[8,128,96]{2,1,0:T(8,128)(2,1)}) custom-call(f32[128,128]{1,0:T(8,128)} %fusion.18.gram_ref, f32[8,16,16]{2,1,0:T(8,128)} %inverse_ref.1), custom_call_target="tpu_custom_call" | custom-call | tf_op jit(solution)/shard_map/prepare/pallas_call | solution.py:110
  122.1 4.7 %passes.1 = (f32[128,128]{1,0:T(8,128)}, bf16[16,136,128]{2,1,0:T(8,128)(2,1)}, f32[1,128]{1,0:T(1,128)}) custom-call(s32[2]{0:T(128)} %pad_add_fusion.where, f32[128,128]{1,0:T(8,128)} %bitcast.5.start_hbm, s32[128,1]{1,0:T(8,128)} %copy.9.labels_hbm, f32[128,128]{1,0:T(8,128)} %dual_hbm.1, f32[8,32,16,128]{3,2,1,0:T(8,128)} %get-tuple-element.18.expanded_hbm, ...), custom_call_target="tpu_custom_call" | custom-call | tf_op jit(solution)/shard_map/passes/pallas_call | solution.py:200
  126.8 7.2 %all-to-all-start.3 = ((bf16[16,136,128]{2,1,0:T(8,128)(2,1)}), bf16[16,136,128]{2,1,0:T(8,128)(2,1)}, u32[]{:S(2)}, u32[]{:S(2)}) async-start(bf16[16,136,128]{2,1,0:T(8,128)(2,1)} %get-tuple-element.20), calls=%async_computation.3 | async-start | bytes 1114112 | tf_op jit(solution)/shard_map/all_to_all | solution.py:434
  134.1 10.3 %all-to-all-done.3.refs_6_ = bf16[16,136,128]{2,1,0:T(8,128)(2,1)} async-done(((bf16[16,136,128]{2,1,0:T(8,128)(2,1)}), bf16[16,136,128]{2,1,0:T(8,128)(2,1)}, u32[]{:S(2)}, u32[]{:S(2)}) %all-to-all-start.3) | async-done | bytes 557088 | tf_op jit(solution)/shard_map/all_to_all | solution.py:434
  144.4 3.0 %delta_first.1 = (bf16[520,128]{1,0:T(8,128)(2,1)S(1)}, bf16[128,2304]{1,0:T(8,128)(2,1)S(1)}, f32[1,128]{1,0:T(1,128)S(1)}) custom-call(s32[2]{0:T(128)S(1)} %copy-done.1, bf16[512,2048]{1,0:T(8,128)(2,1)S(1)} %bitcast.17, bf16[512,2048]{1,0:T(8,128)(2,1)} %collective-permute-done.refs_1_, bf16[320,2048]{1,0:T(8,128)(2,1)S(1)} %collective-permute-done.1.refs_2_, ...), custom_call_target="tpu_custom_call" | custom-call | tf_op jit(solution)/shard_map/delta_first/pallas_call | solution.py:338
  152.0 3.6 %collective-permute-start.14 = (bf16[520,128]{1,0:T(8,128)(2,1)S(1)}, bf16[520,128]{1,0:T(8,128)(2,1)S(1)}, u32[]{:S(2)}, u32[]{:S(2)}) collective-permute-start(bf16[520,128]{1,0:T(8,128)(2,1)S(1)} %delta_next.2), channel_id=1, source_target_pairs={{0,192},{64,0},{128,64},{192,128},{1,193},{65,1},{129,65},{193,129... | collective-permute-start | bytes 399368 | tf_op jit(solution)/shard_map/ppermute | solution.py:34
  155.6 2.2 %collective-permute-start.13 = (bf16[520,128]{1,0:T(8,128)(2,1)S(1)}, bf16[520,128]{1,0:T(8,128)(2,1)S(1)}, u32[]{:S(2)}, u32[]{:S(2)}) collective-permute-start(bf16[520,128]{1,0:T(8,128)(2,1)S(1)} %get-tuple-element.23), channel_id=1, source_target_pairs={{0,128},{64,192},{128,0},{192,64},{1,129},{65,193},{129,1},{193,65... | collective-permute-start | bytes 399368 | tf_op jit(solution)/shard_map/ppermute | solution.py:34
  158.2 8.4 %collective-permute-done.17 = f32[128]{0:T(128)S(1)} collective-permute-done((f32[128]{0:T(128)S(1)}, f32[128]{0:T(128)S(1)}, u32[]{:S(2)}, u32[]{:S(2)}) %collective-permute-start.17) | collective-permute-done | bytes 544 | tf_op jit(solution)/shard_map/ppermute | solution.py:34
  (46 shorter events, 22.0 us)
Async XLA Ops:
  4.9 42.2 %all-to-all-start = ((bf16[16,32,2048]{2,1,0:T(8,128)(2,1)}), bf16[16,32,2048]{2,1,0:T(8,128)(2,1)S(1)}, u32[]{:S(2)}, u32[]{:S(2)}) async-start(bf16[16,32,2048]{2,1,0:T(8,128)(2,1)} %pack.1), calls=%async_computation | async-start | bytes 4194304 | tf_op jit(solution)/shard_map/all_to_all | solution.py:410
  12.5 12.4 %collective-permute-start.3 = (bf16[512,128]{1,0:T(8,128)(2,1)S(1)}, bf16[512,128]{1,0:T(8,128)(2,1)S(1)}, u32[]{:S(2)}, u32[]{:S(2)}) collective-permute-start(bf16[512,128]{1,0:T(8,128)(2,1)S(1)} %copy-done), channel_id=1, source_target_pairs={{0,64},{64,128},{128,192},{192,0},{1,65},{65,129},{129,193},{193,1... | collective-permute-start | bytes 393224 | tf_op jit(solution)/shard_map/ppermute | solution.py:34
  15.9 17.4 %collective-permute-start.5 = (bf16[512,128]{1,0:T(8,128)(2,1)S(1)}, bf16[512,128]{1,0:T(8,128)(2,1)S(1)}, u32[]{:S(2)}, u32[]{:S(2)}) collective-permute-start(bf16[512,128]{1,0:T(8,128)(2,1)S(1)} %copy-done), channel_id=1, source_target_pairs={{0,128},{64,192},{128,0},{192,64},{1,129},{65,193},{129,1},{193,65... | collective-permute-start | bytes 393224 | tf_op jit(solution)/shard_map/ppermute | solution.py:34
  21.3 12.1 %collective-permute-start.7 = (bf16[512,128]{1,0:T(8,128)(2,1)S(1)}, bf16[512,128]{1,0:T(8,128)(2,1)S(1)}, u32[]{:S(2)}, u32[]{:S(2)}) collective-permute-start(bf16[512,128]{1,0:T(8,128)(2,1)S(1)} %copy-done), channel_id=1, source_target_pairs={{0,192},{64,0},{128,64},{192,128},{1,193},{65,1},{129,65},{193,129... | collective-permute-start | bytes 393224 | tf_op jit(solution)/shard_map/ppermute | solution.py:34
  23.9 12.7 %collective-permute-start.2 = (bf16[512,128]{1,0:T(8,128)(2,1)S(1)}, bf16[512,128]{1,0:T(8,128)(2,1)S(1)}, u32[]{:S(2)}, u32[]{:S(2)}) collective-permute-start(bf16[512,128]{1,0:T(8,128)(2,1)S(1)} %copy-done), channel_id=1, source_target_pairs={{0,2},{2,0},{1,3},{3,1},{4,6},{6,4},{5,7},{7,5},{8,10},{10,8},{9,1... | collective-permute-start | bytes 393224 | tf_op jit(solution)/shard_map/ppermute | solution.py:34
  25.0 14.5 %collective-permute-start.4 = (bf16[512,128]{1,0:T(8,128)(2,1)S(1)}, bf16[512,128]{1,0:T(8,128)(2,1)S(1)}, u32[]{:S(2)}, u32[]{:S(2)}) collective-permute-start(bf16[512,128]{1,0:T(8,128)(2,1)S(1)} %collective-permute-done.3), channel_id=1, source_target_pairs={{0,2},{2,0},{1,3},{3,1},{4,6},{6,4},{5,7},{7,5},{8,10},{10,8},{9,1... | collective-permute-start | bytes 393224 | tf_op jit(solution)/shard_map/ppermute | solution.py:34
  33.3 9.0 %collective-permute-start.6 = (bf16[512,128]{1,0:T(8,128)(2,1)S(1)}, bf16[512,128]{1,0:T(8,128)(2,1)S(1)}, u32[]{:S(2)}, u32[]{:S(2)}) collective-permute-start(bf16[512,128]{1,0:T(8,128)(2,1)S(1)} %collective-permute-done.5), channel_id=1, source_target_pairs={{0,2},{2,0},{1,3},{3,1},{4,6},{6,4},{5,7},{7,5},{8,10},{10,8},{9,1... | collective-permute-start | bytes 393224 | tf_op jit(solution)/shard_map/ppermute | solution.py:34
  33.3 10.8 %collective-permute-start.8 = (bf16[512,128]{1,0:T(8,128)(2,1)S(1)}, bf16[512,128]{1,0:T(8,128)(2,1)S(1)}, u32[]{:S(2)}, u32[]{:S(2)}) collective-permute-start(bf16[512,128]{1,0:T(8,128)(2,1)S(1)} %collective-permute-done.7), channel_id=1, source_target_pairs={{0,2},{2,0},{1,3},{3,1},{4,6},{6,4},{5,7},{7,5},{8,10},{10,8},{9,1... | collective-permute-start | bytes 393224 | tf_op jit(solution)/shard_map/ppermute | solution.py:34
  44.3 2.9 %collective-permute-start.9 = (bf16[2048,256]{1,0:T(8,128)(2,1)S(1)}, bf16[2048,256]{1,0:T(8,128)(2,1)}, u32[]{:S(2)}, u32[]{:S(2)}) collective-permute-start(bf16[2048,256]{1,0:T(8,128)(2,1)S(1)} %maximum_maximum_fusion), channel_id=1, source_target_pairs={{0,1},{1,0},{2,3},{3,2},{4,5},{5,4},{6,7},{7,6},{8,9},{9,8},{10,11... | collective-permute-start | bytes 3145736 | tf_op jit(solution)/shard_map/ppermute | solution.py:34
  50.6 22.6 %all-to-all-start.1 = ((f32[16,32,512]{2,1,0:T(8,128)}), f32[16,32,512]{2,1,0:T(8,128)}, u32[]{:S(2)}, u32[]{:S(2)}) async-start(f32[16,32,512]{2,1,0:T(8,128)} %fusion), calls=%async_computation.1 | async-start | bytes 2097152 | tf_op jit(solution)/shard_map/all_to_all | solution.py:424
  59.0 31.9 %collective-permute-start.1 = (bf16[320,2048]{1,0:T(8,128)(2,1)}, bf16[320,2048]{1,0:T(8,128)(2,1)S(1)}, u32[]{:S(2)}, u32[]{:S(2)}) collective-permute-start(bf16[320,2048]{1,0:T(8,128)(2,1)} %bitcast.3), channel_id=1, source_target_pairs={{0,2},{2,0},{1,3},{3,1},{4,6},{6,4},{5,7},{7,5},{8,10},{10,8},{9,1... | collective-permute-start | bytes 3932168 | tf_op jit(solution)/shard_map/ppermute | solution.py:34
  74.2 32.6 %collective-permute-start.10 = (bf16[192,2048]{1,0:T(8,128)(2,1)}, bf16[192,2048]{1,0:T(8,128)(2,1)}, u32[]{:S(2)}, u32[]{:S(2)}) collective-permute-start(bf16[192,2048]{1,0:T(8,128)(2,1)} %slice.11), channel_id=1, source_target_pairs={{0,2},{2,0},{1,3},{3,1},{4,6},{6,4},{5,7},{7,5},{8,10},{10,8},{9,1... | collective-permute-start | bytes 2359304 | tf_op jit(solution)/shard_map/ppermute | solution.py:34
  74.2 70.2 %collective-permute-start = (bf16[512,2048]{1,0:T(8,128)(2,1)S(1)}, bf16[512,2048]{1,0:T(8,128)(2,1)}, u32[]{:S(2)}, u32[]{:S(2)}) collective-permute-start(bf16[512,2048]{1,0:T(8,128)(2,1)S(1)} %bitcast.16), channel_id=1, source_target_pairs={{0,1},{1,0},{2,3},{3,2},{4,5},{5,4},{6,7},{7,6},{8,9},{9,8},{10,11... | collective-permute-start | bytes 6291464 | tf_op jit(solution)/shard_map/ppermute | solution.py:34
  76.2 46.0 %all-to-all-start.2 = ((f32[4,32,128]{2,1,0:T(8,128)}), f32[4,32,128]{2,1,0:T(8,128)}, u32[]{:S(2)}, u32[]{:S(2)}) async-start(f32[4,32,128]{2,1,0:T(8,128)} %gathered.1), calls=%async_computation.2 | async-start | bytes 131072 | tf_op jit(solution)/shard_map/all_to_all | solution.py:429
  80.1 35.5 %copy-start.2 = (s32[128]{0:T(128)S(1)}, s32[128]{0:T(128)}, u32[]{:S(2)}) copy-start(s32[128]{0:T(128)} %param.6) | copy-start | bytes 1540
  90.9 53.5 %collective-permute-start.11 = (bf16[320,2048]{1,0:T(8,128)(2,1)S(1)}, bf16[320,2048]{1,0:T(8,128)(2,1)}, u32[]{:S(2)}, u32[]{:S(2)}) collective-permute-start(bf16[320,2048]{1,0:T(8,128)(2,1)S(1)} %collective-permute-done.1.refs_2_), channel_id=1, source_target_pairs={{0,1},{1,0},{2,3},{3,2},{4,5},{5,4},{6,7},{7,6},{8,9},{9,8},{10,11... | collective-permute-start | bytes 3932168 | tf_op jit(solution)/shard_map/ppermute | solution.py:34
  106.8 37.6 %collective-permute-start.12 = (bf16[192,2048]{1,0:T(8,128)(2,1)}, bf16[192,2048]{1,0:T(8,128)(2,1)}, u32[]{:S(2)}, u32[]{:S(2)}) collective-permute-start(bf16[192,2048]{1,0:T(8,128)(2,1)} %collective-permute-done.10.refs_3_), channel_id=1, source_target_pairs={{0,1},{1,0},{2,3},{3,2},{4,5},{5,4},{6,7},{7,6},{8,9},{9,8},{10,11... | collective-permute-start | bytes 2359304 | tf_op jit(solution)/shard_map/ppermute | solution.py:34
  115.5 28.9 %copy-start.1 = (s32[2]{0:T(128)S(1)}, s32[2]{0:T(128)}, u32[]{:S(2)}) copy-start(s32[2]{0:T(128)} %pad_add_fusion.where) | copy-start | bytes 28
  126.8 17.6 %all-to-all-start.3 = ((bf16[16,136,128]{2,1,0:T(8,128)(2,1)}), bf16[16,136,128]{2,1,0:T(8,128)(2,1)}, u32[]{:S(2)}, u32[]{:S(2)}) async-start(bf16[16,136,128]{2,1,0:T(8,128)(2,1)} %get-tuple-element.20), calls=%async_computation.3 | async-start | bytes 1114112 | tf_op jit(solution)/shard_map/all_to_all | solution.py:434
  134.1 23.7 %collective-permute-start.16 = (f32[128]{0:T(128)}, f32[128]{0:T(128)S(1)}, u32[]{:S(2)}, u32[]{:S(2)}) collective-permute-start(f32[128]{0:T(128)} %bitcast.22), channel_id=1, source_target_pairs={{0,1},{1,0},{2,3},{3,2},{4,5},{5,4},{6,7},{7,6},{8,9},{9,8},{10,11... | collective-permute-start | bytes 1544 | tf_op jit(solution)/shard_map/ppermute | solution.py:34
  149.4 19.7 %collective-permute-start.15 = (bf16[520,128]{1,0:T(8,128)(2,1)S(1)}, bf16[520,128]{1,0:T(8,128)(2,1)S(1)}, u32[]{:S(2)}, u32[]{:S(2)}) collective-permute-start(bf16[520,128]{1,0:T(8,128)(2,1)S(1)} %delta_next.3), channel_id=1, source_target_pairs={{0,64},{64,128},{128,192},{192,0},{1,65},{65,129},{129,193},{193,1... | collective-permute-start | bytes 399368 | tf_op jit(solution)/shard_map/ppermute | solution.py:34
  152.0 17.1 %collective-permute-start.14 = (bf16[520,128]{1,0:T(8,128)(2,1)S(1)}, bf16[520,128]{1,0:T(8,128)(2,1)S(1)}, u32[]{:S(2)}, u32[]{:S(2)}) collective-permute-start(bf16[520,128]{1,0:T(8,128)(2,1)S(1)} %delta_next.2), channel_id=1, source_target_pairs={{0,192},{64,0},{128,64},{192,128},{1,193},{65,1},{129,65},{193,129... | collective-permute-start | bytes 399368 | tf_op jit(solution)/shard_map/ppermute | solution.py:34
  155.6 13.5 %collective-permute-start.13 = (bf16[520,128]{1,0:T(8,128)(2,1)S(1)}, bf16[520,128]{1,0:T(8,128)(2,1)S(1)}, u32[]{:S(2)}, u32[]{:S(2)}) collective-permute-start(bf16[520,128]{1,0:T(8,128)(2,1)S(1)} %get-tuple-element.23), channel_id=1, source_target_pairs={{0,128},{64,192},{128,0},{192,64},{1,129},{65,193},{129,1},{193,65... | collective-permute-start | bytes 399368 | tf_op jit(solution)/shard_map/ppermute | solution.py:34
  157.8 8.8 %collective-permute-start.17 = (f32[128]{0:T(128)S(1)}, f32[128]{0:T(128)S(1)}, u32[]{:S(2)}, u32[]{:S(2)}) collective-permute-start(f32[128]{0:T(128)S(1)} %bitcast_maximum_fusion), channel_id=1, source_target_pairs={{0,2},{2,0},{1,3},{3,1},{4,6},{6,4},{5,7},{7,5},{8,10},{10,8},{9,1... | collective-permute-start | bytes 1544 | tf_op jit(solution)/shard_map/ppermute | solution.py:34
  (2 other events, 16.1 us)

commit v3 on v2

--- a/solution.py
+++ b/solution.py
@@ -34,7 +34,7 @@
     return lax.ppermute(value, axis, [(i, (i + by) % size) for i in range(size)])
 
 
-def pack_kernel(where, rows_hbm, out_hbm, held_ref, in_sems, out_sems):
+def pack_kernel(where, plane, rows_hbm, out_hbm, held_ref, in_sems, out_sems):
     members, part, total = out_hbm.shape
     planes = in_sems.shape[0]
     width = total // planes
@@ -42,7 +42,7 @@
     row = pl.multiple_of(where[0] * part, part)
     loads = []
     for k in range(planes):
-        low = pl.multiple_of(lax.rem(where[1] + (planes - k), planes) * span, span)
+        low = pl.multiple_of(lax.rem(plane[0] + (planes - k), planes) * span, span)
         loads.append(pltpu.make_async_copy(rows_hbm.at[pl.ds(row, part), pl.ds(low, span)], held_ref.at[k], in_sems.at[k]))
     for load in loads:
         load.start()
@@ -61,12 +61,12 @@
         store.wait()
 
 
-def pack(samples, where, planes, members, quarters):
+def pack(samples, where, plane, planes, members, quarters):
     rows, features = samples.shape
     part = rows // quarters
     return pl.pallas_call(
         pack_kernel,
-        in_specs=[IN_SMEM, IN_HBM],
+        in_specs=[IN_SMEM, IN_SMEM, IN_HBM],
         out_specs=IN_HBM,
         out_shape=jax.ShapeDtypeStruct((members, part, features // members), samples.dtype),
         scratch_shapes=[
@@ -76,7 +76,7 @@
         ],
         compiler_params=FULL,
         name="pack",
-    )(where, samples)
+    )(where, plane, samples)
 
 
 def three_pieces(value):
@@ -136,18 +136,21 @@
     return (sums[0] + sums[1]) + (sums[2] + sums[3])
 
 
-def passes_kernel(where, start_hbm, labels_hbm, dual_hbm, expanded_hbm, wide_hbm, alpha_hbm, steps_hbm, top_hbm,
+def passes_kernel(where, start0, start1, start2, start3, labels_hbm, dual_hbm, expanded_hbm, wide_hbm, alpha_hbm, steps_hbm, top_hbm,
                   margin_ref, labels_ref, dual_ref, expanded_ref, wide_ref, alpha_ref, start_ref, sign_ref, change_ref, payload_ref, top_ref, sems):
     rows, width = margin_ref.shape
     blocks = rows // BLOCK
     copies = [
-        pltpu.make_async_copy(start_hbm, start_ref, sems.at[0]),
-        pltpu.make_async_copy(labels_hbm, labels_ref, sems.at[1]),
-        pltpu.make_async_copy(dual_hbm, dual_ref, sems.at[2]),
+        pltpu.make_async_copy(labels_hbm, labels_ref, sems.at[0]),
+        pltpu.make_async_copy(dual_hbm, dual_ref, sems.at[1]),
     ]
+    for d, piece in enumerate((start0, start1, start2, start3)):
+        part = piece.shape[0]
+        low = pl.multiple_of(lax.bitwise_xor(where[0], d) * part, part)
+        copies.append(pltpu.make_async_copy(piece, start_ref.at[pl.ds(low, part)], sems.at[2 + d]))
     parts = [
-        [pltpu.make_async_copy(expanded_hbm.at[b], expanded_ref.at[b], sems.at[3 + b]),
-         pltpu.make_async_copy(wide_hbm.at[b], wide_ref.at[b], sems.at[3 + blocks + b])]
+        [pltpu.make_async_copy(expanded_hbm.at[b], expanded_ref.at[b], sems.at[6 + b]),
+         pltpu.make_async_copy(wide_hbm.at[b], wide_ref.at[b], sems.at[6 + blocks + b])]
         for b in range(blocks)
     ]
     for copy in copies + [part for pair in parts for part in pair]:
@@ -195,11 +198,11 @@
 
 
 def passes(where, start, labels, dual, ready, members):
-    rows, width = start.shape
+    rows, width = dual.shape
     square = pltpu.VMEM((rows, width), F32)
     return pl.pallas_call(
         passes_kernel,
-        in_specs=[IN_SMEM] + [IN_HBM] * 5,
+        in_specs=[IN_SMEM] + [IN_HBM] * (len(start) + 4),
         out_specs=[IN_HBM] * 3,
         out_shape=[
             jax.ShapeDtypeStruct((rows, width), F32),
@@ -218,11 +221,11 @@
             square,
             pltpu.VMEM((rows + GAP_ROWS, width), BF16),
             pltpu.VMEM((1, rows), F32),
-            pltpu.SemaphoreType.DMA((3 + 2 * (rows // BLOCK),)),
+            pltpu.SemaphoreType.DMA((6 + 2 * (rows // BLOCK),)),
         ],
         compiler_params=FULL,
         name="passes",
-    )(where, start, labels, dual, *ready)
+    )(where, *start, labels, dual, *ready)
 
 
 def tail_of(gap):
@@ -374,26 +377,36 @@
     )(*quarters, turned)
 
 
-def gathered_kernel(where, parts_ref, out_ref):
-    members = parts_ref.shape[0]
-    width = out_ref.shape[2]
+def gathered_kernel(parts_hbm, *refs):
+    *outs, parts_ref, sems = refs
+    width = outs[0].shape[1]
+    copies = [pltpu.make_async_copy(parts_hbm.at[g], parts_ref.at[g], sems.at[g]) for g in range(parts_hbm.shape[0])]
+    for copy in copies:
+        copy.start()
+    copies[0].wait()
     total = parts_ref[0]
-    for g in range(1, members):
+    for g in range(1, len(copies)):
+        copies[g].wait()
         total += parts_ref[g]
     for i, d in enumerate(ORDER):
-        out_ref[lax.bitwise_xor(where[0], d)] = total[:, i * width:(i + 1) * width]
-
-
-def gathered(where, parts):
-    _, part, total = parts.shape
+        outs[d][...] = total[:, i * width:(i + 1) * width]
+
+
+def gathered(parts):
+    members, part, total = parts.shape
     return pl.pallas_call(
         gathered_kernel,
-        in_specs=[pl.BlockSpec(memory_space=pltpu.SMEM), pl.BlockSpec(memory_space=pltpu.VMEM)],
-        out_specs=pl.BlockSpec(memory_space=pltpu.VMEM),
-        out_shape=jax.ShapeDtypeStruct((len(ORDER), part, total // len(ORDER)), F32),
+        in_specs=[IN_HBM],
+        out_specs=[IN_VMEM] * len(ORDER),
+        out_shape=[jax.ShapeDtypeStruct((part, total // len(ORDER)), F32)] * len(ORDER),
+        scratch_shapes=[pltpu.VMEM(parts.shape, F32), pltpu.SemaphoreType.DMA((members,))],
         compiler_params=FULL,
         name="gathered",
-    )(where, parts)
+    )(parts)
+
+
+def self_product(value):
+    return lax.dot_general(value, value, (((1,), (1,)), ((), ())), preferred_element_type=F32)
 
 
 def round_of_ascent(samples, labels, weight, dual, inverse):
@@ -404,33 +417,43 @@
     quarters = lax.axis_size(ZL) * lax.axis_size(CORE)
     part = rows // quarters
     mine = lax.axis_index(CLS).astype(jnp.int32)
-    where = jnp.stack([mine, lax.axis_index(ZH).astype(jnp.int32)])
-
-    packed = pack(samples, where, planes, members, quarters)
+    where = mine.reshape(1)
+    plane = lax.axis_index(ZH).astype(jnp.int32).reshape(1)
+
+    packed = pack(samples, where, plane, planes, members, quarters)
     quarter = lax.all_to_all(packed, PLANE, split_axis=0, concat_axis=0, tiled=True)
-    near, lines = [weight], []
-    for k in range(1, planes):
-        near.append(shifted(weight, ZH, k))
+    from_below = shifted(weight, ZH, 1)
+    from_above = shifted(weight, ZH, -1)
+    far_head = shifted(from_below[:depth // 2], ZH, 1)
+    far_rest = shifted(from_above[depth // 2:], ZH, -1)
+    near = [weight, from_below, jnp.concatenate([far_head, far_rest], axis=0), from_above]
+    lines = []
     for k in range(planes):
         lines.append(shifted(near[k], ZL, 1))
     by_pair = jnp.concatenate([jnp.concatenate(pair, axis=1) for pair in zip(near, lines)], axis=0)
     by_all = jnp.concatenate([by_pair, shifted(by_pair, CORE, 1)], axis=1)
-    gram = lax.dot_general(samples, samples, (((1,), (1,)), ((), ())), preferred_element_type=F32)
+    middle = samples.shape[1] // 2
+    gram_head = self_product(samples[:, :middle])
 
     flat = quarter.reshape(members * part, planes * depth)
     early = members * EARLY // 16 * part
     beside_a = shifted(flat[:early], ZL, 1)
     partial = jnp.dot(flat, by_all, preferred_element_type=F32)
+    partial, late = lax.optimization_barrier((partial, flat))
     partial = lax.all_to_all(partial.reshape(members, part, quarters * width), PLANE, split_axis=0, concat_axis=0, tiled=True)
     across = shifted(flat, CORE, 1)
     diagonal_a = shifted(beside_a, CORE, 1)
-    partial, late = lax.optimization_barrier((partial, flat))
-    pieces = gathered(where, partial)
-    start = lax.all_to_all(pieces, CLS, split_axis=0, concat_axis=0, tiled=True).reshape(rows, width)
-    beside_b = shifted(late[early:], ZL, 1)
-
+    gram = gram_head + self_product(samples[:, middle:])
     ready = prepare(gram, inverse, width)
-    alpha, steps, top = passes(where, start, labels[:, None], dual, ready, members)
+    partial, late, tags = lax.optimization_barrier((partial, late[early:], labels[:, None]))
+    own_piece, by_core, by_line, by_both = gathered(partial)
+    by_line = shifted(by_line, ZL, 1)
+    by_both = lax.ppermute(by_both, CLS, [(i, i ^ 3) for i in range(4)])
+    by_core = shifted(by_core, CORE, 1)
+    start = [own_piece, by_core, by_line, by_both]
+    beside_b = shifted(late, ZL, 1)
+
+    alpha, steps, top = passes(where, start, tags, dual, ready, members)
     steps = lax.all_to_all(steps, PLANE, split_axis=0, concat_axis=0, tiled=True)
     diagonal_b = shifted(beside_b, CORE, 1)
 

time: 171 us -> 167 us (0.977)
  waiting for transfers between devices: 77.6 us -> 62.7 us
  starting transfers between devices: 49.4 us -> 59.1 us
    ppermute x18 -> x21, starting transfers between devices: 23.4 us -> 36.8 us  [shifted(): lax.ppermute(value, axis, [(i, (i + by) % size) for i in range(size)])]
    ppermute x18 -> x21, waiting for transfers between devices: 53.1 us -> 41.1 us  [shifted(): lax.ppermute(value, axis, [(i, (i + by) % size) for i in range(size)])]
    all_to_all x1 -> x0, starting transfers between devices: 3.89 us -> none  [round_of_ascent(): lax.all_to_all(pieces, CLS, split_axis=0, concat_axis=0, tiled=True)]
    all_to_all x1, waiting for transfers between devices: 14.2 us -> 11.2 us  [round_of_ascent(): lax.all_to_all(partial.reshape(members, part, quarters * width), PLANE, s...]
    dot_general x1 -> x2, matrix products: 8.71 us -> 10.1 us  [self_product(): lax.dot_general(value, value, (((1,), (1,)), ((), ())), preferred_element...]
  transfers between devices with their start and end apart: 22 -> 25, of which waited for: 11 -> 10; matrix products, arithmetic and copies ran while one was open for 7% -> 9% of each run, Pallas kernels for 13% -> 13%
where the time goes in v3:
time: 167 us; the launch traced here: 165 us
  waiting for transfers between devices  62.7 us (38%)
  starting transfers between devices  59.1 us (35%)
  Pallas kernels  24.6 us (15%)
  matrix products  13.5 us (8%)
  local copies, waits for them, and re-layouts  3.59 us (2%)
    ppermute x21, waiting for transfers between devices, shifted(): lax.ppermute(value, axis, [(i, (i + by) % size) for i in range(size)])  41.1 us
    ppermute x21, starting transfers between devices, shifted(): lax.ppermute(value, axis, [(i, (i + by) % size) for i in range(size)])  36.8 us
    all_to_all x1, waiting for transfers between devices, round_of_ascent(): lax.all_to_all(partial.reshape(members, part, quarters * width), PLANE, s...  11.2 us
    all_to_all x1, waiting for transfers between devices, round_of_ascent(): lax.all_to_all(steps, PLANE, split_axis=0, concat_axis=0, tiled=True)  10.3 us
    dot_general x2, matrix products, self_product(): lax.dot_general(value, value, (((1,), (1,)), ((), ())), preferred_element...  10.1 us
    all_to_all x1, starting transfers between devices, round_of_ascent(): lax.all_to_all(packed, PLANE, split_axis=0, concat_axis=0, tiled=True)  7.62 us
    all_to_all x1, starting transfers between devices, round_of_ascent(): lax.all_to_all(steps, PLANE, split_axis=0, concat_axis=0, tiled=True)  7.24 us
    all_to_all x1, starting transfers between devices, round_of_ascent(): lax.all_to_all(partial.reshape(members, part, quarters * width), PLANE, s...  7.23 us
  transfers between devices with their start and end apart: 25, of which 10 were waited for; matrix products, arithmetic and copies ran while one was open for 9% of the time, Pallas kernels for 13%

profile of v3, /device:TPU:2, one launch (start us, length us, event | category | flops | bytes accessed | tf_op | source)
XLA Modules:
  0.0 164.9 jit_solution(18431717572655695434)
XLA Ops:
  0.6 3.0 %pack.1 = bf16[16,32,2048]{2,1,0:T(8,128)(2,1)} custom-call(s32[1]{0:T(128)} %bitcast.where, s32[1]{0:T(128)} %bitcast.1.plane, bf16[128,32768]{1,0:T(8,128)(2,1)} %rows_hbm.1), custom_call_target="tpu_custom_call" | custom-call | tf_op jit(solution)/shard_map/pack/pallas_call | solution.py:67
  3.7 7.6 %all-to-all-start = ((bf16[16,32,2048]{2,1,0:T(8,128)(2,1)}), bf16[16,32,2048]{2,1,0:T(8,128)(2,1)S(1)}, u32[]{:S(2)}, u32[]{:S(2)}) async-start(bf16[16,32,2048]{2,1,0:T(8,128)(2,1)} %pack.1), calls=%async_computation | async-start | bytes 4194304 | tf_op jit(solution)/shard_map/all_to_all | solution.py:424
  11.3 3.3 %collective-permute-start.3 = (bf16[512,128]{1,0:T(8,128)(2,1)S(1)}, bf16[512,128]{1,0:T(8,128)(2,1)S(1)}, u32[]{:S(2)}, u32[]{:S(2)}) collective-permute-start(bf16[512,128]{1,0:T(8,128)(2,1)S(1)} %copy-done), channel_id=1, source_target_pairs={{0,64},{64,128},{128,192},{192,0},{1,65},{65,129},{129,193},{193,1... | collective-permute-start | bytes 393224 | tf_op jit(solution)/shard_map/ppermute | solution.py:34
  14.6 3.1 %collective-permute-start.6 = (bf16[512,128]{1,0:T(8,128)(2,1)S(1)}, bf16[512,128]{1,0:T(8,128)(2,1)S(1)}, u32[]{:S(2)}, u32[]{:S(2)}) collective-permute-start(bf16[512,128]{1,0:T(8,128)(2,1)S(1)} %copy-done), channel_id=1, source_target_pairs={{0,192},{64,0},{128,64},{192,128},{1,193},{65,1},{129,65},{193,129... | collective-permute-start | bytes 393224 | tf_op jit(solution)/shard_map/ppermute | solution.py:34
  17.8 3.4 %collective-permute-done.3 = bf16[512,128]{1,0:T(8,128)(2,1)S(1)} collective-permute-done((bf16[512,128]{1,0:T(8,128)(2,1)S(1)}, bf16[512,128]{1,0:T(8,128)(2,1)S(1)}, u32[]{:S(2)}, u32[]{:S(2)}) %collective-permute-start.3) | collective-permute-done | bytes 131104 | tf_op jit(solution)/shard_map/ppermute | solution.py:34
  24.6 4.1 %collective-permute-start.7 = (bf16[256,128]{1,0:T(8,128)(2,1)S(1)}, bf16[256,128]{1,0:T(8,128)(2,1)S(1)}, u32[]{:S(2)}, u32[]{:S(2)}) collective-permute-start(bf16[256,128]{1,0:T(8,128)(2,1)S(1)} %slice.30), channel_id=1, source_target_pairs={{0,192},{64,0},{128,64},{192,128},{1,193},{65,1},{129,65},{193,129... | collective-permute-start | bytes 196616 | tf_op jit(solution)/shard_map/ppermute | solution.py:34
  31.6 6.1 %collective-permute-start.8 = (bf16[512,128]{1,0:T(8,128)(2,1)S(1)}, bf16[512,128]{1,0:T(8,128)(2,1)S(1)}, u32[]{:S(2)}, u32[]{:S(2)}) collective-permute-start(bf16[512,128]{1,0:T(8,128)(2,1)S(1)} %constant_dynamic-update-slice_fusion), channel_id=1, source_target_pairs={{0,2},{2,0},{1,3},{3,1},{4,6},{6,4},{5,7},{7,5},{8,10},{10,8},{9,1... | collective-permute-start | bytes 393224 | tf_op jit(solution)/shard_map/ppermute | solution.py:34
  37.9 2.8 %collective-permute-done.8 = bf16[512,128]{1,0:T(8,128)(2,1)S(1)} collective-permute-done((bf16[512,128]{1,0:T(8,128)(2,1)S(1)}, bf16[512,128]{1,0:T(8,128)(2,1)S(1)}, u32[]{:S(2)}, u32[]{:S(2)}) %collective-permute-start.8) | collective-permute-done | bytes 131104 | tf_op jit(solution)/shard_map/ppermute | solution.py:34
  40.9 2.8 %collective-permute-done.10 = bf16[2048,256]{1,0:T(8,128)(2,1)} collective-permute-done((bf16[2048,256]{1,0:T(8,128)(2,1)S(1)}, bf16[2048,256]{1,0:T(8,128)(2,1)}, u32[]{:S(2)}, u32[]{:S(2)}) %collective-permute-start.10) | collective-permute-done | bytes 1048608 | tf_op jit(solution)/shard_map/ppermute | solution.py:34
  43.7 3.5 %fusion.4 = f32[512,512]{1,0:T(8,128)} fusion(bf16[512,2048]{1,0:T(8,128)(2,1)S(1)} %bitcast.10, bf16[2048,256]{1,0:T(8,128)(2,1)} %collective-permute-done.10, bf16[512,128]{1,0:T(8,128)(2,1)S(1)} %collective-permute-done.9, bf16[512,128]{1,0:T(8,128)(2,1)S(1)} %collective-permute-done.6, bf16[512,128]{1,0:T(8,128)(2,1)S(1)} %collective-permute-done.8, ...), kind=kOutput, calls=%fused_computation.4 | convolution fusion | flops 1092616192 | bytes 5242880 | tf_op jit(solution)/shard_map/dot_general | solution.py:441
  47.1 7.2 %all-to-all-start.1 = ((f32[16,32,512]{2,1,0:T(8,128)}), f32[16,32,512]{2,1,0:T(8,128)}, u32[]{:S(2)}, u32[]{:S(2)}) async-start(f32[16,32,512]{2,1,0:T(8,128)} %bitcast.4), calls=%async_computation.1 | async-start | bytes 2097152 | tf_op jit(solution)/shard_map/all_to_all | solution.py:443
  58.6 11.2 %all-to-all-done.1.parts_hbm = f32[16,32,512]{2,1,0:T(8,128)} async-done(((f32[16,32,512]{2,1,0:T(8,128)}), f32[16,32,512]{2,1,0:T(8,128)}, u32[]{:S(2)}, u32[]{:S(2)}) %all-to-all-start.1) | async-done | bytes 1048608 | tf_op jit(solution)/shard_map/all_to_all | solution.py:443
  73.9 13.5 %collective-permute-done.1.refs_2_ = bf16[320,2048]{1,0:T(8,128)(2,1)S(1)} collective-permute-done((bf16[320,2048]{1,0:T(8,128)(2,1)}, bf16[320,2048]{1,0:T(8,128)(2,1)S(1)}, u32[]{:S(2)}, u32[]{:S(2)}) %collective-permute-start.1) | collective-permute-done | bytes 1310752 | tf_op jit(solution)/shard_map/ppermute | solution.py:34
  87.4 4.7 %fusion = f32[128,128]{1,0:T(8,128)S(1)} fusion(bf16[128,32768]{1,0:T(8,128)(2,1)} %rows_hbm.1), kind=kOutput, calls=%fused_computation | convolution fusion | flops 536870912 | bytes 4259840 | tf_op jit(solution)/shard_map/dot_general | solution.py:409
  94.7 9.0 %collective-permute-done.11.refs_3_ = bf16[192,2048]{1,0:T(8,128)(2,1)} collective-permute-done((bf16[192,2048]{1,0:T(8,128)(2,1)}, bf16[192,2048]{1,0:T(8,128)(2,1)}, u32[]{:S(2)}, u32[]{:S(2)}) %collective-permute-start.11) | collective-permute-done | bytes 786464 | tf_op jit(solution)/shard_map/ppermute | solution.py:34
  103.6 5.4 %fusion.22.gram_ref = f32[128,128]{1,0:T(8,128)} fusion(f32[128,128]{1,0:T(8,128)S(1)} %fusion, bf16[128,32768]{1,0:T(8,128)(2,1)} %rows_hbm.1), kind=kOutput, calls=%fused_computation.22 | convolution fusion | flops 536887296 | bytes 4325376 | tf_op jit(solution)/shard_map/dot_general | solution.py:409
  109.0 5.8 %prepare.1 = (f32[8,32,16,128]{3,2,1,0:T(8,128)}, bf16[8,128,96]{2,1,0:T(8,128)(2,1)}) custom-call(f32[128,128]{1,0:T(8,128)} %fusion.22.gram_ref, f32[8,16,16]{2,1,0:T(8,128)} %inverse_ref.1), custom_call_target="tpu_custom_call" | custom-call | tf_op jit(solution)/shard_map/prepare/pallas_call | solution.py:110
  116.2 4.1 %passes.1 = (f32[128,128]{1,0:T(8,128)}, bf16[16,136,128]{2,1,0:T(8,128)(2,1)}, f32[1,128]{1,0:T(1,128)}) custom-call(s32[1]{0:T(128)} %bitcast.where, f32[32,128]{1,0:T(8,128)} %get-tuple-element.27.start0, f32[32,128]{1,0:T(8,128)} %copy-done.1, f32[32,128]{1,0:T(8,128)} %collective-permute-done.15.start2, f32[32,128]{1,0:T(8,128)} %collective-permute-done.16.start3, ...), custom_call_target="tpu_custom_call" | custom-call | tf_op jit(solution)/shard_map/passes/pallas_call | solution.py:203
  120.4 7.2 %all-to-all-start.2 = ((bf16[16,136,128]{2,1,0:T(8,128)(2,1)}), bf16[16,136,128]{2,1,0:T(8,128)(2,1)}, u32[]{:S(2)}, u32[]{:S(2)}) async-start(bf16[16,136,128]{2,1,0:T(8,128)(2,1)} %get-tuple-element.34), calls=%async_computation.2 | async-start | bytes 1114112 | tf_op jit(solution)/shard_map/all_to_all | solution.py:457
  127.6 10.3 %all-to-all-done.2.refs_6_ = bf16[16,136,128]{2,1,0:T(8,128)(2,1)} async-done(((bf16[16,136,128]{2,1,0:T(8,128)(2,1)}), bf16[16,136,128]{2,1,0:T(8,128)(2,1)}, u32[]{:S(2)}, u32[]{:S(2)}) %all-to-all-start.2) | async-done | bytes 557088 | tf_op jit(solution)/shard_map/all_to_all | solution.py:457
  137.9 3.0 %delta_first.1 = (bf16[520,128]{1,0:T(8,128)(2,1)S(1)}, bf16[128,2304]{1,0:T(8,128)(2,1)S(1)}, f32[1,128]{1,0:T(1,128)S(1)}) custom-call(s32[1]{0:T(128)} %bitcast.where, bf16[512,2048]{1,0:T(8,128)(2,1)S(1)} %bitcast.13, bf16[512,2048]{1,0:T(8,128)(2,1)} %collective-permute-done.refs_1_, bf16[320,2048]{1,0:T(8,128)(2,1)S(1)} %collective-permute-done.1.refs_2_, ...), custom_call_target="tpu_custom_call" | custom-call | tf_op jit(solution)/shard_map/delta_first/pallas_call | solution.py:341
  142.9 3.0 %collective-permute-start.19 = (bf16[520,128]{1,0:T(8,128)(2,1)S(1)}, bf16[520,128]{1,0:T(8,128)(2,1)S(1)}, u32[]{:S(2)}, u32[]{:S(2)}) collective-permute-start(bf16[520,128]{1,0:T(8,128)(2,1)S(1)} %delta_next.3), channel_id=1, source_target_pairs={{0,64},{64,128},{128,192},{192,0},{1,65},{65,129},{129,193},{193,1... | collective-permute-start | bytes 399368 | tf_op jit(solution)/shard_map/ppermute | solution.py:34
  149.1 3.6 %collective-permute-start.17 = (bf16[520,128]{1,0:T(8,128)(2,1)S(1)}, bf16[520,128]{1,0:T(8,128)(2,1)S(1)}, u32[]{:S(2)}, u32[]{:S(2)}) collective-permute-start(bf16[520,128]{1,0:T(8,128)(2,1)S(1)} %get-tuple-element.37), channel_id=1, source_target_pairs={{0,128},{64,192},{128,0},{192,64},{1,129},{65,193},{129,1},{193,65... | collective-permute-start | bytes 399368 | tf_op jit(solution)/shard_map/ppermute | solution.py:34
  153.0 8.6 %collective-permute-done.21 = f32[128]{0:T(128)S(1)} collective-permute-done((f32[128]{0:T(128)S(1)}, f32[128]{0:T(128)S(1)}, u32[]{:S(2)}, u32[]{:S(2)}) %collective-permute-start.21) | collective-permute-done | bytes 544 | tf_op jit(solution)/shard_map/ppermute | solution.py:34
  (54 shorter events, 27.7 us)
Async XLA Ops:
  3.7 40.0 %all-to-all-start = ((bf16[16,32,2048]{2,1,0:T(8,128)(2,1)}), bf16[16,32,2048]{2,1,0:T(8,128)(2,1)S(1)}, u32[]{:S(2)}, u32[]{:S(2)}) async-start(bf16[16,32,2048]{2,1,0:T(8,128)(2,1)} %pack.1), calls=%async_computation | async-start | bytes 4194304 | tf_op jit(solution)/shard_map/all_to_all | solution.py:424
  11.3 9.9 %collective-permute-start.3 = (bf16[512,128]{1,0:T(8,128)(2,1)S(1)}, bf16[512,128]{1,0:T(8,128)(2,1)S(1)}, u32[]{:S(2)}, u32[]{:S(2)}) collective-permute-start(bf16[512,128]{1,0:T(8,128)(2,1)S(1)} %copy-done), channel_id=1, source_target_pairs={{0,64},{64,128},{128,192},{192,0},{1,65},{65,129},{129,193},{193,1... | collective-permute-start | bytes 393224 | tf_op jit(solution)/shard_map/ppermute | solution.py:34
  14.6 10.0 %collective-permute-start.6 = (bf16[512,128]{1,0:T(8,128)(2,1)S(1)}, bf16[512,128]{1,0:T(8,128)(2,1)S(1)}, u32[]{:S(2)}, u32[]{:S(2)}) collective-permute-start(bf16[512,128]{1,0:T(8,128)(2,1)S(1)} %copy-done), channel_id=1, source_target_pairs={{0,192},{64,0},{128,64},{192,128},{1,193},{65,1},{129,65},{193,129... | collective-permute-start | bytes 393224 | tf_op jit(solution)/shard_map/ppermute | solution.py:34
  21.2 9.5 %collective-permute-start.5 = (bf16[256,128]{1,0:T(8,128)(2,1)S(1)}, bf16[256,128]{1,0:T(8,128)(2,1)S(1)}, u32[]{:S(2)}, u32[]{:S(2)}) collective-permute-start(bf16[256,128]{1,0:T(8,128)(2,1)S(1)} %slice.29), channel_id=1, source_target_pairs={{0,64},{64,128},{128,192},{192,0},{1,65},{65,129},{129,193},{193,1... | collective-permute-start | bytes 196616 | tf_op jit(solution)/shard_map/ppermute | solution.py:34
  23.8 13.9 %collective-permute-start.2 = (bf16[512,128]{1,0:T(8,128)(2,1)S(1)}, bf16[512,128]{1,0:T(8,128)(2,1)S(1)}, u32[]{:S(2)}, u32[]{:S(2)}) collective-permute-start(bf16[512,128]{1,0:T(8,128)(2,1)S(1)} %copy-done), channel_id=1, source_target_pairs={{0,2},{2,0},{1,3},{3,1},{4,6},{6,4},{5,7},{7,5},{8,10},{10,8},{9,1... | collective-permute-start | bytes 393224 | tf_op jit(solution)/shard_map/ppermute | solution.py:34
  24.6 7.0 %collective-permute-start.7 = (bf16[256,128]{1,0:T(8,128)(2,1)S(1)}, bf16[256,128]{1,0:T(8,128)(2,1)S(1)}, u32[]{:S(2)}, u32[]{:S(2)}) collective-permute-start(bf16[256,128]{1,0:T(8,128)(2,1)S(1)} %slice.30), channel_id=1, source_target_pairs={{0,192},{64,0},{128,64},{192,128},{1,193},{65,1},{129,65},{193,129... | collective-permute-start | bytes 196616 | tf_op jit(solution)/shard_map/ppermute | solution.py:34
  28.7 9.0 %collective-permute-start.4 = (bf16[512,128]{1,0:T(8,128)(2,1)S(1)}, bf16[512,128]{1,0:T(8,128)(2,1)S(1)}, u32[]{:S(2)}, u32[]{:S(2)}) collective-permute-start(bf16[512,128]{1,0:T(8,128)(2,1)S(1)} %collective-permute-done.3), channel_id=1, source_target_pairs={{0,2},{2,0},{1,3},{3,1},{4,6},{6,4},{5,7},{7,5},{8,10},{10,8},{9,1... | collective-permute-start | bytes 393224 | tf_op jit(solution)/shard_map/ppermute | solution.py:34
  28.7 9.2 %collective-permute-start.9 = (bf16[512,128]{1,0:T(8,128)(2,1)S(1)}, bf16[512,128]{1,0:T(8,128)(2,1)S(1)}, u32[]{:S(2)}, u32[]{:S(2)}) collective-permute-start(bf16[512,128]{1,0:T(8,128)(2,1)S(1)} %collective-permute-done.6), channel_id=1, source_target_pairs={{0,2},{2,0},{1,3},{3,1},{4,6},{6,4},{5,7},{7,5},{8,10},{10,8},{9,1... | collective-permute-start | bytes 393224 | tf_op jit(solution)/shard_map/ppermute | solution.py:34
  31.6 9.1 %collective-permute-start.8 = (bf16[512,128]{1,0:T(8,128)(2,1)S(1)}, bf16[512,128]{1,0:T(8,128)(2,1)S(1)}, u32[]{:S(2)}, u32[]{:S(2)}) collective-permute-start(bf16[512,128]{1,0:T(8,128)(2,1)S(1)} %constant_dynamic-update-slice_fusion), channel_id=1, source_target_pairs={{0,2},{2,0},{1,3},{3,1},{4,6},{6,4},{5,7},{7,5},{8,10},{10,8},{9,1... | collective-permute-start | bytes 393224 | tf_op jit(solution)/shard_map/ppermute | solution.py:34
  47.1 22.7 %all-to-all-start.1 = ((f32[16,32,512]{2,1,0:T(8,128)}), f32[16,32,512]{2,1,0:T(8,128)}, u32[]{:S(2)}, u32[]{:S(2)}) async-start(f32[16,32,512]{2,1,0:T(8,128)} %bitcast.4), calls=%async_computation.1 | async-start | bytes 2097152 | tf_op jit(solution)/shard_map/all_to_all | solution.py:443
  55.6 31.9 %collective-permute-start.1 = (bf16[320,2048]{1,0:T(8,128)(2,1)}, bf16[320,2048]{1,0:T(8,128)(2,1)S(1)}, u32[]{:S(2)}, u32[]{:S(2)}) collective-permute-start(bf16[320,2048]{1,0:T(8,128)(2,1)} %bitcast.3), channel_id=1, source_target_pairs={{0,2},{2,0},{1,3},{3,1},{4,6},{6,4},{5,7},{7,5},{8,10},{10,8},{9,1... | collective-permute-start | bytes 3932168 | tf_op jit(solution)/shard_map/ppermute | solution.py:34
  57.6 80.3 %collective-permute-start = (bf16[512,2048]{1,0:T(8,128)(2,1)S(1)}, bf16[512,2048]{1,0:T(8,128)(2,1)}, u32[]{:S(2)}, u32[]{:S(2)}) collective-permute-start(bf16[512,2048]{1,0:T(8,128)(2,1)S(1)} %bitcast.11), channel_id=1, source_target_pairs={{0,1},{1,0},{2,3},{3,2},{4,5},{5,4},{6,7},{7,6},{8,9},{9,8},{10,11... | collective-permute-start | bytes 6291464 | tf_op jit(solution)/shard_map/ppermute | solution.py:34
  69.8 33.8 %collective-permute-start.11 = (bf16[192,2048]{1,0:T(8,128)(2,1)}, bf16[192,2048]{1,0:T(8,128)(2,1)}, u32[]{:S(2)}, u32[]{:S(2)}) collective-permute-start(bf16[192,2048]{1,0:T(8,128)(2,1)} %slice.25), channel_id=1, source_target_pairs={{0,2},{2,0},{1,3},{3,1},{4,6},{6,4},{5,7},{7,5},{8,10},{10,8},{9,1... | collective-permute-start | bytes 2359304 | tf_op jit(solution)/shard_map/ppermute | solution.py:34
  73.8 20.6 %collective-permute-start.14 = (f32[32,128]{1,0:T(8,128)}, f32[32,128]{1,0:T(8,128)S(1)}, u32[]{:S(2)}, u32[]{:S(2)}) collective-permute-start(f32[32,128]{1,0:T(8,128)} %get-tuple-element.28), channel_id=1, source_target_pairs={{0,1},{1,0},{2,3},{3,2},{4,5},{5,4},{6,7},{7,6},{8,9},{9,8},{10,11... | collective-permute-start | bytes 49160 | tf_op jit(solution)/shard_map/ppermute | solution.py:34
  87.4 50.5 %collective-permute-start.12 = (bf16[320,2048]{1,0:T(8,128)(2,1)S(1)}, bf16[320,2048]{1,0:T(8,128)(2,1)}, u32[]{:S(2)}, u32[]{:S(2)}) collective-permute-start(bf16[320,2048]{1,0:T(8,128)(2,1)S(1)} %collective-permute-done.1.refs_2_), channel_id=1, source_target_pairs={{0,1},{1,0},{2,3},{3,2},{4,5},{5,4},{6,7},{7,6},{8,9},{9,8},{10,11... | collective-permute-start | bytes 3932168 | tf_op jit(solution)/shard_map/ppermute | solution.py:34
  92.2 24.0 %collective-permute-start.15 = (f32[32,128]{1,0:T(8,128)}, f32[32,128]{1,0:T(8,128)}, u32[]{:S(2)}, u32[]{:S(2)}) collective-permute-start(f32[32,128]{1,0:T(8,128)} %get-tuple-element.29), channel_id=1, source_target_pairs={{0,2},{2,0},{1,3},{3,1},{4,6},{6,4},{5,7},{7,5},{8,10},{10,8},{9,1... | collective-permute-start | bytes 49160 | tf_op jit(solution)/shard_map/ppermute | solution.py:34
  94.5 21.8 %collective-permute-start.16 = (f32[32,128]{1,0:T(8,128)}, f32[32,128]{1,0:T(8,128)}, u32[]{:S(2)}, u32[]{:S(2)}) collective-permute-start(f32[32,128]{1,0:T(8,128)} %get-tuple-element.30), channel_id=1, source_target_pairs={{0,3},{1,2},{2,1},{3,0},{4,7},{5,6},{6,5},{7,4},{8,11},{9,10},{10,... | collective-permute-start | bytes 49160 | tf_op jit(solution)/shard_map/ppermute | solution.py:451
  103.6 34.3 %collective-permute-start.13 = (bf16[192,2048]{1,0:T(8,128)(2,1)}, bf16[192,2048]{1,0:T(8,128)(2,1)}, u32[]{:S(2)}, u32[]{:S(2)}) collective-permute-start(bf16[192,2048]{1,0:T(8,128)(2,1)} %collective-permute-done.11.refs_3_), channel_id=1, source_target_pairs={{0,1},{1,0},{2,3},{3,2},{4,5},{5,4},{6,7},{7,6},{8,9},{9,8},{10,11... | collective-permute-start | bytes 2359304 | tf_op jit(solution)/shard_map/ppermute | solution.py:34
  120.4 17.6 %all-to-all-start.2 = ((bf16[16,136,128]{2,1,0:T(8,128)(2,1)}), bf16[16,136,128]{2,1,0:T(8,128)(2,1)}, u32[]{:S(2)}, u32[]{:S(2)}) async-start(bf16[16,136,128]{2,1,0:T(8,128)(2,1)} %get-tuple-element.34), calls=%async_computation.2 | async-start | bytes 1114112 | tf_op jit(solution)/shard_map/all_to_all | solution.py:457
  127.6 25.1 %collective-permute-start.20 = (f32[128]{0:T(128)}, f32[128]{0:T(128)S(1)}, u32[]{:S(2)}, u32[]{:S(2)}) collective-permute-start(f32[128]{0:T(128)} %bitcast.18), channel_id=1, source_target_pairs={{0,1},{1,0},{2,3},{3,2},{4,5},{5,4},{6,7},{7,6},{8,9},{9,8},{10,11... | collective-permute-start | bytes 1544 | tf_op jit(solution)/shard_map/ppermute | solution.py:34
  142.9 21.2 %collective-permute-start.19 = (bf16[520,128]{1,0:T(8,128)(2,1)S(1)}, bf16[520,128]{1,0:T(8,128)(2,1)S(1)}, u32[]{:S(2)}, u32[]{:S(2)}) collective-permute-start(bf16[520,128]{1,0:T(8,128)(2,1)S(1)} %delta_next.3), channel_id=1, source_target_pairs={{0,64},{64,128},{128,192},{192,0},{1,65},{65,129},{129,193},{193,1... | collective-permute-start | bytes 399368 | tf_op jit(solution)/shard_map/ppermute | solution.py:34
  147.8 16.3 %collective-permute-start.18 = (bf16[520,128]{1,0:T(8,128)(2,1)S(1)}, bf16[520,128]{1,0:T(8,128)(2,1)S(1)}, u32[]{:S(2)}, u32[]{:S(2)}) collective-permute-start(bf16[520,128]{1,0:T(8,128)(2,1)S(1)} %delta_next.2), channel_id=1, source_target_pairs={{0,192},{64,0},{128,64},{192,128},{1,193},{65,1},{129,65},{193,129... | collective-permute-start | bytes 399368 | tf_op jit(solution)/shard_map/ppermute | solution.py:34
  149.1 15.0 %collective-permute-start.17 = (bf16[520,128]{1,0:T(8,128)(2,1)S(1)}, bf16[520,128]{1,0:T(8,128)(2,1)S(1)}, u32[]{:S(2)}, u32[]{:S(2)}) collective-permute-start(bf16[520,128]{1,0:T(8,128)(2,1)S(1)} %get-tuple-element.37), channel_id=1, source_target_pairs={{0,128},{64,192},{128,0},{192,64},{1,129},{65,193},{129,1},{193,65... | collective-permute-start | bytes 399368 | tf_op jit(solution)/shard_map/ppermute | solution.py:34
  152.7 8.9 %collective-permute-start.21 = (f32[128]{0:T(128)S(1)}, f32[128]{0:T(128)S(1)}, u32[]{:S(2)}, u32[]{:S(2)}) collective-permute-start(f32[128]{0:T(128)S(1)} %bitcast_maximum_fusion), channel_id=1, source_target_pairs={{0,2},{2,0},{1,3},{3,1},{4,6},{6,4},{5,7},{7,5},{8,10},{10,8},{9,1... | collective-permute-start | bytes 1544 | tf_op jit(solution)/shard_map/ppermute | solution.py:34
  (4 other events, 34.9 us)

commit v4 on v3

--- a/solution.py
+++ b/solution.py
@@ -159,7 +159,8 @@
     for copy in copies:
         copy.wait()
     class_ids = where[0] * width + lax.broadcasted_iota(jnp.int32, (rows, width), 1)
-    sign_ref[...] = jnp.where(labels_ref[...] == class_ids, 1.0, -1.0).astype(F32)
+    tags = jnp.broadcast_to(labels_ref[...].astype(F32), (width, rows)).T
+    sign_ref[...] = jnp.where(tags == class_ids.astype(F32), 1.0, -1.0)
     margin_ref[...] = start_ref[...]
     alpha_ref[...] = dual_ref[...]
     margin = start_ref[:BLOCK]
@@ -445,7 +446,7 @@
     diagonal_a = shifted(beside_a, CORE, 1)
     gram = gram_head + self_product(samples[:, middle:])
     ready = prepare(gram, inverse, width)
-    partial, late, tags = lax.optimization_barrier((partial, late[early:], labels[:, None]))
+    partial, late = lax.optimization_barrier((partial, late[early:]))
     own_piece, by_core, by_line, by_both = gathered(partial)
     by_line = shifted(by_line, ZL, 1)
     by_both = lax.ppermute(by_both, CLS, [(i, i ^ 3) for i in range(4)])
@@ -453,7 +454,7 @@
     start = [own_piece, by_core, by_line, by_both]
     beside_b = shifted(late, ZL, 1)
 
-    alpha, steps, top = passes(where, start, tags, dual, ready, members)
+    alpha, steps, top = passes(where, start, labels[None, :], dual, ready, members)
     steps = lax.all_to_all(steps, PLANE, split_axis=0, concat_axis=0, tiled=True)
     diagonal_b = shifted(beside_b, CORE, 1)
 

time: 167 us -> 166 us (level)
  transfers between devices with their start and end apart: 25 -> 25, of which waited for: 10 -> 10; matrix products, arithmetic and copies ran while one was open for 9% -> 8% of each run, Pallas kernels for 13% -> 13%
where the time goes in v4:
time: 166 us; the launch traced here: 164 us
  waiting for transfers between devices  62.6 us (38%)
  starting transfers between devices  59.1 us (36%)
  Pallas kernels  24.6 us (15%)
  matrix products  13.5 us (8%)
  local copies, waits for them, and re-layouts  2.8 us (2%)
    ppermute x21, waiting for transfers between devices, shifted(): lax.ppermute(value, axis, [(i, (i + by) % size) for i in range(size)])  41.1 us
    ppermute x21, starting transfers between devices, shifted(): lax.ppermute(value, axis, [(i, (i + by) % size) for i in range(size)])  36.8 us
    all_to_all x1, waiting for transfers between devices, round_of_ascent(): lax.all_to_all(partial.reshape(members, part, quarters * width), PLANE, s...  11.3 us
    all_to_all x1, waiting for transfers between devices, round_of_ascent(): lax.all_to_all(steps, PLANE, split_axis=0, concat_axis=0, tiled=True)  10.3 us
    dot_general x2, matrix products, self_product(): lax.dot_general(value, value, (((1,), (1,)), ((), ())), preferred_element...  10.1 us
    all_to_all x1, starting transfers between devices, round_of_ascent(): lax.all_to_all(packed, PLANE, split_axis=0, concat_axis=0, tiled=True)  7.62 us
    all_to_all x1, starting transfers between devices, round_of_ascent(): lax.all_to_all(steps, PLANE, split_axis=0, concat_axis=0, tiled=True)  7.24 us
    all_to_all x1, starting transfers between devices, round_of_ascent(): lax.all_to_all(partial.reshape(members, part, quarters * width), PLANE, s...  7.23 us
  transfers between devices with their start and end apart: 25, of which 10 were waited for; matrix products, arithmetic and copies ran while one was open for 8% of the time, Pallas kernels for 13%

profile of v4, /device:TPU:2, one launch (start us, length us, event | category | flops | bytes accessed | tf_op | source)
XLA Modules:
  0.0 164.1 jit_solution(10675407851188673069)
XLA Ops:
  0.6 3.0 %pack.1 = bf16[16,32,2048]{2,1,0:T(8,128)(2,1)} custom-call(s32[1]{0:T(128)} %bitcast.where, s32[1]{0:T(128)} %bitcast.1.plane, bf16[128,32768]{1,0:T(8,128)(2,1)} %rows_hbm.1), custom_call_target="tpu_custom_call" | custom-call | tf_op jit(solution)/shard_map/pack/pallas_call | solution.py:67
  3.7 7.6 %all-to-all-start = ((bf16[16,32,2048]{2,1,0:T(8,128)(2,1)}), bf16[16,32,2048]{2,1,0:T(8,128)(2,1)S(1)}, u32[]{:S(2)}, u32[]{:S(2)}) async-start(bf16[16,32,2048]{2,1,0:T(8,128)(2,1)} %pack.1), calls=%async_computation | async-start | bytes 4194304 | tf_op jit(solution)/shard_map/all_to_all | solution.py:425
  11.3 3.3 %collective-permute-start.3 = (bf16[512,128]{1,0:T(8,128)(2,1)S(1)}, bf16[512,128]{1,0:T(8,128)(2,1)S(1)}, u32[]{:S(2)}, u32[]{:S(2)}) collective-permute-start(bf16[512,128]{1,0:T(8,128)(2,1)S(1)} %copy-done), channel_id=1, source_target_pairs={{0,64},{64,128},{128,192},{192,0},{1,65},{65,129},{129,193},{193,1... | collective-permute-start | bytes 393224 | tf_op jit(solution)/shard_map/ppermute | solution.py:34
  14.7 3.1 %collective-permute-start.6 = (bf16[512,128]{1,0:T(8,128)(2,1)S(1)}, bf16[512,128]{1,0:T(8,128)(2,1)S(1)}, u32[]{:S(2)}, u32[]{:S(2)}) collective-permute-start(bf16[512,128]{1,0:T(8,128)(2,1)S(1)} %copy-done), channel_id=1, source_target_pairs={{0,192},{64,0},{128,64},{192,128},{1,193},{65,1},{129,65},{193,129... | collective-permute-start | bytes 393224 | tf_op jit(solution)/shard_map/ppermute | solution.py:34
  17.8 3.4 %collective-permute-done.3 = bf16[512,128]{1,0:T(8,128)(2,1)S(1)} collective-permute-done((bf16[512,128]{1,0:T(8,128)(2,1)S(1)}, bf16[512,128]{1,0:T(8,128)(2,1)S(1)}, u32[]{:S(2)}, u32[]{:S(2)}) %collective-permute-start.3) | collective-permute-done | bytes 131104 | tf_op jit(solution)/shard_map/ppermute | solution.py:34
  24.6 4.1 %collective-permute-start.7 = (bf16[256,128]{1,0:T(8,128)(2,1)S(1)}, bf16[256,128]{1,0:T(8,128)(2,1)S(1)}, u32[]{:S(2)}, u32[]{:S(2)}) collective-permute-start(bf16[256,128]{1,0:T(8,128)(2,1)S(1)} %slice.30), channel_id=1, source_target_pairs={{0,192},{64,0},{128,64},{192,128},{1,193},{65,1},{129,65},{193,129... | collective-permute-start | bytes 196616 | tf_op jit(solution)/shard_map/ppermute | solution.py:34
  31.6 6.1 %collective-permute-start.8 = (bf16[512,128]{1,0:T(8,128)(2,1)S(1)}, bf16[512,128]{1,0:T(8,128)(2,1)S(1)}, u32[]{:S(2)}, u32[]{:S(2)}) collective-permute-start(bf16[512,128]{1,0:T(8,128)(2,1)S(1)} %constant_dynamic-update-slice_fusion), channel_id=1, source_target_pairs={{0,2},{2,0},{1,3},{3,1},{4,6},{6,4},{5,7},{7,5},{8,10},{10,8},{9,1... | collective-permute-start | bytes 393224 | tf_op jit(solution)/shard_map/ppermute | solution.py:34
  37.9 2.8 %collective-permute-done.8 = bf16[512,128]{1,0:T(8,128)(2,1)S(1)} collective-permute-done((bf16[512,128]{1,0:T(8,128)(2,1)S(1)}, bf16[512,128]{1,0:T(8,128)(2,1)S(1)}, u32[]{:S(2)}, u32[]{:S(2)}) %collective-permute-start.8) | collective-permute-done | bytes 131104 | tf_op jit(solution)/shard_map/ppermute | solution.py:34
  40.9 2.8 %collective-permute-done.10 = bf16[2048,256]{1,0:T(8,128)(2,1)} collective-permute-done((bf16[2048,256]{1,0:T(8,128)(2,1)S(1)}, bf16[2048,256]{1,0:T(8,128)(2,1)}, u32[]{:S(2)}, u32[]{:S(2)}) %collective-permute-start.10) | collective-permute-done | bytes 1048608 | tf_op jit(solution)/shard_map/ppermute | solution.py:34
  43.7 3.5 %fusion.4 = f32[512,512]{1,0:T(8,128)} fusion(bf16[512,2048]{1,0:T(8,128)(2,1)S(1)} %bitcast.10, bf16[2048,256]{1,0:T(8,128)(2,1)} %collective-permute-done.10, bf16[512,128]{1,0:T(8,128)(2,1)S(1)} %collective-permute-done.9, bf16[512,128]{1,0:T(8,128)(2,1)S(1)} %collective-permute-done.6, bf16[512,128]{1,0:T(8,128)(2,1)S(1)} %collective-permute-done.8, ...), kind=kOutput, calls=%fused_computation.4 | convolution fusion | flops 1092616192 | bytes 5242880 | tf_op jit(solution)/shard_map/dot_general | solution.py:442
  47.2 7.2 %all-to-all-start.1 = ((f32[16,32,512]{2,1,0:T(8,128)}), f32[16,32,512]{2,1,0:T(8,128)}, u32[]{:S(2)}, u32[]{:S(2)}) async-start(f32[16,32,512]{2,1,0:T(8,128)} %bitcast.4), calls=%async_computation.1 | async-start | bytes 2097152 | tf_op jit(solution)/shard_map/all_to_all | solution.py:444
  58.6 11.3 %all-to-all-done.1.parts_hbm = f32[16,32,512]{2,1,0:T(8,128)} async-done(((f32[16,32,512]{2,1,0:T(8,128)}), f32[16,32,512]{2,1,0:T(8,128)}, u32[]{:S(2)}, u32[]{:S(2)}) %all-to-all-start.1) | async-done | bytes 1048608 | tf_op jit(solution)/shard_map/all_to_all | solution.py:444
  74.0 13.5 %collective-permute-done.1.refs_2_ = bf16[320,2048]{1,0:T(8,128)(2,1)S(1)} collective-permute-done((bf16[320,2048]{1,0:T(8,128)(2,1)}, bf16[320,2048]{1,0:T(8,128)(2,1)S(1)}, u32[]{:S(2)}, u32[]{:S(2)}) %collective-permute-start.1) | collective-permute-done | bytes 1310752 | tf_op jit(solution)/shard_map/ppermute | solution.py:34
  87.4 4.7 %fusion = f32[128,128]{1,0:T(8,128)S(1)} fusion(bf16[128,32768]{1,0:T(8,128)(2,1)} %rows_hbm.1), kind=kOutput, calls=%fused_computation | convolution fusion | flops 536870912 | bytes 4259840 | tf_op jit(solution)/shard_map/dot_general | solution.py:410
  94.7 8.9 %collective-permute-done.11.refs_3_ = bf16[192,2048]{1,0:T(8,128)(2,1)} collective-permute-done((bf16[192,2048]{1,0:T(8,128)(2,1)}, bf16[192,2048]{1,0:T(8,128)(2,1)}, u32[]{:S(2)}, u32[]{:S(2)}) %collective-permute-start.11) | collective-permute-done | bytes 786464 | tf_op jit(solution)/shard_map/ppermute | solution.py:34
  103.6 5.4 %fusion.22.gram_ref = f32[128,128]{1,0:T(8,128)} fusion(f32[128,128]{1,0:T(8,128)S(1)} %fusion, bf16[128,32768]{1,0:T(8,128)(2,1)} %rows_hbm.1), kind=kOutput, calls=%fused_computation.22 | convolution fusion | flops 536887296 | bytes 4325376 | tf_op jit(solution)/shard_map/dot_general | solution.py:410
  109.0 5.8 %prepare.1 = (f32[8,32,16,128]{3,2,1,0:T(8,128)}, bf16[8,128,96]{2,1,0:T(8,128)(2,1)}) custom-call(f32[128,128]{1,0:T(8,128)} %fusion.22.gram_ref, f32[8,16,16]{2,1,0:T(8,128)} %inverse_ref.1), custom_call_target="tpu_custom_call" | custom-call | tf_op jit(solution)/shard_map/prepare/pallas_call | solution.py:110
  115.5 4.1 %passes.1 = (f32[128,128]{1,0:T(8,128)}, bf16[16,136,128]{2,1,0:T(8,128)(2,1)}, f32[1,128]{1,0:T(1,128)}) custom-call(s32[1]{0:T(128)} %bitcast.where, f32[32,128]{1,0:T(8,128)} %get-tuple-element.26.start0, f32[32,128]{1,0:T(8,128)} %copy-done.1, f32[32,128]{1,0:T(8,128)} %copy-done.2, f32[32,128]{1,0:T(8,128)} %copy-done.3, s32[1,128]{1,0:T(1,128)} %bitcast.17, ...), custom_call_target="tpu_custom_call" | custom-call | tf_op jit(solution)/shard_map/passes/pallas_call | solution.py:204
  119.6 7.2 %all-to-all-start.2 = ((bf16[16,136,128]{2,1,0:T(8,128)(2,1)}), bf16[16,136,128]{2,1,0:T(8,128)(2,1)}, u32[]{:S(2)}, u32[]{:S(2)}) async-start(bf16[16,136,128]{2,1,0:T(8,128)(2,1)} %get-tuple-element.32), calls=%async_computation.2 | async-start | bytes 1114112 | tf_op jit(solution)/shard_map/all_to_all | solution.py:458
  126.8 10.3 %all-to-all-done.2.refs_6_ = bf16[16,136,128]{2,1,0:T(8,128)(2,1)} async-done(((bf16[16,136,128]{2,1,0:T(8,128)(2,1)}), bf16[16,136,128]{2,1,0:T(8,128)(2,1)}, u32[]{:S(2)}, u32[]{:S(2)}) %all-to-all-start.2) | async-done | bytes 557088 | tf_op jit(solution)/shard_map/all_to_all | solution.py:458
  137.2 3.0 %delta_first.1 = (bf16[520,128]{1,0:T(8,128)(2,1)S(1)}, bf16[128,2304]{1,0:T(8,128)(2,1)S(1)}, f32[1,128]{1,0:T(1,128)S(1)}) custom-call(s32[1]{0:T(128)} %bitcast.where, bf16[512,2048]{1,0:T(8,128)(2,1)S(1)} %bitcast.13, bf16[512,2048]{1,0:T(8,128)(2,1)} %collective-permute-done.refs_1_, bf16[320,2048]{1,0:T(8,128)(2,1)S(1)} %collective-permute-done.1.refs_2_, ...), custom_call_target="tpu_custom_call" | custom-call | tf_op jit(solution)/shard_map/delta_first/pallas_call | solution.py:342
  142.1 3.0 %collective-permute-start.19 = (bf16[520,128]{1,0:T(8,128)(2,1)S(1)}, bf16[520,128]{1,0:T(8,128)(2,1)S(1)}, u32[]{:S(2)}, u32[]{:S(2)}) collective-permute-start(bf16[520,128]{1,0:T(8,128)(2,1)S(1)} %delta_next.3), channel_id=1, source_target_pairs={{0,64},{64,128},{128,192},{192,0},{1,65},{65,129},{129,193},{193,1... | collective-permute-start | bytes 399368 | tf_op jit(solution)/shard_map/ppermute | solution.py:34
  148.3 3.6 %collective-permute-start.17 = (bf16[520,128]{1,0:T(8,128)(2,1)S(1)}, bf16[520,128]{1,0:T(8,128)(2,1)S(1)}, u32[]{:S(2)}, u32[]{:S(2)}) collective-permute-start(bf16[520,128]{1,0:T(8,128)(2,1)S(1)} %get-tuple-element.35), channel_id=1, source_target_pairs={{0,128},{64,192},{128,0},{192,64},{1,129},{65,193},{129,1},{193,65... | collective-permute-start | bytes 399368 | tf_op jit(solution)/shard_map/ppermute | solution.py:34
  152.3 8.6 %collective-permute-done.21 = f32[128]{0:T(128)S(1)} collective-permute-done((f32[128]{0:T(128)S(1)}, f32[128]{0:T(128)S(1)}, u32[]{:S(2)}, u32[]{:S(2)}) %collective-permute-start.21) | collective-permute-done | bytes 544 | tf_op jit(solution)/shard_map/ppermute | solution.py:34
  (61 shorter events, 26.9 us)
Async XLA Ops:
  3.7 40.0 %all-to-all-start = ((bf16[16,32,2048]{2,1,0:T(8,128)(2,1)}), bf16[16,32,2048]{2,1,0:T(8,128)(2,1)S(1)}, u32[]{:S(2)}, u32[]{:S(2)}) async-start(bf16[16,32,2048]{2,1,0:T(8,128)(2,1)} %pack.1), calls=%async_computation | async-start | bytes 4194304 | tf_op jit(solution)/shard_map/all_to_all | solution.py:425
  11.3 9.9 %collective-permute-start.3 = (bf16[512,128]{1,0:T(8,128)(2,1)S(1)}, bf16[512,128]{1,0:T(8,128)(2,1)S(1)}, u32[]{:S(2)}, u32[]{:S(2)}) collective-permute-start(bf16[512,128]{1,0:T(8,128)(2,1)S(1)} %copy-done), channel_id=1, source_target_pairs={{0,64},{64,128},{128,192},{192,0},{1,65},{65,129},{129,193},{193,1... | collective-permute-start | bytes 393224 | tf_op jit(solution)/shard_map/ppermute | solution.py:34
  14.7 10.0 %collective-permute-start.6 = (bf16[512,128]{1,0:T(8,128)(2,1)S(1)}, bf16[512,128]{1,0:T(8,128)(2,1)S(1)}, u32[]{:S(2)}, u32[]{:S(2)}) collective-permute-start(bf16[512,128]{1,0:T(8,128)(2,1)S(1)} %copy-done), channel_id=1, source_target_pairs={{0,192},{64,0},{128,64},{192,128},{1,193},{65,1},{129,65},{193,129... | collective-permute-start | bytes 393224 | tf_op jit(solution)/shard_map/ppermute | solution.py:34
  21.2 9.5 %collective-permute-start.5 = (bf16[256,128]{1,0:T(8,128)(2,1)S(1)}, bf16[256,128]{1,0:T(8,128)(2,1)S(1)}, u32[]{:S(2)}, u32[]{:S(2)}) collective-permute-start(bf16[256,128]{1,0:T(8,128)(2,1)S(1)} %slice.29), channel_id=1, source_target_pairs={{0,64},{64,128},{128,192},{192,0},{1,65},{65,129},{129,193},{193,1... | collective-permute-start | bytes 196616 | tf_op jit(solution)/shard_map/ppermute | solution.py:34
  23.9 13.9 %collective-permute-start.2 = (bf16[512,128]{1,0:T(8,128)(2,1)S(1)}, bf16[512,128]{1,0:T(8,128)(2,1)S(1)}, u32[]{:S(2)}, u32[]{:S(2)}) collective-permute-start(bf16[512,128]{1,0:T(8,128)(2,1)S(1)} %copy-done), channel_id=1, source_target_pairs={{0,2},{2,0},{1,3},{3,1},{4,6},{6,4},{5,7},{7,5},{8,10},{10,8},{9,1... | collective-permute-start | bytes 393224 | tf_op jit(solution)/shard_map/ppermute | solution.py:34
  24.6 7.0 %collective-permute-start.7 = (bf16[256,128]{1,0:T(8,128)(2,1)S(1)}, bf16[256,128]{1,0:T(8,128)(2,1)S(1)}, u32[]{:S(2)}, u32[]{:S(2)}) collective-permute-start(bf16[256,128]{1,0:T(8,128)(2,1)S(1)} %slice.30), channel_id=1, source_target_pairs={{0,192},{64,0},{128,64},{192,128},{1,193},{65,1},{129,65},{193,129... | collective-permute-start | bytes 196616 | tf_op jit(solution)/shard_map/ppermute | solution.py:34
  28.7 9.0 %collective-permute-start.4 = (bf16[512,128]{1,0:T(8,128)(2,1)S(1)}, bf16[512,128]{1,0:T(8,128)(2,1)S(1)}, u32[]{:S(2)}, u32[]{:S(2)}) collective-permute-start(bf16[512,128]{1,0:T(8,128)(2,1)S(1)} %collective-permute-done.3), channel_id=1, source_target_pairs={{0,2},{2,0},{1,3},{3,1},{4,6},{6,4},{5,7},{7,5},{8,10},{10,8},{9,1... | collective-permute-start | bytes 393224 | tf_op jit(solution)/shard_map/ppermute | solution.py:34
  28.7 9.2 %collective-permute-start.9 = (bf16[512,128]{1,0:T(8,128)(2,1)S(1)}, bf16[512,128]{1,0:T(8,128)(2,1)S(1)}, u32[]{:S(2)}, u32[]{:S(2)}) collective-permute-start(bf16[512,128]{1,0:T(8,128)(2,1)S(1)} %collective-permute-done.6), channel_id=1, source_target_pairs={{0,2},{2,0},{1,3},{3,1},{4,6},{6,4},{5,7},{7,5},{8,10},{10,8},{9,1... | collective-permute-start | bytes 393224 | tf_op jit(solution)/shard_map/ppermute | solution.py:34
  31.6 9.1 %collective-permute-start.8 = (bf16[512,128]{1,0:T(8,128)(2,1)S(1)}, bf16[512,128]{1,0:T(8,128)(2,1)S(1)}, u32[]{:S(2)}, u32[]{:S(2)}) collective-permute-start(bf16[512,128]{1,0:T(8,128)(2,1)S(1)} %constant_dynamic-update-slice_fusion), channel_id=1, source_target_pairs={{0,2},{2,0},{1,3},{3,1},{4,6},{6,4},{5,7},{7,5},{8,10},{10,8},{9,1... | collective-permute-start | bytes 393224 | tf_op jit(solution)/shard_map/ppermute | solution.py:34
  47.2 22.7 %all-to-all-start.1 = ((f32[16,32,512]{2,1,0:T(8,128)}), f32[16,32,512]{2,1,0:T(8,128)}, u32[]{:S(2)}, u32[]{:S(2)}) async-start(f32[16,32,512]{2,1,0:T(8,128)} %bitcast.4), calls=%async_computation.1 | async-start | bytes 2097152 | tf_op jit(solution)/shard_map/all_to_all | solution.py:444
  55.6 31.9 %collective-permute-start.1 = (bf16[320,2048]{1,0:T(8,128)(2,1)}, bf16[320,2048]{1,0:T(8,128)(2,1)S(1)}, u32[]{:S(2)}, u32[]{:S(2)}) collective-permute-start(bf16[320,2048]{1,0:T(8,128)(2,1)} %bitcast.3), channel_id=1, source_target_pairs={{0,2},{2,0},{1,3},{3,1},{4,6},{6,4},{5,7},{7,5},{8,10},{10,8},{9,1... | collective-permute-start | bytes 3932168 | tf_op jit(solution)/shard_map/ppermute | solution.py:34
  57.6 79.5 %collective-permute-start = (bf16[512,2048]{1,0:T(8,128)(2,1)S(1)}, bf16[512,2048]{1,0:T(8,128)(2,1)}, u32[]{:S(2)}, u32[]{:S(2)}) collective-permute-start(bf16[512,2048]{1,0:T(8,128)(2,1)S(1)} %bitcast.11), channel_id=1, source_target_pairs={{0,1},{1,0},{2,3},{3,2},{4,5},{5,4},{6,7},{7,6},{8,9},{9,8},{10,11... | collective-permute-start | bytes 6291464 | tf_op jit(solution)/shard_map/ppermute | solution.py:34
  69.8 33.8 %collective-permute-start.11 = (bf16[192,2048]{1,0:T(8,128)(2,1)}, bf16[192,2048]{1,0:T(8,128)(2,1)}, u32[]{:S(2)}, u32[]{:S(2)}) collective-permute-start(bf16[192,2048]{1,0:T(8,128)(2,1)} %slice.25), channel_id=1, source_target_pairs={{0,2},{2,0},{1,3},{3,1},{4,6},{6,4},{5,7},{7,5},{8,10},{10,8},{9,1... | collective-permute-start | bytes 2359304 | tf_op jit(solution)/shard_map/ppermute | solution.py:34
  73.9 20.6 %collective-permute-start.14 = (f32[32,128]{1,0:T(8,128)}, f32[32,128]{1,0:T(8,128)S(1)}, u32[]{:S(2)}, u32[]{:S(2)}) collective-permute-start(f32[32,128]{1,0:T(8,128)} %get-tuple-element.27), channel_id=1, source_target_pairs={{0,1},{1,0},{2,3},{3,2},{4,5},{5,4},{6,7},{7,6},{8,9},{9,8},{10,11... | collective-permute-start | bytes 49160 | tf_op jit(solution)/shard_map/ppermute | solution.py:34
  87.4 49.7 %collective-permute-start.12 = (bf16[320,2048]{1,0:T(8,128)(2,1)S(1)}, bf16[320,2048]{1,0:T(8,128)(2,1)}, u32[]{:S(2)}, u32[]{:S(2)}) collective-permute-start(bf16[320,2048]{1,0:T(8,128)(2,1)S(1)} %collective-permute-done.1.refs_2_), channel_id=1, source_target_pairs={{0,1},{1,0},{2,3},{3,2},{4,5},{5,4},{6,7},{7,6},{8,9},{9,8},{10,11... | collective-permute-start | bytes 3932168 | tf_op jit(solution)/shard_map/ppermute | solution.py:34
  92.2 22.7 %collective-permute-start.15 = (f32[32,128]{1,0:T(8,128)S(1)}, f32[32,128]{1,0:T(8,128)S(1)}, u32[]{:S(2)}, u32[]{:S(2)}) collective-permute-start(f32[32,128]{1,0:T(8,128)S(1)} %copy-done.5), channel_id=1, source_target_pairs={{0,2},{2,0},{1,3},{3,1},{4,6},{6,4},{5,7},{7,5},{8,10},{10,8},{9,1... | collective-permute-start | bytes 49160 | tf_op jit(solution)/shard_map/ppermute | solution.py:34
  94.5 20.4 %collective-permute-start.16 = (f32[32,128]{1,0:T(8,128)S(1)}, f32[32,128]{1,0:T(8,128)S(1)}, u32[]{:S(2)}, u32[]{:S(2)}) collective-permute-start(f32[32,128]{1,0:T(8,128)S(1)} %copy-done.4), channel_id=1, source_target_pairs={{0,3},{1,2},{2,1},{3,0},{4,7},{5,6},{6,5},{7,4},{8,11},{9,10},{10,... | collective-permute-start | bytes 49160 | tf_op jit(solution)/shard_map/ppermute | solution.py:452
  103.6 33.5 %collective-permute-start.13 = (bf16[192,2048]{1,0:T(8,128)(2,1)}, bf16[192,2048]{1,0:T(8,128)(2,1)}, u32[]{:S(2)}, u32[]{:S(2)}) collective-permute-start(bf16[192,2048]{1,0:T(8,128)(2,1)} %collective-permute-done.11.refs_3_), channel_id=1, source_target_pairs={{0,1},{1,0},{2,3},{3,2},{4,5},{5,4},{6,7},{7,6},{8,9},{9,8},{10,11... | collective-permute-start | bytes 2359304 | tf_op jit(solution)/shard_map/ppermute | solution.py:34
  119.6 17.6 %all-to-all-start.2 = ((bf16[16,136,128]{2,1,0:T(8,128)(2,1)}), bf16[16,136,128]{2,1,0:T(8,128)(2,1)}, u32[]{:S(2)}, u32[]{:S(2)}) async-start(bf16[16,136,128]{2,1,0:T(8,128)(2,1)} %get-tuple-element.32), calls=%async_computation.2 | async-start | bytes 1114112 | tf_op jit(solution)/shard_map/all_to_all | solution.py:458
  126.8 25.1 %collective-permute-start.20 = (f32[128]{0:T(128)}, f32[128]{0:T(128)S(1)}, u32[]{:S(2)}, u32[]{:S(2)}) collective-permute-start(f32[128]{0:T(128)} %bitcast.18), channel_id=1, source_target_pairs={{0,1},{1,0},{2,3},{3,2},{4,5},{5,4},{6,7},{7,6},{8,9},{9,8},{10,11... | collective-permute-start | bytes 1544 | tf_op jit(solution)/shard_map/ppermute | solution.py:34
  142.1 21.2 %collective-permute-start.19 = (bf16[520,128]{1,0:T(8,128)(2,1)S(1)}, bf16[520,128]{1,0:T(8,128)(2,1)S(1)}, u32[]{:S(2)}, u32[]{:S(2)}) collective-permute-start(bf16[520,128]{1,0:T(8,128)(2,1)S(1)} %delta_next.3), channel_id=1, source_target_pairs={{0,64},{64,128},{128,192},{192,0},{1,65},{65,129},{129,193},{193,1... | collective-permute-start | bytes 399368 | tf_op jit(solution)/shard_map/ppermute | solution.py:34
  147.0 16.3 %collective-permute-start.18 = (bf16[520,128]{1,0:T(8,128)(2,1)S(1)}, bf16[520,128]{1,0:T(8,128)(2,1)S(1)}, u32[]{:S(2)}, u32[]{:S(2)}) collective-permute-start(bf16[520,128]{1,0:T(8,128)(2,1)S(1)} %delta_next.2), channel_id=1, source_target_pairs={{0,192},{64,0},{128,64},{192,128},{1,193},{65,1},{129,65},{193,129... | collective-permute-start | bytes 399368 | tf_op jit(solution)/shard_map/ppermute | solution.py:34
  148.3 15.0 %collective-permute-start.17 = (bf16[520,128]{1,0:T(8,128)(2,1)S(1)}, bf16[520,128]{1,0:T(8,128)(2,1)S(1)}, u32[]{:S(2)}, u32[]{:S(2)}) collective-permute-start(bf16[520,128]{1,0:T(8,128)(2,1)S(1)} %get-tuple-element.35), channel_id=1, source_target_pairs={{0,128},{64,192},{128,0},{192,64},{1,129},{65,193},{129,1},{193,65... | collective-permute-start | bytes 399368 | tf_op jit(solution)/shard_map/ppermute | solution.py:34
  151.9 8.9 %collective-permute-start.21 = (f32[128]{0:T(128)S(1)}, f32[128]{0:T(128)S(1)}, u32[]{:S(2)}, u32[]{:S(2)}) collective-permute-start(f32[128]{0:T(128)S(1)} %bitcast_maximum_fusion), channel_id=1, source_target_pairs={{0,2},{2,0},{1,3},{3,1},{4,6},{6,4},{5,7},{7,5},{8,10},{10,8},{9,1... | collective-permute-start | bytes 1544 | tf_op jit(solution)/shard_map/ppermute | solution.py:34
  (8 other events, 75.0 us)

commit v5 on v4

--- a/solution.py
+++ b/solution.py
@@ -406,6 +406,91 @@
     )(parts)
 
 
+def streamed(rows_hbm, weights_hbm, rows_ref, weights_ref, total_ref, sems, halves):
+    chunks, _, depth = rows_ref.shape
+    loads, stores = [], []
+    for k in range(chunks):
+        loads.append(pltpu.make_async_copy(rows_hbm.at[:, pl.ds(k * depth, depth)], rows_ref.at[k], sems.at[2 * k]))
+        loads.append(pltpu.make_async_copy(weights_hbm.at[pl.ds(k * depth, depth)], weights_ref.at[k], sems.at[2 * k + 1]))
+    for load in loads:
+        load.start()
+    for k in range(chunks):
+        loads[2 * k].wait()
+        at = 0
+        for h, half in enumerate(halves):
+            count = half.shape[0]
+            stores.append(pltpu.make_async_copy(
+                rows_ref.at[k, pl.ds(at, count)], half.at[:, pl.ds(k * depth, depth)], sems.at[2 * chunks + len(halves) * k + h]
+            ))
+            stores[-1].start()
+            at += count
+        loads[2 * k + 1].wait()
+        term = jnp.dot(rows_ref[k], weights_ref[k], preferred_element_type=F32)
+        if k == 0:
+            total_ref[...] = term
+        else:
+            total_ref[...] += term
+    return stores
+
+
+def first_product_kernel(rows_hbm, weights_hbm, half_hbm, early_hbm, late_hbm, rows_ref, weights_ref, total_ref, sems):
+    stores = streamed(rows_hbm, weights_hbm, rows_ref, weights_ref, total_ref, sems, (early_hbm, late_hbm))
+    stores.append(pltpu.make_async_copy(total_ref, half_hbm, sems.at[0]))
+    stores[-1].start()
+    for store in stores:
+        store.wait()
+
+
+def second_product_kernel(rows_hbm, weights_hbm, half_ref, out_hbm, rows_ref, weights_ref, total_ref, sems):
+    width = total_ref.shape[1]
+    begun = pltpu.make_async_copy(half_ref, out_hbm.at[:, pl.ds(0, width)], sems.at[2 * rows_ref.shape[0]])
+    begun.start()
+    streamed(rows_hbm, weights_hbm, rows_ref, weights_ref, total_ref, sems, ())
+    store = pltpu.make_async_copy(total_ref, out_hbm.at[:, pl.ds(width, width)], sems.at[0])
+    store.start()
+    store.wait()
+    begun.wait()
+
+
+def product_scratch(rows, weights, chunks):
+    depth = rows.shape[1] // chunks
+    return [
+        pltpu.VMEM((chunks, rows.shape[0], depth), BF16),
+        pltpu.VMEM((chunks, depth, weights.shape[1]), BF16),
+        pltpu.VMEM((rows.shape[0], weights.shape[1]), F32),
+        pltpu.SemaphoreType.DMA((4 * chunks,)),
+    ]
+
+
+def first_product(rows, weights, chunks, early):
+    count, features = rows.shape
+    return pl.pallas_call(
+        first_product_kernel,
+        in_specs=[IN_HBM] * 2,
+        out_specs=[IN_HBM] * 3,
+        out_shape=[
+            jax.ShapeDtypeStruct((count, weights.shape[1]), F32),
+            jax.ShapeDtypeStruct((early, features), BF16),
+            jax.ShapeDtypeStruct((count - early, features), BF16),
+        ],
+        scratch_shapes=product_scratch(rows, weights, chunks),
+        compiler_params=FULL,
+        name="product_first",
+    )(rows, weights)
+
+
+def second_product(rows, weights, half, chunks):
+    return pl.pallas_call(
+        second_product_kernel,
+        in_specs=[IN_HBM] * 2 + [IN_VMEM],
+        out_specs=IN_HBM,
+        out_shape=jax.ShapeDtypeStruct((half.shape[0], 2 * half.shape[1]), F32),
+        scratch_shapes=product_scratch(rows, weights, chunks),
+        compiler_params=FULL,
+        name="product_second",
+    )(rows, weights, half)
+
+
 def self_product(value):
     return lax.dot_general(value, value, (((1,), (1,)), ((), ())), preferred_element_type=F32)
 
@@ -432,27 +517,26 @@
     for k in range(planes):
         lines.append(shifted(near[k], ZL, 1))
     by_pair = jnp.concatenate([jnp.concatenate(pair, axis=1) for pair in zip(near, lines)], axis=0)
-    by_all = jnp.concatenate([by_pair, shifted(by_pair, CORE, 1)], axis=1)
+    by_core_pair = shifted(by_pair, CORE, 1)
     middle = samples.shape[1] // 2
     gram_head = self_product(samples[:, :middle])
 
     flat = quarter.reshape(members * part, planes * depth)
     early = members * EARLY // 16 * part
-    beside_a = shifted(flat[:early], ZL, 1)
-    partial = jnp.dot(flat, by_all, preferred_element_type=F32)
-    partial, late = lax.optimization_barrier((partial, flat))
+    partial, early_rows, late_rows = first_product(flat, by_pair, planes, early)
+    beside_a = shifted(early_rows, ZL, 1)
+    partial = second_product(flat, by_core_pair, partial, planes)
     partial = lax.all_to_all(partial.reshape(members, part, quarters * width), PLANE, split_axis=0, concat_axis=0, tiled=True)
     across = shifted(flat, CORE, 1)
     diagonal_a = shifted(beside_a, CORE, 1)
     gram = gram_head + self_product(samples[:, middle:])
     ready = prepare(gram, inverse, width)
-    partial, late = lax.optimization_barrier((partial, late[early:]))
     own_piece, by_core, by_line, by_both = gathered(partial)
     by_line = shifted(by_line, ZL, 1)
     by_both = lax.ppermute(by_both, CLS, [(i, i ^ 3) for i in range(4)])
     by_core = shifted(by_core, CORE, 1)
     start = [own_piece, by_core, by_line, by_both]
-    beside_b = shifted(late, ZL, 1)
+    beside_b = shifted(late_rows, ZL, 1)
 
     alpha, steps, top = passes(where, start, labels[None, :], dual, ready, members)
     steps = lax.all_to_all(steps, PLANE, split_axis=0, concat_axis=0, tiled=True)

time: 166 us -> 159 us (0.958)
  waiting for transfers between devices: 62.6 us -> 52.7 us
  Pallas kernels: 24.6 us -> 32.9 us
  matrix products: 13.5 us -> 10.1 us
  starting transfers between devices: 59.1 us -> 57.4 us
    ppermute x21, waiting for transfers between devices: 41.1 us -> 27.2 us  [shifted(): lax.ppermute(value, axis, [(i, (i + by) % size) for i in range(size)])]
    pallas_call x0 -> x2, Pallas kernels: none -> 8.3 us  [the longest x1 4.79 us: second_product(): pl.pallas_call(second_product_kernel, in_specs=[IN_HBM] * 2 + [IN_VMEM],...]
    all_to_all x1, waiting for transfers between devices: 11.3 us -> 15.4 us  [round_of_ascent(): lax.all_to_all(partial.reshape(members, part, quarters * width), PLANE, s...]
    dot_general x1 -> x0, matrix products: 3.46 us -> none  [round_of_ascent(): partial = jnp.dot(flat, by_all, preferred_element_type=F32)]
    slice x2 -> x0, local copies, waits for them, and re-layouts: 2.15 us -> none  [the longest x1 1.2 us: round_of_ascent(): beside_a = shifted(flat[:early], ZL, 1)]
    ppermute x21, starting transfers between devices: 36.8 us -> 34.9 us  [shifted(): lax.ppermute(value, axis, [(i, (i + by) % size) for i in range(size)])]
  transfers between devices with their start and end apart: 25 -> 25, of which waited for: 10 -> 8; matrix products, arithmetic and copies ran while one was open for 8% -> 7% of each run, Pallas kernels for 13% -> 18%
where the time goes in v5:
time: 159 us; the launch traced here: 158 us
  starting transfers between devices  57.4 us (36%)
  waiting for transfers between devices  52.7 us (33%)
  Pallas kernels  32.9 us (21%)
  matrix products  10.1 us (6%)
  local copies, waits for them, and re-layouts  2.02 us (1%)
  other arithmetic  1.62 us (1%)
    ppermute x21, starting transfers between devices, shifted(): lax.ppermute(value, axis, [(i, (i + by) % size) for i in range(size)])  34.9 us
    ppermute x21, waiting for transfers between devices, shifted(): lax.ppermute(value, axis, [(i, (i + by) % size) for i in range(size)])  27.2 us
    all_to_all x1, waiting for transfers between devices, round_of_ascent(): lax.all_to_all(partial.reshape(members, part, quarters * width), PLANE, s...  15.4 us
    all_to_all x1, waiting for transfers between devices, round_of_ascent(): lax.all_to_all(steps, PLANE, split_axis=0, concat_axis=0, tiled=True)  10.1 us
    dot_general x2, matrix products, self_product(): lax.dot_general(value, value, (((1,), (1,)), ((), ())), preferred_element...  10.1 us
    all_to_all x1, starting transfers between devices, round_of_ascent(): lax.all_to_all(packed, PLANE, split_axis=0, concat_axis=0, tiled=True)  7.62 us
    all_to_all x1, starting transfers between devices, round_of_ascent(): lax.all_to_all(partial.reshape(members, part, quarters * width), PLANE, s...  7.37 us
    all_to_all x1, starting transfers between devices, round_of_ascent(): lax.all_to_all(steps, PLANE, split_axis=0, concat_axis=0, tiled=True)  7.24 us
  transfers between devices with their start and end apart: 25, of which 8 were waited for; matrix products, arithmetic and copies ran while one was open for 7% of the time, Pallas kernels for 18%

profile of v5, /device:TPU:2, one launch (start us, length us, event | category | flops | bytes accessed | tf_op | source)
XLA Modules:
  0.0 157.5 jit_solution(15470088238552919247)
XLA Ops:
  0.6 3.0 %pack.1 = bf16[16,32,2048]{2,1,0:T(8,128)(2,1)} custom-call(s32[1]{0:T(128)} %bitcast.where, s32[1]{0:T(128)} %bitcast.1.plane, bf16[128,32768]{1,0:T(8,128)(2,1)} %rows_hbm.1), custom_call_target="tpu_custom_call" | custom-call | tf_op jit(solution)/shard_map/pack/pallas_call | solution.py:67
  3.7 7.6 %all-to-all-start = ((bf16[16,32,2048]{2,1,0:T(8,128)(2,1)}), bf16[16,32,2048]{2,1,0:T(8,128)(2,1)S(1)}, u32[]{:S(2)}, u32[]{:S(2)}) async-start(bf16[16,32,2048]{2,1,0:T(8,128)(2,1)} %pack.1), calls=%async_computation | async-start | bytes 4194304 | tf_op jit(solution)/shard_map/all_to_all | solution.py:510
  11.3 3.3 %collective-permute-start.2 = (bf16[512,128]{1,0:T(8,128)(2,1)S(1)}, bf16[512,128]{1,0:T(8,128)(2,1)S(1)}, u32[]{:S(2)}, u32[]{:S(2)}) collective-permute-start(bf16[512,128]{1,0:T(8,128)(2,1)S(1)} %copy-done.2), channel_id=1, source_target_pairs={{0,64},{64,128},{128,192},{192,0},{1,65},{65,129},{129,193},{193,1... | collective-permute-start | bytes 393224 | tf_op jit(solution)/shard_map/ppermute | solution.py:34
  14.7 3.1 %collective-permute-start.5 = (bf16[512,128]{1,0:T(8,128)(2,1)S(1)}, bf16[512,128]{1,0:T(8,128)(2,1)S(1)}, u32[]{:S(2)}, u32[]{:S(2)}) collective-permute-start(bf16[512,128]{1,0:T(8,128)(2,1)S(1)} %copy-done.2), channel_id=1, source_target_pairs={{0,192},{64,0},{128,64},{192,128},{1,193},{65,1},{129,65},{193,129... | collective-permute-start | bytes 393224 | tf_op jit(solution)/shard_map/ppermute | solution.py:34
  17.8 3.4 %collective-permute-done.2 = bf16[512,128]{1,0:T(8,128)(2,1)S(1)} collective-permute-done((bf16[512,128]{1,0:T(8,128)(2,1)S(1)}, bf16[512,128]{1,0:T(8,128)(2,1)S(1)}, u32[]{:S(2)}, u32[]{:S(2)}) %collective-permute-start.2) | collective-permute-done | bytes 131104 | tf_op jit(solution)/shard_map/ppermute | solution.py:34
  21.2 2.6 %collective-permute-start.4 = (bf16[256,128]{1,0:T(8,128)(2,1)S(1)}, bf16[256,128]{1,0:T(8,128)(2,1)S(1)}, u32[]{:S(2)}, u32[]{:S(2)}) collective-permute-start(bf16[256,128]{1,0:T(8,128)(2,1)S(1)} %slice.16), channel_id=1, source_target_pairs={{0,64},{64,128},{128,192},{192,0},{1,65},{65,129},{129,193},{193,1... | collective-permute-start | bytes 196616 | tf_op jit(solution)/shard_map/ppermute | solution.py:34
  24.6 4.1 %collective-permute-start.6 = (bf16[256,128]{1,0:T(8,128)(2,1)S(1)}, bf16[256,128]{1,0:T(8,128)(2,1)S(1)}, u32[]{:S(2)}, u32[]{:S(2)}) collective-permute-start(bf16[256,128]{1,0:T(8,128)(2,1)S(1)} %slice.17), channel_id=1, source_target_pairs={{0,192},{64,0},{128,64},{192,128},{1,193},{65,1},{129,65},{193,129... | collective-permute-start | bytes 196616 | tf_op jit(solution)/shard_map/ppermute | solution.py:34
  31.6 6.1 %collective-permute-start.7 = (bf16[512,128]{1,0:T(8,128)(2,1)S(1)}, bf16[512,128]{1,0:T(8,128)(2,1)S(1)}, u32[]{:S(2)}, u32[]{:S(2)}) collective-permute-start(bf16[512,128]{1,0:T(8,128)(2,1)S(1)} %constant_dynamic-update-slice_fusion), channel_id=1, source_target_pairs={{0,2},{2,0},{1,3},{3,1},{4,6},{6,4},{5,7},{7,5},{8,10},{10,8},{9,1... | collective-permute-start | bytes 393224 | tf_op jit(solution)/shard_map/ppermute | solution.py:34
  37.9 2.8 %collective-permute-done.7 = bf16[512,128]{1,0:T(8,128)(2,1)S(1)} collective-permute-done((bf16[512,128]{1,0:T(8,128)(2,1)S(1)}, bf16[512,128]{1,0:T(8,128)(2,1)S(1)}, u32[]{:S(2)}, u32[]{:S(2)}) %collective-permute-start.7) | collective-permute-done | bytes 131104 | tf_op jit(solution)/shard_map/ppermute | solution.py:34
  43.2 3.5 %product_first.1 = (f32[512,256]{1,0:T(8,128)}, bf16[320,2048]{1,0:T(8,128)(2,1)}, bf16[192,2048]{1,0:T(8,128)(2,1)}) custom-call(bf16[512,2048]{1,0:T(8,128)(2,1)} %bitcast.8, bf16[2048,256]{1,0:T(8,128)(2,1)} %maximum_maximum_fusion.weights_hbm), custom_call_target="tpu_custom_call" | custom-call | tf_op jit(solution)/shard_map/product_first/pallas_call | solution.py:467
  48.8 4.8 %product_second.1 = f32[512,512]{1,0:T(8,128)} custom-call(bf16[512,2048]{1,0:T(8,128)(2,1)} %bitcast.9, bf16[2048,256]{1,0:T(8,128)(2,1)} %collective-permute-done.13.weights_hbm, f32[512,256]{1,0:T(8,128)} %get-tuple-element.23.half_ref), custom_call_target="tpu_custom_call" | custom-call | tf_op jit(solution)/shard_map/product_second/pallas_call | solution.py:483
  53.6 7.4 %all-to-all-start.1 = ((f32[16,32,512]{2,1,0:T(8,128)}), f32[16,32,512]{2,1,0:T(8,128)}, u32[]{:S(2)}, u32[]{:S(2)}) async-start(f32[16,32,512]{2,1,0:T(8,128)} %bitcast.15), calls=%async_computation.1 | async-start | bytes 2097152 | tf_op jit(solution)/shard_map/all_to_all | solution.py:529
  61.2 15.4 %all-to-all-done.1.parts_hbm = f32[16,32,512]{2,1,0:T(8,128)} async-done(((f32[16,32,512]{2,1,0:T(8,128)}), f32[16,32,512]{2,1,0:T(8,128)}, u32[]{:S(2)}, u32[]{:S(2)}) %all-to-all-start.1) | async-done | bytes 1048608 | tf_op jit(solution)/shard_map/all_to_all | solution.py:529
  79.2 4.7 %fusion = f32[128,128]{1,0:T(8,128)S(1)} fusion(bf16[128,32768]{1,0:T(8,128)(2,1)} %rows_hbm.1), kind=kOutput, calls=%fused_computation | convolution fusion | flops 536870912 | bytes 4259840 | tf_op jit(solution)/shard_map/dot_general | solution.py:495
  83.9 11.5 %collective-permute-done.10.refs_3_ = bf16[192,2048]{1,0:T(8,128)(2,1)} collective-permute-done((bf16[192,2048]{1,0:T(8,128)(2,1)}, bf16[192,2048]{1,0:T(8,128)(2,1)}, u32[]{:S(2)}, u32[]{:S(2)}) %collective-permute-start.10) | collective-permute-done | bytes 786464 | tf_op jit(solution)/shard_map/ppermute | solution.py:34
  97.4 5.4 %fusion.4.gram_ref = f32[128,128]{1,0:T(8,128)} fusion(f32[128,128]{1,0:T(8,128)S(1)} %fusion, bf16[128,32768]{1,0:T(8,128)(2,1)} %rows_hbm.1), kind=kOutput, calls=%fused_computation.4 | convolution fusion | flops 536887296 | bytes 4325376 | tf_op jit(solution)/shard_map/dot_general | solution.py:495
  102.7 5.9 %prepare.1 = (f32[8,32,16,128]{3,2,1,0:T(8,128)}, bf16[8,128,96]{2,1,0:T(8,128)(2,1)}) custom-call(f32[128,128]{1,0:T(8,128)} %fusion.4.gram_ref, f32[8,16,16]{2,1,0:T(8,128)} %inverse_ref.1), custom_call_target="tpu_custom_call" | custom-call | tf_op jit(solution)/shard_map/prepare/pallas_call | solution.py:110
  109.2 4.1 %passes.1 = (f32[128,128]{1,0:T(8,128)}, bf16[16,136,128]{2,1,0:T(8,128)(2,1)}, f32[1,128]{1,0:T(1,128)}) custom-call(s32[1]{0:T(128)} %bitcast.where, f32[32,128]{1,0:T(8,128)} %get-tuple-element.24.start0, f32[32,128]{1,0:T(8,128)} %copy-done.3, f32[32,128]{1,0:T(8,128)} %copy-done.4, f32[32,128]{1,0:T(8,128)} %copy-done.5, s32[1,128]{1,0:T(1,128)} %bitcast.16, ...), custom_call_target="tpu_custom_call" | custom-call | tf_op jit(solution)/shard_map/passes/pallas_call | solution.py:204
  113.3 7.2 %all-to-all-start.2 = ((bf16[16,136,128]{2,1,0:T(8,128)(2,1)}), bf16[16,136,128]{2,1,0:T(8,128)(2,1)}, u32[]{:S(2)}, u32[]{:S(2)}) async-start(bf16[16,136,128]{2,1,0:T(8,128)(2,1)} %get-tuple-element.30), calls=%async_computation.2 | async-start | bytes 1114112 | tf_op jit(solution)/shard_map/all_to_all | solution.py:542
  120.6 10.1 %all-to-all-done.2.refs_6_ = bf16[16,136,128]{2,1,0:T(8,128)(2,1)} async-done(((bf16[16,136,128]{2,1,0:T(8,128)(2,1)}), bf16[16,136,128]{2,1,0:T(8,128)(2,1)}, u32[]{:S(2)}, u32[]{:S(2)}) %all-to-all-start.2) | async-done | bytes 557088 | tf_op jit(solution)/shard_map/all_to_all | solution.py:542
  130.7 3.0 %delta_first.1 = (bf16[520,128]{1,0:T(8,128)(2,1)S(1)}, bf16[128,2304]{1,0:T(8,128)(2,1)S(1)}, f32[1,128]{1,0:T(1,128)S(1)}) custom-call(s32[1]{0:T(128)} %bitcast.where, bf16[512,2048]{1,0:T(8,128)(2,1)S(1)} %bitcast.11, bf16[512,2048]{1,0:T(8,128)(2,1)} %collective-permute-done.refs_1_, bf16[320,2048]{1,0:T(8,128)(2,1)S(1)} %collective-permute-done.9.refs_2_, ...), custom_call_target="tpu_custom_call" | custom-call | tf_op jit(solution)/shard_map/delta_first/pallas_call | solution.py:342
  135.6 3.0 %collective-permute-start.19 = (bf16[520,128]{1,0:T(8,128)(2,1)S(1)}, bf16[520,128]{1,0:T(8,128)(2,1)S(1)}, u32[]{:S(2)}, u32[]{:S(2)}) collective-permute-start(bf16[520,128]{1,0:T(8,128)(2,1)S(1)} %delta_next.3), channel_id=1, source_target_pairs={{0,64},{64,128},{128,192},{192,0},{1,65},{65,129},{129,193},{193,1... | collective-permute-start | bytes 399368 | tf_op jit(solution)/shard_map/ppermute | solution.py:34
  141.9 3.6 %collective-permute-start.17 = (bf16[520,128]{1,0:T(8,128)(2,1)S(1)}, bf16[520,128]{1,0:T(8,128)(2,1)S(1)}, u32[]{:S(2)}, u32[]{:S(2)}) collective-permute-start(bf16[520,128]{1,0:T(8,128)(2,1)S(1)} %get-tuple-element.33), channel_id=1, source_target_pairs={{0,128},{64,192},{128,0},{192,64},{1,129},{65,193},{129,1},{193,65... | collective-permute-start | bytes 399368 | tf_op jit(solution)/shard_map/ppermute | solution.py:34
  145.8 8.4 %collective-permute-done.21 = f32[128]{0:T(128)S(1)} collective-permute-done((f32[128]{0:T(128)S(1)}, f32[128]{0:T(128)S(1)}, u32[]{:S(2)}, u32[]{:S(2)}) %collective-permute-start.21) | collective-permute-done | bytes 544 | tf_op jit(solution)/shard_map/ppermute | solution.py:34
  (64 shorter events, 22.6 us)
Async XLA Ops:
  3.7 38.1 %all-to-all-start = ((bf16[16,32,2048]{2,1,0:T(8,128)(2,1)}), bf16[16,32,2048]{2,1,0:T(8,128)(2,1)S(1)}, u32[]{:S(2)}, u32[]{:S(2)}) async-start(bf16[16,32,2048]{2,1,0:T(8,128)(2,1)} %pack.1), calls=%async_computation | async-start | bytes 4194304 | tf_op jit(solution)/shard_map/all_to_all | solution.py:510
  11.3 9.9 %collective-permute-start.2 = (bf16[512,128]{1,0:T(8,128)(2,1)S(1)}, bf16[512,128]{1,0:T(8,128)(2,1)S(1)}, u32[]{:S(2)}, u32[]{:S(2)}) collective-permute-start(bf16[512,128]{1,0:T(8,128)(2,1)S(1)} %copy-done.2), channel_id=1, source_target_pairs={{0,64},{64,128},{128,192},{192,0},{1,65},{65,129},{129,193},{193,1... | collective-permute-start | bytes 393224 | tf_op jit(solution)/shard_map/ppermute | solution.py:34
  14.7 10.0 %collective-permute-start.5 = (bf16[512,128]{1,0:T(8,128)(2,1)S(1)}, bf16[512,128]{1,0:T(8,128)(2,1)S(1)}, u32[]{:S(2)}, u32[]{:S(2)}) collective-permute-start(bf16[512,128]{1,0:T(8,128)(2,1)S(1)} %copy-done.2), channel_id=1, source_target_pairs={{0,192},{64,0},{128,64},{192,128},{1,193},{65,1},{129,65},{193,129... | collective-permute-start | bytes 393224 | tf_op jit(solution)/shard_map/ppermute | solution.py:34
  21.2 9.5 %collective-permute-start.4 = (bf16[256,128]{1,0:T(8,128)(2,1)S(1)}, bf16[256,128]{1,0:T(8,128)(2,1)S(1)}, u32[]{:S(2)}, u32[]{:S(2)}) collective-permute-start(bf16[256,128]{1,0:T(8,128)(2,1)S(1)} %slice.16), channel_id=1, source_target_pairs={{0,64},{64,128},{128,192},{192,0},{1,65},{65,129},{129,193},{193,1... | collective-permute-start | bytes 196616 | tf_op jit(solution)/shard_map/ppermute | solution.py:34
  23.9 13.9 %collective-permute-start.1 = (bf16[512,128]{1,0:T(8,128)(2,1)S(1)}, bf16[512,128]{1,0:T(8,128)(2,1)S(1)}, u32[]{:S(2)}, u32[]{:S(2)}) collective-permute-start(bf16[512,128]{1,0:T(8,128)(2,1)S(1)} %copy-done.2), channel_id=1, source_target_pairs={{0,2},{2,0},{1,3},{3,1},{4,6},{6,4},{5,7},{7,5},{8,10},{10,8},{9,1... | collective-permute-start | bytes 393224 | tf_op jit(solution)/shard_map/ppermute | solution.py:34
  28.7 9.0 %collective-permute-start.3 = (bf16[512,128]{1,0:T(8,128)(2,1)S(1)}, bf16[512,128]{1,0:T(8,128)(2,1)S(1)}, u32[]{:S(2)}, u32[]{:S(2)}) collective-permute-start(bf16[512,128]{1,0:T(8,128)(2,1)S(1)} %collective-permute-done.2), channel_id=1, source_target_pairs={{0,2},{2,0},{1,3},{3,1},{4,6},{6,4},{5,7},{7,5},{8,10},{10,8},{9,1... | collective-permute-start | bytes 393224 | tf_op jit(solution)/shard_map/ppermute | solution.py:34
  28.7 9.2 %collective-permute-start.8 = (bf16[512,128]{1,0:T(8,128)(2,1)S(1)}, bf16[512,128]{1,0:T(8,128)(2,1)S(1)}, u32[]{:S(2)}, u32[]{:S(2)}) collective-permute-start(bf16[512,128]{1,0:T(8,128)(2,1)S(1)} %collective-permute-done.5), channel_id=1, source_target_pairs={{0,2},{2,0},{1,3},{3,1},{4,6},{6,4},{5,7},{7,5},{8,10},{10,8},{9,1... | collective-permute-start | bytes 393224 | tf_op jit(solution)/shard_map/ppermute | solution.py:34
  31.6 9.1 %collective-permute-start.7 = (bf16[512,128]{1,0:T(8,128)(2,1)S(1)}, bf16[512,128]{1,0:T(8,128)(2,1)S(1)}, u32[]{:S(2)}, u32[]{:S(2)}) collective-permute-start(bf16[512,128]{1,0:T(8,128)(2,1)S(1)} %constant_dynamic-update-slice_fusion), channel_id=1, source_target_pairs={{0,2},{2,0},{1,3},{3,1},{4,6},{6,4},{5,7},{7,5},{8,10},{10,8},{9,1... | collective-permute-start | bytes 393224 | tf_op jit(solution)/shard_map/ppermute | solution.py:34
  41.8 7.0 %collective-permute-start.13 = (bf16[2048,256]{1,0:T(8,128)(2,1)}, bf16[2048,256]{1,0:T(8,128)(2,1)}, u32[]{:S(2)}, u32[]{:S(2)}) collective-permute-start(bf16[2048,256]{1,0:T(8,128)(2,1)} %maximum_maximum_fusion.weights_hbm), channel_id=1, source_target_pairs={{0,1},{1,0},{2,3},{3,2},{4,5},{5,4},{6,7},{7,6},{8,9},{9,8},{10,11... | collective-permute-start | bytes 3145736 | tf_op jit(solution)/shard_map/ppermute | solution.py:34
  46.7 32.0 %collective-permute-start.9 = (bf16[320,2048]{1,0:T(8,128)(2,1)}, bf16[320,2048]{1,0:T(8,128)(2,1)S(1)}, u32[]{:S(2)}, u32[]{:S(2)}) collective-permute-start(bf16[320,2048]{1,0:T(8,128)(2,1)} %get-tuple-element.21), channel_id=1, source_target_pairs={{0,2},{2,0},{1,3},{3,1},{4,6},{6,4},{5,7},{7,5},{8,10},{10,8},{9,1... | collective-permute-start | bytes 3932168 | tf_op jit(solution)/shard_map/ppermute | solution.py:34
  53.6 22.9 %all-to-all-start.1 = ((f32[16,32,512]{2,1,0:T(8,128)}), f32[16,32,512]{2,1,0:T(8,128)}, u32[]{:S(2)}, u32[]{:S(2)}) async-start(f32[16,32,512]{2,1,0:T(8,128)} %bitcast.15), calls=%async_computation.1 | async-start | bytes 2097152 | tf_op jit(solution)/shard_map/all_to_all | solution.py:529
  61.0 69.7 %collective-permute-start = (bf16[512,2048]{1,0:T(8,128)(2,1)S(1)}, bf16[512,2048]{1,0:T(8,128)(2,1)}, u32[]{:S(2)}, u32[]{:S(2)}) collective-permute-start(bf16[512,2048]{1,0:T(8,128)(2,1)S(1)} %bitcast.10), channel_id=1, source_target_pairs={{0,1},{1,0},{2,3},{3,2},{4,5},{5,4},{6,7},{7,6},{8,9},{9,8},{10,11... | collective-permute-start | bytes 6291464 | tf_op jit(solution)/shard_map/ppermute | solution.py:34
  61.1 34.3 %collective-permute-start.10 = (bf16[192,2048]{1,0:T(8,128)(2,1)}, bf16[192,2048]{1,0:T(8,128)(2,1)}, u32[]{:S(2)}, u32[]{:S(2)}) collective-permute-start(bf16[192,2048]{1,0:T(8,128)(2,1)} %get-tuple-element.22), channel_id=1, source_target_pairs={{0,2},{2,0},{1,3},{3,1},{4,6},{6,4},{5,7},{7,5},{8,10},{10,8},{9,1... | collective-permute-start | bytes 2359304 | tf_op jit(solution)/shard_map/ppermute | solution.py:34
  78.6 18.6 %collective-permute-start.14 = (f32[32,128]{1,0:T(8,128)}, f32[32,128]{1,0:T(8,128)S(1)}, u32[]{:S(2)}, u32[]{:S(2)}) collective-permute-start(f32[32,128]{1,0:T(8,128)} %get-tuple-element.25), channel_id=1, source_target_pairs={{0,1},{1,0},{2,3},{3,2},{4,5},{5,4},{6,7},{7,6},{8,9},{9,8},{10,11... | collective-permute-start | bytes 49160 | tf_op jit(solution)/shard_map/ppermute | solution.py:34
  78.7 52.1 %collective-permute-start.11 = (bf16[320,2048]{1,0:T(8,128)(2,1)S(1)}, bf16[320,2048]{1,0:T(8,128)(2,1)}, u32[]{:S(2)}, u32[]{:S(2)}) collective-permute-start(bf16[320,2048]{1,0:T(8,128)(2,1)S(1)} %collective-permute-done.9.refs_2_), channel_id=1, source_target_pairs={{0,1},{1,0},{2,3},{3,2},{4,5},{5,4},{6,7},{7,6},{8,9},{9,8},{10,11... | collective-permute-start | bytes 3932168 | tf_op jit(solution)/shard_map/ppermute | solution.py:34
  95.4 35.3 %collective-permute-start.12 = (bf16[192,2048]{1,0:T(8,128)(2,1)}, bf16[192,2048]{1,0:T(8,128)(2,1)}, u32[]{:S(2)}, u32[]{:S(2)}) collective-permute-start(bf16[192,2048]{1,0:T(8,128)(2,1)} %collective-permute-done.10.refs_3_), channel_id=1, source_target_pairs={{0,1},{1,0},{2,3},{3,2},{4,5},{5,4},{6,7},{7,6},{8,9},{9,8},{10,11... | collective-permute-start | bytes 2359304 | tf_op jit(solution)/shard_map/ppermute | solution.py:34
  95.4 13.2 %collective-permute-start.15 = (f32[32,128]{1,0:T(8,128)S(1)}, f32[32,128]{1,0:T(8,128)S(1)}, u32[]{:S(2)}, u32[]{:S(2)}) collective-permute-start(f32[32,128]{1,0:T(8,128)S(1)} %copy-done.7), channel_id=1, source_target_pairs={{0,2},{2,0},{1,3},{3,1},{4,6},{6,4},{5,7},{7,5},{8,10},{10,8},{9,1... | collective-permute-start | bytes 49160 | tf_op jit(solution)/shard_map/ppermute | solution.py:34
  97.2 11.4 %collective-permute-start.16 = (f32[32,128]{1,0:T(8,128)S(1)}, f32[32,128]{1,0:T(8,128)S(1)}, u32[]{:S(2)}, u32[]{:S(2)}) collective-permute-start(f32[32,128]{1,0:T(8,128)S(1)} %copy-done.6), channel_id=1, source_target_pairs={{0,3},{1,2},{2,1},{3,0},{4,7},{5,6},{6,5},{7,4},{8,11},{9,10},{10,... | collective-permute-start | bytes 49160 | tf_op jit(solution)/shard_map/ppermute | solution.py:536
  113.3 17.4 %all-to-all-start.2 = ((bf16[16,136,128]{2,1,0:T(8,128)(2,1)}), bf16[16,136,128]{2,1,0:T(8,128)(2,1)}, u32[]{:S(2)}, u32[]{:S(2)}) async-start(bf16[16,136,128]{2,1,0:T(8,128)(2,1)} %get-tuple-element.30), calls=%async_computation.2 | async-start | bytes 1114112 | tf_op jit(solution)/shard_map/all_to_all | solution.py:542
  120.6 24.9 %collective-permute-start.20 = (f32[128]{0:T(128)}, f32[128]{0:T(128)S(1)}, u32[]{:S(2)}, u32[]{:S(2)}) collective-permute-start(f32[128]{0:T(128)} %bitcast.17), channel_id=1, source_target_pairs={{0,1},{1,0},{2,3},{3,2},{4,5},{5,4},{6,7},{7,6},{8,9},{9,8},{10,11... | collective-permute-start | bytes 1544 | tf_op jit(solution)/shard_map/ppermute | solution.py:34
  135.6 21.0 %collective-permute-start.19 = (bf16[520,128]{1,0:T(8,128)(2,1)S(1)}, bf16[520,128]{1,0:T(8,128)(2,1)S(1)}, u32[]{:S(2)}, u32[]{:S(2)}) collective-permute-start(bf16[520,128]{1,0:T(8,128)(2,1)S(1)} %delta_next.3), channel_id=1, source_target_pairs={{0,64},{64,128},{128,192},{192,0},{1,65},{65,129},{129,193},{193,1... | collective-permute-start | bytes 399368 | tf_op jit(solution)/shard_map/ppermute | solution.py:34
  140.6 16.1 %collective-permute-start.18 = (bf16[520,128]{1,0:T(8,128)(2,1)S(1)}, bf16[520,128]{1,0:T(8,128)(2,1)S(1)}, u32[]{:S(2)}, u32[]{:S(2)}) collective-permute-start(bf16[520,128]{1,0:T(8,128)(2,1)S(1)} %delta_next.2), channel_id=1, source_target_pairs={{0,192},{64,0},{128,64},{192,128},{1,193},{65,1},{129,65},{193,129... | collective-permute-start | bytes 399368 | tf_op jit(solution)/shard_map/ppermute | solution.py:34
  141.9 14.8 %collective-permute-start.17 = (bf16[520,128]{1,0:T(8,128)(2,1)S(1)}, bf16[520,128]{1,0:T(8,128)(2,1)S(1)}, u32[]{:S(2)}, u32[]{:S(2)}) collective-permute-start(bf16[520,128]{1,0:T(8,128)(2,1)S(1)} %get-tuple-element.33), channel_id=1, source_target_pairs={{0,128},{64,192},{128,0},{192,64},{1,129},{65,193},{129,1},{193,65... | collective-permute-start | bytes 399368 | tf_op jit(solution)/shard_map/ppermute | solution.py:34
  145.5 8.7 %collective-permute-start.21 = (f32[128]{0:T(128)S(1)}, f32[128]{0:T(128)S(1)}, u32[]{:S(2)}, u32[]{:S(2)}) collective-permute-start(f32[128]{0:T(128)S(1)} %bitcast_maximum_fusion), channel_id=1, source_target_pairs={{0,2},{2,0},{1,3},{3,1},{4,6},{6,4},{5,7},{7,5},{8,10},{10,8},{9,1... | collective-permute-start | bytes 1544 | tf_op jit(solution)/shard_map/ppermute | solution.py:34
  (10 other events, 75.5 us)

commit v6 on v4

--- a/solution.py
+++ b/solution.py
@@ -17,6 +17,7 @@
 SAMP = (ZH, X, Y)
 CLS = (ZL, CORE)
 GAP_ROWS = 8
+PACK_PIECES = 4
 EARLY = 10
 ORDER = (0, 2, 1, 3)
 F32, BF16 = jnp.float32, jnp.bfloat16
@@ -36,24 +37,28 @@
 
 def pack_kernel(where, plane, rows_hbm, out_hbm, held_ref, in_sems, out_sems):
     members, part, total = out_hbm.shape
-    planes = in_sems.shape[0]
+    planes, pieces = in_sems.shape
     width = total // planes
     span = members * width
+    some = members // pieces
     row = pl.multiple_of(where[0] * part, part)
-    loads = []
+    loads = {}
     for k in range(planes):
         low = pl.multiple_of(lax.rem(plane[0] + (planes - k), planes) * span, span)
-        loads.append(pltpu.make_async_copy(rows_hbm.at[pl.ds(row, part), pl.ds(low, span)], held_ref.at[k], in_sems.at[k]))
-    for load in loads:
+        for i in range(pieces):
+            loads[k, i] = pltpu.make_async_copy(
+                rows_hbm.at[pl.ds(row, part), pl.ds(low + i * some * width, some * width)], held_ref.at[k, i], in_sems.at[k, i]
+            )
+    for load in loads.values():
         load.start()
     stores = []
-    for k in range(planes):
-        loads[k].wait()
-        for place in range(members):
+    for (k, i), load in loads.items():
+        load.wait()
+        for place in range(some):
             store = pltpu.make_async_copy(
-                held_ref.at[k, :, pl.ds(place * width, width)],
-                out_hbm.at[place, :, pl.ds(k * width, width)],
-                out_sems.at[k * members + place],
+                held_ref.at[k, i, :, pl.ds(place * width, width)],
+                out_hbm.at[i * some + place, :, pl.ds(k * width, width)],
+                out_sems.at[k, i * some + place],
             )
             store.start()
             stores.append(store)
@@ -70,9 +75,9 @@
         out_specs=IN_HBM,
         out_shape=jax.ShapeDtypeStruct((members, part, features // members), samples.dtype),
         scratch_shapes=[
-            pltpu.VMEM((planes, part, features // planes), samples.dtype),
-            pltpu.SemaphoreType.DMA((planes,)),
-            pltpu.SemaphoreType.DMA((planes * members,)),
+            pltpu.VMEM((planes, PACK_PIECES, part, features // (planes * PACK_PIECES)), samples.dtype),
+            pltpu.SemaphoreType.DMA((planes, PACK_PIECES)),
+            pltpu.SemaphoreType.DMA((planes, members)),
         ],
         compiler_params=FULL,
         name="pack",
@@ -427,11 +432,12 @@
     from_above = shifted(weight, ZH, -1)
     far_head = shifted(from_below[:depth // 2], ZH, 1)
     far_rest = shifted(from_above[depth // 2:], ZH, -1)
-    near = [weight, from_below, jnp.concatenate([far_head, far_rest], axis=0), from_above]
-    lines = []
-    for k in range(planes):
-        lines.append(shifted(near[k], ZL, 1))
-    by_pair = jnp.concatenate([jnp.concatenate(pair, axis=1) for pair in zip(near, lines)], axis=0)
+    near = {"0": weight, "1": from_below, "2_head": far_head, "2_rest": far_rest, "3": from_above}
+    pairs = []
+    for piece in near.values():
+        other = shifted(piece, ZL, 1)
+        pairs.append(jnp.concatenate([piece, other], axis=1))
+    by_pair = jnp.concatenate(pairs, axis=0)
     by_all = jnp.concatenate([by_pair, shifted(by_pair, CORE, 1)], axis=1)
     middle = samples.shape[1] // 2
     gram_head = self_product(samples[:, :middle])

time: 166 us -> 163 us (0.982)
  starting transfers between devices: 59.1 us -> 53 us
  waiting for transfers between devices: 62.6 us -> 66 us
    ppermute x21 -> x22, starting transfers between devices: 36.8 us -> 30.3 us  [shifted(): lax.ppermute(value, axis, [(i, (i + by) % size) for i in range(size)])]
    ppermute x21 -> x22, waiting for transfers between devices: 41.1 us -> 43.7 us  [shifted(): lax.ppermute(value, axis, [(i, (i + by) % size) for i in range(size)])]
  transfers between devices with their start and end apart: 25 -> 26, of which waited for: 10 -> 10; matrix products, arithmetic and copies ran while one was open for 8% -> 8% of each run, Pallas kernels for 13% -> 13%
where the time goes in v6:
time: 163 us; the launch traced here: 161 us
  waiting for transfers between devices  66 us (40%)
  starting transfers between devices  53 us (33%)
  Pallas kernels  24.6 us (15%)
  matrix products  13.5 us (8%)
  local copies, waits for them, and re-layouts  2.8 us (2%)
    ppermute x22, waiting for transfers between devices, shifted(): lax.ppermute(value, axis, [(i, (i + by) % size) for i in range(size)])  43.7 us
    ppermute x22, starting transfers between devices, shifted(): lax.ppermute(value, axis, [(i, (i + by) % size) for i in range(size)])  30.3 us
    all_to_all x1, waiting for transfers between devices, round_of_ascent(): lax.all_to_all(partial.reshape(members, part, quarters * width), PLANE, s...  11.9 us
    all_to_all x1, waiting for transfers between devices, round_of_ascent(): lax.all_to_all(steps, PLANE, split_axis=0, concat_axis=0, tiled=True)  10.3 us
    dot_general x2, matrix products, self_product(): lax.dot_general(value, value, (((1,), (1,)), ((), ())), preferred_element...  10.1 us
    all_to_all x1, starting transfers between devices, round_of_ascent(): lax.all_to_all(packed, PLANE, split_axis=0, concat_axis=0, tiled=True)  7.62 us
    all_to_all x1, starting transfers between devices, round_of_ascent(): lax.all_to_all(steps, PLANE, split_axis=0, concat_axis=0, tiled=True)  7.24 us
    all_to_all x1, starting transfers between devices, round_of_ascent(): lax.all_to_all(partial.reshape(members, part, quarters * width), PLANE, s...  7.23 us
  transfers between devices with their start and end apart: 26, of which 10 were waited for; matrix products, arithmetic and copies ran while one was open for 8% of the time, Pallas kernels for 13%

profile of v6, /device:TPU:2, one launch (start us, length us, event | category | flops | bytes accessed | tf_op | source)
XLA Modules:
  0.0 161.4 jit_solution(3667787459548706123)
XLA Ops:
  0.6 3.1 %pack.1 = bf16[16,32,2048]{2,1,0:T(8,128)(2,1)} custom-call(s32[1]{0:T(128)} %bitcast.where, s32[1]{0:T(128)} %bitcast.1.plane, bf16[128,32768]{1,0:T(8,128)(2,1)} %rows_hbm.1), custom_call_target="tpu_custom_call" | custom-call | tf_op jit(solution)/shard_map/pack/pallas_call | solution.py:72
  3.7 7.6 %all-to-all-start = ((bf16[16,32,2048]{2,1,0:T(8,128)(2,1)}), bf16[16,32,2048]{2,1,0:T(8,128)(2,1)S(1)}, u32[]{:S(2)}, u32[]{:S(2)}) async-start(bf16[16,32,2048]{2,1,0:T(8,128)(2,1)} %pack.1), calls=%async_computation | async-start | bytes 4194304 | tf_op jit(solution)/shard_map/all_to_all | solution.py:430
  11.4 3.3 %collective-permute-start.3 = (bf16[512,128]{1,0:T(8,128)(2,1)S(1)}, bf16[512,128]{1,0:T(8,128)(2,1)S(1)}, u32[]{:S(2)}, u32[]{:S(2)}) collective-permute-start(bf16[512,128]{1,0:T(8,128)(2,1)S(1)} %copy-done), channel_id=1, source_target_pairs={{0,64},{64,128},{128,192},{192,0},{1,65},{65,129},{129,193},{193,1... | collective-permute-start | bytes 393224 | tf_op jit(solution)/shard_map/ppermute | solution.py:35
  14.7 3.1 %collective-permute-start.7 = (bf16[512,128]{1,0:T(8,128)(2,1)S(1)}, bf16[512,128]{1,0:T(8,128)(2,1)S(1)}, u32[]{:S(2)}, u32[]{:S(2)}) collective-permute-start(bf16[512,128]{1,0:T(8,128)(2,1)S(1)} %copy-done), channel_id=1, source_target_pairs={{0,192},{64,0},{128,64},{192,128},{1,193},{65,1},{129,65},{193,129... | collective-permute-start | bytes 393224 | tf_op jit(solution)/shard_map/ppermute | solution.py:35
  18.9 3.4 %collective-permute-done.3 = bf16[512,128]{1,0:T(8,128)(2,1)S(1)} collective-permute-done((bf16[512,128]{1,0:T(8,128)(2,1)S(1)}, bf16[512,128]{1,0:T(8,128)(2,1)S(1)}, u32[]{:S(2)}, u32[]{:S(2)}) %collective-permute-start.3) | collective-permute-done | bytes 131104 | tf_op jit(solution)/shard_map/ppermute | solution.py:35
  22.3 2.3 %collective-permute-start.4 = (bf16[512,128]{1,0:T(8,128)(2,1)S(1)}, bf16[512,128]{1,0:T(8,128)(2,1)S(1)}, u32[]{:S(2)}, u32[]{:S(2)}) collective-permute-start(bf16[512,128]{1,0:T(8,128)(2,1)S(1)} %collective-permute-done.3), channel_id=1, source_target_pairs={{0,2},{2,0},{1,3},{3,1},{4,6},{6,4},{5,7},{7,5},{8,10},{10,8},{9,1... | collective-permute-start | bytes 393224 | tf_op jit(solution)/shard_map/ppermute | solution.py:35
  25.1 3.7 %collective-permute-start.8 = (bf16[256,128]{1,0:T(8,128)(2,1)S(1)}, bf16[256,128]{1,0:T(8,128)(2,1)S(1)}, u32[]{:S(2)}, u32[]{:S(2)}) collective-permute-start(bf16[256,128]{1,0:T(8,128)(2,1)S(1)} %slice.30), channel_id=1, source_target_pairs={{0,192},{64,0},{128,64},{192,128},{1,193},{65,1},{129,65},{193,129... | collective-permute-start | bytes 196616 | tf_op jit(solution)/shard_map/ppermute | solution.py:35
  29.6 4.2 %collective-permute-done.5 = bf16[256,128]{1,0:T(8,128)(2,1)S(1)} collective-permute-done((bf16[256,128]{1,0:T(8,128)(2,1)S(1)}, bf16[256,128]{1,0:T(8,128)(2,1)S(1)}, u32[]{:S(2)}, u32[]{:S(2)}) %collective-permute-start.5) | collective-permute-done | bytes 65568 | tf_op jit(solution)/shard_map/ppermute | solution.py:35
  39.0 2.8 %collective-permute-done.11 = bf16[2048,256]{1,0:T(8,128)(2,1)} collective-permute-done((bf16[2048,256]{1,0:T(8,128)(2,1)S(1)}, bf16[2048,256]{1,0:T(8,128)(2,1)}, u32[]{:S(2)}, u32[]{:S(2)}) %collective-permute-start.11) | collective-permute-done | bytes 1048608 | tf_op jit(solution)/shard_map/ppermute | solution.py:35
  41.8 3.5 %fusion.4 = f32[512,512]{1,0:T(8,128)} fusion(bf16[512,2048]{1,0:T(8,128)(2,1)S(1)} %bitcast.10, bf16[2048,256]{1,0:T(8,128)(2,1)} %collective-permute-done.11, bf16[2048,256]{1,0:T(8,128)(2,1)S(1)} %maximum_dynamic-update-slice_fusion), kind=kOutput, calls=%fused_computation.4 | convolution fusion | flops 1077936128 | bytes 5242880 | tf_op jit(solution)/shard_map/dot_general | solution.py:448
  45.3 7.2 %all-to-all-start.1 = ((f32[16,32,512]{2,1,0:T(8,128)}), f32[16,32,512]{2,1,0:T(8,128)}, u32[]{:S(2)}, u32[]{:S(2)}) async-start(f32[16,32,512]{2,1,0:T(8,128)} %bitcast.4), calls=%async_computation.1 | async-start | bytes 2097152 | tf_op jit(solution)/shard_map/all_to_all | solution.py:450
  56.0 11.9 %all-to-all-done.1.parts_hbm = f32[16,32,512]{2,1,0:T(8,128)} async-done(((f32[16,32,512]{2,1,0:T(8,128)}), f32[16,32,512]{2,1,0:T(8,128)}, u32[]{:S(2)}, u32[]{:S(2)}) %all-to-all-start.1) | async-done | bytes 1048608 | tf_op jit(solution)/shard_map/all_to_all | solution.py:450
  71.4 14.2 %collective-permute-done.1.refs_2_ = bf16[320,2048]{1,0:T(8,128)(2,1)S(1)} collective-permute-done((bf16[320,2048]{1,0:T(8,128)(2,1)}, bf16[320,2048]{1,0:T(8,128)(2,1)S(1)}, u32[]{:S(2)}, u32[]{:S(2)}) %collective-permute-start.1) | collective-permute-done | bytes 1310752 | tf_op jit(solution)/shard_map/ppermute | solution.py:35
  85.6 4.7 %fusion = f32[128,128]{1,0:T(8,128)S(1)} fusion(bf16[128,32768]{1,0:T(8,128)(2,1)} %rows_hbm.1), kind=kOutput, calls=%fused_computation | convolution fusion | flops 536870912 | bytes 4259840 | tf_op jit(solution)/shard_map/dot_general | solution.py:415
  92.3 9.2 %collective-permute-done.12.refs_3_ = bf16[192,2048]{1,0:T(8,128)(2,1)} collective-permute-done((bf16[192,2048]{1,0:T(8,128)(2,1)}, bf16[192,2048]{1,0:T(8,128)(2,1)}, u32[]{:S(2)}, u32[]{:S(2)}) %collective-permute-start.12) | collective-permute-done | bytes 786464 | tf_op jit(solution)/shard_map/ppermute | solution.py:35
  101.5 5.4 %fusion.8.gram_ref = f32[128,128]{1,0:T(8,128)} fusion(f32[128,128]{1,0:T(8,128)S(1)} %fusion, bf16[128,32768]{1,0:T(8,128)(2,1)} %rows_hbm.1), kind=kOutput, calls=%fused_computation.8 | convolution fusion | flops 536887296 | bytes 4325376 | tf_op jit(solution)/shard_map/dot_general | solution.py:415
  106.8 5.8 %prepare.1 = (f32[8,32,16,128]{3,2,1,0:T(8,128)}, bf16[8,128,96]{2,1,0:T(8,128)(2,1)}) custom-call(f32[128,128]{1,0:T(8,128)} %fusion.8.gram_ref, f32[8,16,16]{2,1,0:T(8,128)} %inverse_ref.1), custom_call_target="tpu_custom_call" | custom-call | tf_op jit(solution)/shard_map/prepare/pallas_call | solution.py:115
  113.3 4.1 %passes.1 = (f32[128,128]{1,0:T(8,128)}, bf16[16,136,128]{2,1,0:T(8,128)(2,1)}, f32[1,128]{1,0:T(1,128)}) custom-call(s32[1]{0:T(128)} %bitcast.where, f32[32,128]{1,0:T(8,128)} %get-tuple-element.26.start0, f32[32,128]{1,0:T(8,128)} %copy-done.1, f32[32,128]{1,0:T(8,128)} %copy-done.2, f32[32,128]{1,0:T(8,128)} %copy-done.3, s32[1,128]{1,0:T(1,128)} %bitcast.17, ...), custom_call_target="tpu_custom_call" | custom-call | tf_op jit(solution)/shard_map/passes/pallas_call | solution.py:209
  117.4 7.2 %all-to-all-start.2 = ((bf16[16,136,128]{2,1,0:T(8,128)(2,1)}), bf16[16,136,128]{2,1,0:T(8,128)(2,1)}, u32[]{:S(2)}, u32[]{:S(2)}) async-start(bf16[16,136,128]{2,1,0:T(8,128)(2,1)} %get-tuple-element.32), calls=%async_computation.2 | async-start | bytes 1114112 | tf_op jit(solution)/shard_map/all_to_all | solution.py:464
  124.7 10.3 %all-to-all-done.2.refs_6_ = bf16[16,136,128]{2,1,0:T(8,128)(2,1)} async-done(((bf16[16,136,128]{2,1,0:T(8,128)(2,1)}), bf16[16,136,128]{2,1,0:T(8,128)(2,1)}, u32[]{:S(2)}, u32[]{:S(2)}) %all-to-all-start.2) | async-done | bytes 557088 | tf_op jit(solution)/shard_map/all_to_all | solution.py:464
  135.0 3.0 %delta_first.1 = (bf16[520,128]{1,0:T(8,128)(2,1)S(1)}, bf16[128,2304]{1,0:T(8,128)(2,1)S(1)}, f32[1,128]{1,0:T(1,128)S(1)}) custom-call(s32[1]{0:T(128)} %bitcast.where, bf16[512,2048]{1,0:T(8,128)(2,1)S(1)} %bitcast.13, bf16[512,2048]{1,0:T(8,128)(2,1)} %collective-permute-done.refs_1_, bf16[320,2048]{1,0:T(8,128)(2,1)S(1)} %collective-permute-done.1.refs_2_, ...), custom_call_target="tpu_custom_call" | custom-call | tf_op jit(solution)/shard_map/delta_first/pallas_call | solution.py:347
  140.0 2.5 %collective-permute-start.20 = (bf16[520,128]{1,0:T(8,128)(2,1)S(1)}, bf16[520,128]{1,0:T(8,128)(2,1)S(1)}, u32[]{:S(2)}, u32[]{:S(2)}) collective-permute-start(bf16[520,128]{1,0:T(8,128)(2,1)S(1)} %delta_next.3), channel_id=1, source_target_pairs={{0,64},{64,128},{128,192},{192,0},{1,65},{65,129},{129,193},{193,1... | collective-permute-start | bytes 399368 | tf_op jit(solution)/shard_map/ppermute | solution.py:35
  146.2 3.6 %collective-permute-start.18 = (bf16[520,128]{1,0:T(8,128)(2,1)S(1)}, bf16[520,128]{1,0:T(8,128)(2,1)S(1)}, u32[]{:S(2)}, u32[]{:S(2)}) collective-permute-start(bf16[520,128]{1,0:T(8,128)(2,1)S(1)} %get-tuple-element.35), channel_id=1, source_target_pairs={{0,128},{64,192},{128,0},{192,64},{1,129},{65,193},{129,1},{193,65... | collective-permute-start | bytes 399368 | tf_op jit(solution)/shard_map/ppermute | solution.py:35
  151.1 7.0 %collective-permute-done.22 = f32[128]{0:T(128)S(1)} collective-permute-done((f32[128]{0:T(128)S(1)}, f32[128]{0:T(128)S(1)}, u32[]{:S(2)}, u32[]{:S(2)}) %collective-permute-start.22) | collective-permute-done | bytes 544 | tf_op jit(solution)/shard_map/ppermute | solution.py:35
  (65 shorter events, 27.3 us)
Async XLA Ops:
  3.7 38.0 %all-to-all-start = ((bf16[16,32,2048]{2,1,0:T(8,128)(2,1)}), bf16[16,32,2048]{2,1,0:T(8,128)(2,1)S(1)}, u32[]{:S(2)}, u32[]{:S(2)}) async-start(bf16[16,32,2048]{2,1,0:T(8,128)(2,1)} %pack.1), calls=%async_computation | async-start | bytes 4194304 | tf_op jit(solution)/shard_map/all_to_all | solution.py:430
  11.4 10.9 %collective-permute-start.3 = (bf16[512,128]{1,0:T(8,128)(2,1)S(1)}, bf16[512,128]{1,0:T(8,128)(2,1)S(1)}, u32[]{:S(2)}, u32[]{:S(2)}) collective-permute-start(bf16[512,128]{1,0:T(8,128)(2,1)S(1)} %copy-done), channel_id=1, source_target_pairs={{0,64},{64,128},{128,192},{192,0},{1,65},{65,129},{129,193},{193,1... | collective-permute-start | bytes 393224 | tf_op jit(solution)/shard_map/ppermute | solution.py:35
  14.7 10.3 %collective-permute-start.7 = (bf16[512,128]{1,0:T(8,128)(2,1)S(1)}, bf16[512,128]{1,0:T(8,128)(2,1)S(1)}, u32[]{:S(2)}, u32[]{:S(2)}) collective-permute-start(bf16[512,128]{1,0:T(8,128)(2,1)S(1)} %copy-done), channel_id=1, source_target_pairs={{0,192},{64,0},{128,64},{192,128},{1,193},{65,1},{129,65},{193,129... | collective-permute-start | bytes 393224 | tf_op jit(solution)/shard_map/ppermute | solution.py:35
  17.8 11.8 %collective-permute-start.2 = (bf16[512,128]{1,0:T(8,128)(2,1)S(1)}, bf16[512,128]{1,0:T(8,128)(2,1)S(1)}, u32[]{:S(2)}, u32[]{:S(2)}) collective-permute-start(bf16[512,128]{1,0:T(8,128)(2,1)S(1)} %copy-done), channel_id=1, source_target_pairs={{0,2},{2,0},{1,3},{3,1},{4,6},{6,4},{5,7},{7,5},{8,10},{10,8},{9,1... | collective-permute-start | bytes 393224 | tf_op jit(solution)/shard_map/ppermute | solution.py:35
  22.3 13.6 %collective-permute-start.4 = (bf16[512,128]{1,0:T(8,128)(2,1)S(1)}, bf16[512,128]{1,0:T(8,128)(2,1)S(1)}, u32[]{:S(2)}, u32[]{:S(2)}) collective-permute-start(bf16[512,128]{1,0:T(8,128)(2,1)S(1)} %collective-permute-done.3), channel_id=1, source_target_pairs={{0,2},{2,0},{1,3},{3,1},{4,6},{6,4},{5,7},{7,5},{8,10},{10,8},{9,1... | collective-permute-start | bytes 393224 | tf_op jit(solution)/shard_map/ppermute | solution.py:35
  24.6 9.3 %collective-permute-start.5 = (bf16[256,128]{1,0:T(8,128)(2,1)S(1)}, bf16[256,128]{1,0:T(8,128)(2,1)S(1)}, u32[]{:S(2)}, u32[]{:S(2)}) collective-permute-start(bf16[256,128]{1,0:T(8,128)(2,1)S(1)} %slice.29), channel_id=1, source_target_pairs={{0,64},{64,128},{128,192},{192,0},{1,65},{65,129},{129,193},{193,1... | collective-permute-start | bytes 196616 | tf_op jit(solution)/shard_map/ppermute | solution.py:35
  25.1 8.8 %collective-permute-start.8 = (bf16[256,128]{1,0:T(8,128)(2,1)S(1)}, bf16[256,128]{1,0:T(8,128)(2,1)S(1)}, u32[]{:S(2)}, u32[]{:S(2)}) collective-permute-start(bf16[256,128]{1,0:T(8,128)(2,1)S(1)} %slice.30), channel_id=1, source_target_pairs={{0,192},{64,0},{128,64},{192,128},{1,193},{65,1},{129,65},{193,129... | collective-permute-start | bytes 196616 | tf_op jit(solution)/shard_map/ppermute | solution.py:35
  28.8 10.1 %collective-permute-start.10 = (bf16[512,128]{1,0:T(8,128)(2,1)S(1)}, bf16[512,128]{1,0:T(8,128)(2,1)S(1)}, u32[]{:S(2)}, u32[]{:S(2)}) collective-permute-start(bf16[512,128]{1,0:T(8,128)(2,1)S(1)} %collective-permute-done.7), channel_id=1, source_target_pairs={{0,2},{2,0},{1,3},{3,1},{4,6},{6,4},{5,7},{7,5},{8,10},{10,8},{9,1... | collective-permute-start | bytes 393224 | tf_op jit(solution)/shard_map/ppermute | solution.py:35
  33.9 5.0 %collective-permute-start.9 = (bf16[256,128]{1,0:T(8,128)(2,1)S(1)}, bf16[256,128]{1,0:T(8,128)(2,1)S(1)}, u32[]{:S(2)}, u32[]{:S(2)}) collective-permute-start(bf16[256,128]{1,0:T(8,128)(2,1)S(1)} %collective-permute-done.8), channel_id=1, source_target_pairs={{0,2},{2,0},{1,3},{3,1},{4,6},{6,4},{5,7},{7,5},{8,10},{10,8},{9,1... | collective-permute-start | bytes 196616 | tf_op jit(solution)/shard_map/ppermute | solution.py:35
  45.3 22.7 %all-to-all-start.1 = ((f32[16,32,512]{2,1,0:T(8,128)}), f32[16,32,512]{2,1,0:T(8,128)}, u32[]{:S(2)}, u32[]{:S(2)}) async-start(f32[16,32,512]{2,1,0:T(8,128)} %bitcast.4), calls=%async_computation.1 | async-start | bytes 2097152 | tf_op jit(solution)/shard_map/all_to_all | solution.py:450
  53.7 31.9 %collective-permute-start.1 = (bf16[320,2048]{1,0:T(8,128)(2,1)}, bf16[320,2048]{1,0:T(8,128)(2,1)S(1)}, u32[]{:S(2)}, u32[]{:S(2)}) collective-permute-start(bf16[320,2048]{1,0:T(8,128)(2,1)} %bitcast.3), channel_id=1, source_target_pairs={{0,2},{2,0},{1,3},{3,1},{4,6},{6,4},{5,7},{7,5},{8,10},{10,8},{9,1... | collective-permute-start | bytes 3932168 | tf_op jit(solution)/shard_map/ppermute | solution.py:35
  55.0 80.0 %collective-permute-start = (bf16[512,2048]{1,0:T(8,128)(2,1)S(1)}, bf16[512,2048]{1,0:T(8,128)(2,1)}, u32[]{:S(2)}, u32[]{:S(2)}) collective-permute-start(bf16[512,2048]{1,0:T(8,128)(2,1)S(1)} %bitcast.11), channel_id=1, source_target_pairs={{0,1},{1,0},{2,3},{3,2},{4,5},{5,4},{6,7},{7,6},{8,9},{9,8},{10,11... | collective-permute-start | bytes 6291464 | tf_op jit(solution)/shard_map/ppermute | solution.py:35
  67.9 33.6 %collective-permute-start.12 = (bf16[192,2048]{1,0:T(8,128)(2,1)}, bf16[192,2048]{1,0:T(8,128)(2,1)}, u32[]{:S(2)}, u32[]{:S(2)}) collective-permute-start(bf16[192,2048]{1,0:T(8,128)(2,1)} %slice.25), channel_id=1, source_target_pairs={{0,2},{2,0},{1,3},{3,1},{4,6},{6,4},{5,7},{7,5},{8,10},{10,8},{9,1... | collective-permute-start | bytes 2359304 | tf_op jit(solution)/shard_map/ppermute | solution.py:35
  71.3 20.4 %collective-permute-start.15 = (f32[32,128]{1,0:T(8,128)}, f32[32,128]{1,0:T(8,128)S(1)}, u32[]{:S(2)}, u32[]{:S(2)}) collective-permute-start(f32[32,128]{1,0:T(8,128)} %get-tuple-element.27), channel_id=1, source_target_pairs={{0,1},{1,0},{2,3},{3,2},{4,5},{5,4},{6,7},{7,6},{8,9},{9,8},{10,11... | collective-permute-start | bytes 49160 | tf_op jit(solution)/shard_map/ppermute | solution.py:35
  85.6 49.4 %collective-permute-start.13 = (bf16[320,2048]{1,0:T(8,128)(2,1)S(1)}, bf16[320,2048]{1,0:T(8,128)(2,1)}, u32[]{:S(2)}, u32[]{:S(2)}) collective-permute-start(bf16[320,2048]{1,0:T(8,128)(2,1)S(1)} %collective-permute-done.1.refs_2_), channel_id=1, source_target_pairs={{0,1},{1,0},{2,3},{3,2},{4,5},{5,4},{6,7},{7,6},{8,9},{9,8},{10,11... | collective-permute-start | bytes 3932168 | tf_op jit(solution)/shard_map/ppermute | solution.py:35
  90.3 22.4 %collective-permute-start.16 = (f32[32,128]{1,0:T(8,128)S(1)}, f32[32,128]{1,0:T(8,128)S(1)}, u32[]{:S(2)}, u32[]{:S(2)}) collective-permute-start(f32[32,128]{1,0:T(8,128)S(1)} %copy-done.5), channel_id=1, source_target_pairs={{0,2},{2,0},{1,3},{3,1},{4,6},{6,4},{5,7},{7,5},{8,10},{10,8},{9,1... | collective-permute-start | bytes 49160 | tf_op jit(solution)/shard_map/ppermute | solution.py:35
  91.7 21.0 %collective-permute-start.17 = (f32[32,128]{1,0:T(8,128)S(1)}, f32[32,128]{1,0:T(8,128)S(1)}, u32[]{:S(2)}, u32[]{:S(2)}) collective-permute-start(f32[32,128]{1,0:T(8,128)S(1)} %copy-done.4), channel_id=1, source_target_pairs={{0,3},{1,2},{2,1},{3,0},{4,7},{5,6},{6,5},{7,4},{8,11},{9,10},{10,... | collective-permute-start | bytes 49160 | tf_op jit(solution)/shard_map/ppermute | solution.py:458
  101.5 33.5 %collective-permute-start.14 = (bf16[192,2048]{1,0:T(8,128)(2,1)}, bf16[192,2048]{1,0:T(8,128)(2,1)}, u32[]{:S(2)}, u32[]{:S(2)}) collective-permute-start(bf16[192,2048]{1,0:T(8,128)(2,1)} %collective-permute-done.12.refs_3_), channel_id=1, source_target_pairs={{0,1},{1,0},{2,3},{3,2},{4,5},{5,4},{6,7},{7,6},{8,9},{9,8},{10,11... | collective-permute-start | bytes 2359304 | tf_op jit(solution)/shard_map/ppermute | solution.py:35
  117.4 17.6 %all-to-all-start.2 = ((bf16[16,136,128]{2,1,0:T(8,128)(2,1)}), bf16[16,136,128]{2,1,0:T(8,128)(2,1)}, u32[]{:S(2)}, u32[]{:S(2)}) async-start(bf16[16,136,128]{2,1,0:T(8,128)(2,1)} %get-tuple-element.32), calls=%async_computation.2 | async-start | bytes 1114112 | tf_op jit(solution)/shard_map/all_to_all | solution.py:464
  124.7 25.1 %collective-permute-start.21 = (f32[128]{0:T(128)}, f32[128]{0:T(128)S(1)}, u32[]{:S(2)}, u32[]{:S(2)}) collective-permute-start(f32[128]{0:T(128)} %bitcast.18), channel_id=1, source_target_pairs={{0,1},{1,0},{2,3},{3,2},{4,5},{5,4},{6,7},{7,6},{8,9},{9,8},{10,11... | collective-permute-start | bytes 1544 | tf_op jit(solution)/shard_map/ppermute | solution.py:35
  140.0 20.6 %collective-permute-start.20 = (bf16[520,128]{1,0:T(8,128)(2,1)S(1)}, bf16[520,128]{1,0:T(8,128)(2,1)S(1)}, u32[]{:S(2)}, u32[]{:S(2)}) collective-permute-start(bf16[520,128]{1,0:T(8,128)(2,1)S(1)} %delta_next.3), channel_id=1, source_target_pairs={{0,64},{64,128},{128,192},{192,0},{1,65},{65,129},{129,193},{193,1... | collective-permute-start | bytes 399368 | tf_op jit(solution)/shard_map/ppermute | solution.py:35
  144.4 16.2 %collective-permute-start.19 = (bf16[520,128]{1,0:T(8,128)(2,1)S(1)}, bf16[520,128]{1,0:T(8,128)(2,1)S(1)}, u32[]{:S(2)}, u32[]{:S(2)}) collective-permute-start(bf16[520,128]{1,0:T(8,128)(2,1)S(1)} %delta_next.2), channel_id=1, source_target_pairs={{0,192},{64,0},{128,64},{192,128},{1,193},{65,1},{129,65},{193,129... | collective-permute-start | bytes 399368 | tf_op jit(solution)/shard_map/ppermute | solution.py:35
  146.2 14.5 %collective-permute-start.18 = (bf16[520,128]{1,0:T(8,128)(2,1)S(1)}, bf16[520,128]{1,0:T(8,128)(2,1)S(1)}, u32[]{:S(2)}, u32[]{:S(2)}) collective-permute-start(bf16[520,128]{1,0:T(8,128)(2,1)S(1)} %get-tuple-element.35), channel_id=1, source_target_pairs={{0,128},{64,192},{128,0},{192,64},{1,129},{65,193},{129,1},{193,65... | collective-permute-start | bytes 399368 | tf_op jit(solution)/shard_map/ppermute | solution.py:35
  149.8 8.3 %collective-permute-start.22 = (f32[128]{0:T(128)S(1)}, f32[128]{0:T(128)S(1)}, u32[]{:S(2)}, u32[]{:S(2)}) collective-permute-start(f32[128]{0:T(128)S(1)} %bitcast_maximum_fusion), channel_id=1, source_target_pairs={{0,2},{2,0},{1,3},{3,1},{4,6},{6,4},{5,7},{7,5},{8,10},{10,8},{9,1... | collective-permute-start | bytes 1544 | tf_op jit(solution)/shard_map/ppermute | solution.py:35
  (9 other events, 80.5 us)

commit v7 on v6

--- a/solution.py
+++ b/solution.py
@@ -92,38 +92,44 @@
     return first, second, third
 
 
-def prepare_kernel(gram_ref, inverse_ref, expanded_ref, wide_ref):
+def prepare_kernel(gram_ref, inverse_ref, expanded_ref, wide_ref, columns_ref):
     rows = gram_ref.shape[0]
-    _, size, _ = inverse_ref.shape
+    count, size, _ = inverse_ref.shape
     lanes = expanded_ref.shape[3]
-    b = pl.program_id(0)
-    low = pl.multiple_of(b * size, size)
-    high = pl.multiple_of(lax.rem(b + 1, pl.num_programs(0)) * size, size)
-    spot = lax.broadcasted_iota(jnp.int32, (rows, size), 0) == low + lax.broadcasted_iota(jnp.int32, (rows, size), 1)
-    picks = jnp.where(spot, 1.0, 0.0).astype(BF16)
-    sides = [jnp.dot(piece, picks, preferred_element_type=F32) for piece in three_pieces(COUPLING * gram_ref[...])]
-    exact = jnp.dot(gram_ref[pl.ds(high, size)], jnp.where(spot, 1.0, 0.0), precision=lax.Precision.HIGHEST, preferred_element_type=F32)
-    for k in range(size):
-        expanded_ref[0, k] = jnp.broadcast_to(inverse_ref[0, :, k:k + 1], (size, lanes))
-        expanded_ref[0, size + k] = COUPLING * jnp.broadcast_to(exact[:, k:k + 1], (size, lanes))
-    wide_ref[0] = jnp.concatenate([sides[p].astype(BF16) for p in LEFT], axis=1)
+    blocks = rows // size
+    pieces = three_pieces(COUPLING * gram_ref[...])
+    for i in range(count):
+        b = pl.program_id(0) * count + i
+        low = pl.multiple_of(b * size, size)
+        high = pl.multiple_of(lax.rem(b + 1, blocks) * size, size)
+        spot = lax.broadcasted_iota(jnp.int32, (rows, size), 0) == low + lax.broadcasted_iota(jnp.int32, (rows, size), 1)
+        picks = jnp.where(spot, 1.0, 0.0).astype(BF16)
+        sides = [jnp.dot(piece, picks, preferred_element_type=F32) for piece in pieces]
+        columns_ref[i] = (sides[0] + sides[1]) + sides[2]
+        ahead = columns_ref[i, pl.ds(high, size)]
+        for k in range(size):
+            expanded_ref[i, k] = jnp.broadcast_to(inverse_ref[i, :, k:k + 1], (size, lanes))
+            expanded_ref[i, size + k] = jnp.broadcast_to(ahead[:, k:k + 1], (size, lanes))
+        wide_ref[i] = jnp.concatenate([sides[p].astype(BF16) for p in LEFT], axis=1)
 
 
 def prepare(gram, inverse, lanes):
     rows = gram.shape[0]
     blocks, size, _ = inverse.shape
+    some = 2
     return pl.pallas_call(
         prepare_kernel,
-        grid=(blocks,),
-        in_specs=[pl.BlockSpec((rows, rows), lambda b: (0, 0)), pl.BlockSpec((1, size, size), lambda b: (b, 0, 0))],
+        grid=(blocks // some,),
+        in_specs=[pl.BlockSpec((rows, rows), lambda b: (0, 0)), pl.BlockSpec((some, size, size), lambda b: (b, 0, 0))],
         out_specs=[
-            pl.BlockSpec((1, 2 * size, size, lanes), lambda b: (b, 0, 0, 0)),
-            pl.BlockSpec((1, rows, len(LEFT) * size), lambda b: (b, 0, 0)),
+            pl.BlockSpec((some, 2 * size, size, lanes), lambda b: (b, 0, 0, 0)),
+            pl.BlockSpec((some, rows, len(LEFT) * size), lambda b: (b, 0, 0)),
         ],
         out_shape=[
             jax.ShapeDtypeStruct((blocks, 2 * size, size, lanes), F32),
             jax.ShapeDtypeStruct((blocks, rows, len(LEFT) * size), BF16),
         ],
+        scratch_shapes=[pltpu.VMEM((some, rows, size), F32)],
         compiler_params=FULL,
         name="prepare",
     )(gram, inverse)
@@ -439,7 +445,7 @@
         pairs.append(jnp.concatenate([piece, other], axis=1))
     by_pair = jnp.concatenate(pairs, axis=0)
     by_all = jnp.concatenate([by_pair, shifted(by_pair, CORE, 1)], axis=1)
-    middle = samples.shape[1] // 2
+    middle = samples.shape[1] * 3 // 4
     gram_head = self_product(samples[:, :middle])
 
     flat = quarter.reshape(members * part, planes * depth)
@@ -450,7 +456,8 @@
     partial = lax.all_to_all(partial.reshape(members, part, quarters * width), PLANE, split_axis=0, concat_axis=0, tiled=True)
     across = shifted(flat, CORE, 1)
     diagonal_a = shifted(beside_a, CORE, 1)
-    gram = gram_head + self_product(samples[:, middle:])
+    gram_rest = lax.optimization_barrier(self_product(samples[:, middle:]))
+    gram = gram_head + gram_rest
     ready = prepare(gram, inverse, width)
     partial, late = lax.optimization_barrier((partial, late[early:]))
     own_piece, by_core, by_line, by_both = gathered(partial)
@@ -474,7 +481,7 @@
     far = planes // 2
     sent, turned, gap = first_delta(where, held, steps, planes, far)
     came = [shifted(sent, ZH, planes - far)]
-    for k in range(1, planes):
+    for k in reversed(range(1, planes)):
         if k != far:
             sent = next_delta(held, turned, gap, planes, k)
             came.append(shifted(sent, ZH, planes - k))

time: 163 us -> 161 us (0.988)
  Pallas kernels: 24.6 us -> 22.7 us
    pallas_call x1, Pallas kernels: 5.84 us -> 3.97 us  [prepare(): pl.pallas_call(prepare_kernel, grid=(blocks // some,), in_specs=[pl.Block...]
  transfers between devices with their start and end apart: 26 -> 26, of which waited for: 10 -> 11; matrix products, arithmetic and copies ran while one was open for 8% -> 8% of each run, Pallas kernels for 13% -> 12%
where the time goes in v7:
time: 161 us; the launch traced here: 158 us
  waiting for transfers between devices  65.5 us (41%)
  starting transfers between devices  52.1 us (32%)
  Pallas kernels  22.7 us (14%)
  matrix products  13.4 us (8%)
  local copies, waits for them, and re-layouts  2.8 us (2%)
    ppermute x22, waiting for transfers between devices, shifted(): lax.ppermute(value, axis, [(i, (i + by) % size) for i in range(size)])  43.2 us
    ppermute x22, starting transfers between devices, shifted(): lax.ppermute(value, axis, [(i, (i + by) % size) for i in range(size)])  29.4 us
    all_to_all x1, waiting for transfers between devices, round_of_ascent(): lax.all_to_all(partial.reshape(members, part, quarters * width), PLANE, s...  11.9 us
    all_to_all x1, waiting for transfers between devices, round_of_ascent(): lax.all_to_all(steps, PLANE, split_axis=0, concat_axis=0, tiled=True)  10.3 us
    dot_general x2, matrix products, self_product(): lax.dot_general(value, value, (((1,), (1,)), ((), ())), preferred_element...  9.96 us
    all_to_all x1, starting transfers between devices, round_of_ascent(): lax.all_to_all(packed, PLANE, split_axis=0, concat_axis=0, tiled=True)  7.62 us
    all_to_all x1, starting transfers between devices, round_of_ascent(): lax.all_to_all(steps, PLANE, split_axis=0, concat_axis=0, tiled=True)  7.24 us
    all_to_all x1, starting transfers between devices, round_of_ascent(): lax.all_to_all(partial.reshape(members, part, quarters * width), PLANE, s...  7.23 us
  transfers between devices with their start and end apart: 26, of which 11 were waited for; matrix products, arithmetic and copies ran while one was open for 8% of the time, Pallas kernels for 12%

profile of v7, /device:TPU:2, one launch (start us, length us, event | category | flops | bytes accessed | tf_op | source)
XLA Modules:
  0.0 158.0 jit_solution(3070741439645754232)
XLA Ops:
  0.6 3.1 %pack.1 = bf16[16,32,2048]{2,1,0:T(8,128)(2,1)} custom-call(s32[1]{0:T(128)} %bitcast.where, s32[1]{0:T(128)} %bitcast.1.plane, bf16[128,32768]{1,0:T(8,128)(2,1)} %rows_hbm.1), custom_call_target="tpu_custom_call" | custom-call | tf_op jit(solution)/shard_map/pack/pallas_call | solution.py:72
  3.7 7.6 %all-to-all-start = ((bf16[16,32,2048]{2,1,0:T(8,128)(2,1)}), bf16[16,32,2048]{2,1,0:T(8,128)(2,1)S(1)}, u32[]{:S(2)}, u32[]{:S(2)}) async-start(bf16[16,32,2048]{2,1,0:T(8,128)(2,1)} %pack.1), calls=%async_computation | async-start | bytes 4194304 | tf_op jit(solution)/shard_map/all_to_all | solution.py:436
  11.4 3.3 %collective-permute-start.3 = (bf16[512,128]{1,0:T(8,128)(2,1)S(1)}, bf16[512,128]{1,0:T(8,128)(2,1)S(1)}, u32[]{:S(2)}, u32[]{:S(2)}) collective-permute-start(bf16[512,128]{1,0:T(8,128)(2,1)S(1)} %copy-done), channel_id=1, source_target_pairs={{0,64},{64,128},{128,192},{192,0},{1,65},{65,129},{129,193},{193,1... | collective-permute-start | bytes 393224 | tf_op jit(solution)/shard_map/ppermute | solution.py:35
  14.7 3.1 %collective-permute-start.7 = (bf16[512,128]{1,0:T(8,128)(2,1)S(1)}, bf16[512,128]{1,0:T(8,128)(2,1)S(1)}, u32[]{:S(2)}, u32[]{:S(2)}) collective-permute-start(bf16[512,128]{1,0:T(8,128)(2,1)S(1)} %copy-done), channel_id=1, source_target_pairs={{0,192},{64,0},{128,64},{192,128},{1,193},{65,1},{129,65},{193,129... | collective-permute-start | bytes 393224 | tf_op jit(solution)/shard_map/ppermute | solution.py:35
  18.9 3.4 %collective-permute-done.3 = bf16[512,128]{1,0:T(8,128)(2,1)S(1)} collective-permute-done((bf16[512,128]{1,0:T(8,128)(2,1)S(1)}, bf16[512,128]{1,0:T(8,128)(2,1)S(1)}, u32[]{:S(2)}, u32[]{:S(2)}) %collective-permute-start.3) | collective-permute-done | bytes 131104 | tf_op jit(solution)/shard_map/ppermute | solution.py:35
  22.3 2.3 %collective-permute-start.4 = (bf16[512,128]{1,0:T(8,128)(2,1)S(1)}, bf16[512,128]{1,0:T(8,128)(2,1)S(1)}, u32[]{:S(2)}, u32[]{:S(2)}) collective-permute-start(bf16[512,128]{1,0:T(8,128)(2,1)S(1)} %collective-permute-done.3), channel_id=1, source_target_pairs={{0,2},{2,0},{1,3},{3,1},{4,6},{6,4},{5,7},{7,5},{8,10},{10,8},{9,1... | collective-permute-start | bytes 393224 | tf_op jit(solution)/shard_map/ppermute | solution.py:35
  25.1 3.7 %collective-permute-start.8 = (bf16[256,128]{1,0:T(8,128)(2,1)S(1)}, bf16[256,128]{1,0:T(8,128)(2,1)S(1)}, u32[]{:S(2)}, u32[]{:S(2)}) collective-permute-start(bf16[256,128]{1,0:T(8,128)(2,1)S(1)} %slice.30), channel_id=1, source_target_pairs={{0,192},{64,0},{128,64},{192,128},{1,193},{65,1},{129,65},{193,129... | collective-permute-start | bytes 196616 | tf_op jit(solution)/shard_map/ppermute | solution.py:35
  29.6 4.2 %collective-permute-done.5 = bf16[256,128]{1,0:T(8,128)(2,1)S(1)} collective-permute-done((bf16[256,128]{1,0:T(8,128)(2,1)S(1)}, bf16[256,128]{1,0:T(8,128)(2,1)S(1)}, u32[]{:S(2)}, u32[]{:S(2)}) %collective-permute-start.5) | collective-permute-done | bytes 65568 | tf_op jit(solution)/shard_map/ppermute | solution.py:35
  35.9 2.2 %collective-permute-done.6 = bf16[256,128]{1,0:T(8,128)(2,1)S(1)} collective-permute-done((bf16[256,128]{1,0:T(8,128)(2,1)S(1)}, bf16[256,128]{1,0:T(8,128)(2,1)S(1)}, u32[]{:S(2)}, u32[]{:S(2)}) %collective-permute-start.6) | collective-permute-done | bytes 65568 | tf_op jit(solution)/shard_map/ppermute | solution.py:35
  39.0 2.8 %collective-permute-done.11 = bf16[2048,256]{1,0:T(8,128)(2,1)} collective-permute-done((bf16[2048,256]{1,0:T(8,128)(2,1)S(1)}, bf16[2048,256]{1,0:T(8,128)(2,1)}, u32[]{:S(2)}, u32[]{:S(2)}) %collective-permute-start.11) | collective-permute-done | bytes 1048608 | tf_op jit(solution)/shard_map/ppermute | solution.py:35
  41.8 3.5 %fusion.2 = f32[512,512]{1,0:T(8,128)} fusion(bf16[512,2048]{1,0:T(8,128)(2,1)S(1)} %bitcast.10, bf16[2048,256]{1,0:T(8,128)(2,1)} %collective-permute-done.11, bf16[2048,256]{1,0:T(8,128)(2,1)S(1)} %maximum_dynamic-update-slice_fusion), kind=kOutput, calls=%fused_computation.2 | convolution fusion | flops 1077936128 | bytes 5242880 | tf_op jit(solution)/shard_map/dot_general | solution.py:454
  45.3 7.2 %all-to-all-start.1 = ((f32[16,32,512]{2,1,0:T(8,128)}), f32[16,32,512]{2,1,0:T(8,128)}, u32[]{:S(2)}, u32[]{:S(2)}) async-start(f32[16,32,512]{2,1,0:T(8,128)} %bitcast.4), calls=%async_computation.1 | async-start | bytes 2097152 | tf_op jit(solution)/shard_map/all_to_all | solution.py:456
  56.0 11.9 %all-to-all-done.1.parts_hbm = f32[16,32,512]{2,1,0:T(8,128)} async-done(((f32[16,32,512]{2,1,0:T(8,128)}), f32[16,32,512]{2,1,0:T(8,128)}, u32[]{:S(2)}, u32[]{:S(2)}) %all-to-all-start.1) | async-done | bytes 1048608 | tf_op jit(solution)/shard_map/all_to_all | solution.py:456
  71.4 14.2 %collective-permute-done.1.refs_2_ = bf16[320,2048]{1,0:T(8,128)(2,1)S(1)} collective-permute-done((bf16[320,2048]{1,0:T(8,128)(2,1)}, bf16[320,2048]{1,0:T(8,128)(2,1)S(1)}, u32[]{:S(2)}, u32[]{:S(2)}) %collective-permute-start.1) | collective-permute-done | bytes 1310752 | tf_op jit(solution)/shard_map/ppermute | solution.py:35
  85.6 2.9 %fusion.6 = f32[128,128]{1,0:T(8,128)S(1)} fusion(bf16[128,32768]{1,0:T(8,128)(2,1)} %rows_hbm.1), kind=kOutput, calls=%fused_computation.6 | convolution fusion | flops 268435456 | bytes 2162688 | tf_op jit(solution)/shard_map/dot_general | solution.py:421
  90.7 10.8 %collective-permute-done.12.refs_3_ = bf16[192,2048]{1,0:T(8,128)(2,1)} collective-permute-done((bf16[192,2048]{1,0:T(8,128)(2,1)}, bf16[192,2048]{1,0:T(8,128)(2,1)}, u32[]{:S(2)}, u32[]{:S(2)}) %collective-permute-start.12) | collective-permute-done | bytes 786464 | tf_op jit(solution)/shard_map/ppermute | solution.py:35
  101.5 7.0 %fusion.8.gram_ref = f32[128,128]{1,0:T(8,128)} fusion(f32[128,128]{1,0:T(8,128)S(1)} %fusion.6, bf16[128,32768]{1,0:T(8,128)(2,1)} %rows_hbm.1), kind=kOutput, calls=%fused_computation.8 | convolution fusion | flops 805322752 | bytes 6422528 | tf_op jit(solution)/shard_map/dot_general | solution.py:421
  108.5 4.0 %prepare.1 = (f32[8,32,16,128]{3,2,1,0:T(8,128)}, bf16[8,128,96]{2,1,0:T(8,128)(2,1)}) custom-call(f32[128,128]{1,0:T(8,128)} %fusion.8.gram_ref, f32[8,16,16]{2,1,0:T(8,128)} %inverse_ref.1), custom_call_target="tpu_custom_call" | custom-call | tf_op jit(solution)/shard_map/prepare/pallas_call | solution.py:120
  113.1 4.1 %passes.1 = (f32[128,128]{1,0:T(8,128)}, bf16[16,136,128]{2,1,0:T(8,128)(2,1)}, f32[1,128]{1,0:T(1,128)}) custom-call(s32[1]{0:T(128)} %bitcast.where, f32[32,128]{1,0:T(8,128)} %get-tuple-element.26.start0, f32[32,128]{1,0:T(8,128)} %copy-done.1, f32[32,128]{1,0:T(8,128)} %copy-done.2, f32[32,128]{1,0:T(8,128)} %copy-done.3, s32[1,128]{1,0:T(1,128)} %bitcast.17, ...), custom_call_target="tpu_custom_call" | custom-call | tf_op jit(solution)/shard_map/passes/pallas_call | solution.py:215
  117.2 7.2 %all-to-all-start.2 = ((bf16[16,136,128]{2,1,0:T(8,128)(2,1)}), bf16[16,136,128]{2,1,0:T(8,128)(2,1)}, u32[]{:S(2)}, u32[]{:S(2)}) async-start(bf16[16,136,128]{2,1,0:T(8,128)(2,1)} %get-tuple-element.32), calls=%async_computation.2 | async-start | bytes 1114112 | tf_op jit(solution)/shard_map/all_to_all | solution.py:471
  124.5 10.3 %all-to-all-done.2.refs_6_ = bf16[16,136,128]{2,1,0:T(8,128)(2,1)} async-done(((bf16[16,136,128]{2,1,0:T(8,128)(2,1)}), bf16[16,136,128]{2,1,0:T(8,128)(2,1)}, u32[]{:S(2)}, u32[]{:S(2)}) %all-to-all-start.2) | async-done | bytes 557088 | tf_op jit(solution)/shard_map/all_to_all | solution.py:471
  134.8 3.0 %delta_first.1 = (bf16[520,128]{1,0:T(8,128)(2,1)S(1)}, bf16[128,2304]{1,0:T(8,128)(2,1)S(1)}, f32[1,128]{1,0:T(1,128)S(1)}) custom-call(s32[1]{0:T(128)} %bitcast.where, bf16[512,2048]{1,0:T(8,128)(2,1)S(1)} %bitcast.13, bf16[512,2048]{1,0:T(8,128)(2,1)} %collective-permute-done.refs_1_, bf16[320,2048]{1,0:T(8,128)(2,1)S(1)} %collective-permute-done.1.refs_2_, ...), custom_call_target="tpu_custom_call" | custom-call | tf_op jit(solution)/shard_map/delta_first/pallas_call | solution.py:353
  144.8 3.6 %collective-permute-start.18 = (bf16[520,128]{1,0:T(8,128)(2,1)S(1)}, bf16[520,128]{1,0:T(8,128)(2,1)S(1)}, u32[]{:S(2)}, u32[]{:S(2)}) collective-permute-start(bf16[520,128]{1,0:T(8,128)(2,1)S(1)} %get-tuple-element.35), channel_id=1, source_target_pairs={{0,128},{64,192},{128,0},{192,64},{1,129},{65,193},{129,1},{193,65... | collective-permute-start | bytes 399368 | tf_op jit(solution)/shard_map/ppermute | solution.py:35
  149.8 3.3 %collective-permute-done.22 = f32[128]{0:T(128)S(1)} collective-permute-done((f32[128]{0:T(128)S(1)}, f32[128]{0:T(128)S(1)}, u32[]{:S(2)}, u32[]{:S(2)}) %collective-permute-start.22) | collective-permute-done | bytes 544 | tf_op jit(solution)/shard_map/ppermute | solution.py:35
  (65 shorter events, 28.2 us)
Async XLA Ops:
  3.7 38.0 %all-to-all-start = ((bf16[16,32,2048]{2,1,0:T(8,128)(2,1)}), bf16[16,32,2048]{2,1,0:T(8,128)(2,1)S(1)}, u32[]{:S(2)}, u32[]{:S(2)}) async-start(bf16[16,32,2048]{2,1,0:T(8,128)(2,1)} %pack.1), calls=%async_computation | async-start | bytes 4194304 | tf_op jit(solution)/shard_map/all_to_all | solution.py:436
  11.4 10.9 %collective-permute-start.3 = (bf16[512,128]{1,0:T(8,128)(2,1)S(1)}, bf16[512,128]{1,0:T(8,128)(2,1)S(1)}, u32[]{:S(2)}, u32[]{:S(2)}) collective-permute-start(bf16[512,128]{1,0:T(8,128)(2,1)S(1)} %copy-done), channel_id=1, source_target_pairs={{0,64},{64,128},{128,192},{192,0},{1,65},{65,129},{129,193},{193,1... | collective-permute-start | bytes 393224 | tf_op jit(solution)/shard_map/ppermute | solution.py:35
  14.7 10.3 %collective-permute-start.7 = (bf16[512,128]{1,0:T(8,128)(2,1)S(1)}, bf16[512,128]{1,0:T(8,128)(2,1)S(1)}, u32[]{:S(2)}, u32[]{:S(2)}) collective-permute-start(bf16[512,128]{1,0:T(8,128)(2,1)S(1)} %copy-done), channel_id=1, source_target_pairs={{0,192},{64,0},{128,64},{192,128},{1,193},{65,1},{129,65},{193,129... | collective-permute-start | bytes 393224 | tf_op jit(solution)/shard_map/ppermute | solution.py:35
  17.8 11.8 %collective-permute-start.2 = (bf16[512,128]{1,0:T(8,128)(2,1)S(1)}, bf16[512,128]{1,0:T(8,128)(2,1)S(1)}, u32[]{:S(2)}, u32[]{:S(2)}) collective-permute-start(bf16[512,128]{1,0:T(8,128)(2,1)S(1)} %copy-done), channel_id=1, source_target_pairs={{0,2},{2,0},{1,3},{3,1},{4,6},{6,4},{5,7},{7,5},{8,10},{10,8},{9,1... | collective-permute-start | bytes 393224 | tf_op jit(solution)/shard_map/ppermute | solution.py:35
  22.3 13.6 %collective-permute-start.4 = (bf16[512,128]{1,0:T(8,128)(2,1)S(1)}, bf16[512,128]{1,0:T(8,128)(2,1)S(1)}, u32[]{:S(2)}, u32[]{:S(2)}) collective-permute-start(bf16[512,128]{1,0:T(8,128)(2,1)S(1)} %collective-permute-done.3), channel_id=1, source_target_pairs={{0,2},{2,0},{1,3},{3,1},{4,6},{6,4},{5,7},{7,5},{8,10},{10,8},{9,1... | collective-permute-start | bytes 393224 | tf_op jit(solution)/shard_map/ppermute | solution.py:35
  24.6 9.3 %collective-permute-start.5 = (bf16[256,128]{1,0:T(8,128)(2,1)S(1)}, bf16[256,128]{1,0:T(8,128)(2,1)S(1)}, u32[]{:S(2)}, u32[]{:S(2)}) collective-permute-start(bf16[256,128]{1,0:T(8,128)(2,1)S(1)} %slice.29), channel_id=1, source_target_pairs={{0,64},{64,128},{128,192},{192,0},{1,65},{65,129},{129,193},{193,1... | collective-permute-start | bytes 196616 | tf_op jit(solution)/shard_map/ppermute | solution.py:35
  25.1 8.8 %collective-permute-start.8 = (bf16[256,128]{1,0:T(8,128)(2,1)S(1)}, bf16[256,128]{1,0:T(8,128)(2,1)S(1)}, u32[]{:S(2)}, u32[]{:S(2)}) collective-permute-start(bf16[256,128]{1,0:T(8,128)(2,1)S(1)} %slice.30), channel_id=1, source_target_pairs={{0,192},{64,0},{128,64},{192,128},{1,193},{65,1},{129,65},{193,129... | collective-permute-start | bytes 196616 | tf_op jit(solution)/shard_map/ppermute | solution.py:35
  28.8 10.1 %collective-permute-start.10 = (bf16[512,128]{1,0:T(8,128)(2,1)S(1)}, bf16[512,128]{1,0:T(8,128)(2,1)S(1)}, u32[]{:S(2)}, u32[]{:S(2)}) collective-permute-start(bf16[512,128]{1,0:T(8,128)(2,1)S(1)} %collective-permute-done.7), channel_id=1, source_target_pairs={{0,2},{2,0},{1,3},{3,1},{4,6},{6,4},{5,7},{7,5},{8,10},{10,8},{9,1... | collective-permute-start | bytes 393224 | tf_op jit(solution)/shard_map/ppermute | solution.py:35
  33.9 5.0 %collective-permute-start.9 = (bf16[256,128]{1,0:T(8,128)(2,1)S(1)}, bf16[256,128]{1,0:T(8,128)(2,1)S(1)}, u32[]{:S(2)}, u32[]{:S(2)}) collective-permute-start(bf16[256,128]{1,0:T(8,128)(2,1)S(1)} %collective-permute-done.8), channel_id=1, source_target_pairs={{0,2},{2,0},{1,3},{3,1},{4,6},{6,4},{5,7},{7,5},{8,10},{10,8},{9,1... | collective-permute-start | bytes 196616 | tf_op jit(solution)/shard_map/ppermute | solution.py:35
  45.3 22.7 %all-to-all-start.1 = ((f32[16,32,512]{2,1,0:T(8,128)}), f32[16,32,512]{2,1,0:T(8,128)}, u32[]{:S(2)}, u32[]{:S(2)}) async-start(f32[16,32,512]{2,1,0:T(8,128)} %bitcast.4), calls=%async_computation.1 | async-start | bytes 2097152 | tf_op jit(solution)/shard_map/all_to_all | solution.py:456
  53.7 31.9 %collective-permute-start.1 = (bf16[320,2048]{1,0:T(8,128)(2,1)}, bf16[320,2048]{1,0:T(8,128)(2,1)S(1)}, u32[]{:S(2)}, u32[]{:S(2)}) collective-permute-start(bf16[320,2048]{1,0:T(8,128)(2,1)} %bitcast.3), channel_id=1, source_target_pairs={{0,2},{2,0},{1,3},{3,1},{4,6},{6,4},{5,7},{7,5},{8,10},{10,8},{9,1... | collective-permute-start | bytes 3932168 | tf_op jit(solution)/shard_map/ppermute | solution.py:35
  55.0 79.8 %collective-permute-start = (bf16[512,2048]{1,0:T(8,128)(2,1)S(1)}, bf16[512,2048]{1,0:T(8,128)(2,1)}, u32[]{:S(2)}, u32[]{:S(2)}) collective-permute-start(bf16[512,2048]{1,0:T(8,128)(2,1)S(1)} %bitcast.11), channel_id=1, source_target_pairs={{0,1},{1,0},{2,3},{3,2},{4,5},{5,4},{6,7},{7,6},{8,9},{9,8},{10,11... | collective-permute-start | bytes 6291464 | tf_op jit(solution)/shard_map/ppermute | solution.py:35
  67.9 33.6 %collective-permute-start.12 = (bf16[192,2048]{1,0:T(8,128)(2,1)}, bf16[192,2048]{1,0:T(8,128)(2,1)}, u32[]{:S(2)}, u32[]{:S(2)}) collective-permute-start(bf16[192,2048]{1,0:T(8,128)(2,1)} %slice.25), channel_id=1, source_target_pairs={{0,2},{2,0},{1,3},{3,1},{4,6},{6,4},{5,7},{7,5},{8,10},{10,8},{9,1... | collective-permute-start | bytes 2359304 | tf_op jit(solution)/shard_map/ppermute | solution.py:35
  71.3 18.8 %collective-permute-start.15 = (f32[32,128]{1,0:T(8,128)}, f32[32,128]{1,0:T(8,128)S(1)}, u32[]{:S(2)}, u32[]{:S(2)}) collective-permute-start(f32[32,128]{1,0:T(8,128)} %get-tuple-element.27), channel_id=1, source_target_pairs={{0,1},{1,0},{2,3},{3,2},{4,5},{5,4},{6,7},{7,6},{8,9},{9,8},{10,11... | collective-permute-start | bytes 49160 | tf_op jit(solution)/shard_map/ppermute | solution.py:35
  85.6 49.3 %collective-permute-start.13 = (bf16[320,2048]{1,0:T(8,128)(2,1)S(1)}, bf16[320,2048]{1,0:T(8,128)(2,1)}, u32[]{:S(2)}, u32[]{:S(2)}) collective-permute-start(bf16[320,2048]{1,0:T(8,128)(2,1)S(1)} %collective-permute-done.1.refs_2_), channel_id=1, source_target_pairs={{0,1},{1,0},{2,3},{3,2},{4,5},{5,4},{6,7},{7,6},{8,9},{9,8},{10,11... | collective-permute-start | bytes 3932168 | tf_op jit(solution)/shard_map/ppermute | solution.py:35
  88.5 24.0 %collective-permute-start.16 = (f32[32,128]{1,0:T(8,128)S(1)}, f32[32,128]{1,0:T(8,128)S(1)}, u32[]{:S(2)}, u32[]{:S(2)}) collective-permute-start(f32[32,128]{1,0:T(8,128)S(1)} %copy-done.5), channel_id=1, source_target_pairs={{0,2},{2,0},{1,3},{3,1},{4,6},{6,4},{5,7},{7,5},{8,10},{10,8},{9,1... | collective-permute-start | bytes 49160 | tf_op jit(solution)/shard_map/ppermute | solution.py:35
  90.1 22.4 %collective-permute-start.17 = (f32[32,128]{1,0:T(8,128)S(1)}, f32[32,128]{1,0:T(8,128)S(1)}, u32[]{:S(2)}, u32[]{:S(2)}) collective-permute-start(f32[32,128]{1,0:T(8,128)S(1)} %copy-done.4), channel_id=1, source_target_pairs={{0,3},{1,2},{2,1},{3,0},{4,7},{5,6},{6,5},{7,4},{8,11},{9,10},{10,... | collective-permute-start | bytes 49160 | tf_op jit(solution)/shard_map/ppermute | solution.py:465
  101.5 33.3 %collective-permute-start.14 = (bf16[192,2048]{1,0:T(8,128)(2,1)}, bf16[192,2048]{1,0:T(8,128)(2,1)}, u32[]{:S(2)}, u32[]{:S(2)}) collective-permute-start(bf16[192,2048]{1,0:T(8,128)(2,1)} %collective-permute-done.12.refs_3_), channel_id=1, source_target_pairs={{0,1},{1,0},{2,3},{3,2},{4,5},{5,4},{6,7},{7,6},{8,9},{9,8},{10,11... | collective-permute-start | bytes 2359304 | tf_op jit(solution)/shard_map/ppermute | solution.py:35
  117.2 17.6 %all-to-all-start.2 = ((bf16[16,136,128]{2,1,0:T(8,128)(2,1)}), bf16[16,136,128]{2,1,0:T(8,128)(2,1)}, u32[]{:S(2)}, u32[]{:S(2)}) async-start(bf16[16,136,128]{2,1,0:T(8,128)(2,1)} %get-tuple-element.32), calls=%async_computation.2 | async-start | bytes 1114112 | tf_op jit(solution)/shard_map/all_to_all | solution.py:471
  124.5 23.9 %collective-permute-start.21 = (f32[128]{0:T(128)}, f32[128]{0:T(128)S(1)}, u32[]{:S(2)}, u32[]{:S(2)}) collective-permute-start(f32[128]{0:T(128)} %bitcast.18), channel_id=1, source_target_pairs={{0,1},{1,0},{2,3},{3,2},{4,5},{5,4},{6,7},{7,6},{8,9},{9,8},{10,11... | collective-permute-start | bytes 1544 | tf_op jit(solution)/shard_map/ppermute | solution.py:35
  139.8 15.8 %collective-permute-start.20 = (bf16[520,128]{1,0:T(8,128)(2,1)S(1)}, bf16[520,128]{1,0:T(8,128)(2,1)S(1)}, u32[]{:S(2)}, u32[]{:S(2)}) collective-permute-start(bf16[520,128]{1,0:T(8,128)(2,1)S(1)} %delta_next.3), channel_id=1, source_target_pairs={{0,192},{64,0},{128,64},{192,128},{1,193},{65,1},{129,65},{193,129... | collective-permute-start | bytes 399368 | tf_op jit(solution)/shard_map/ppermute | solution.py:35
  143.9 13.3 %collective-permute-start.19 = (bf16[520,128]{1,0:T(8,128)(2,1)S(1)}, bf16[520,128]{1,0:T(8,128)(2,1)S(1)}, u32[]{:S(2)}, u32[]{:S(2)}) collective-permute-start(bf16[520,128]{1,0:T(8,128)(2,1)S(1)} %delta_next.2), channel_id=1, source_target_pairs={{0,64},{64,128},{128,192},{192,0},{1,65},{65,129},{129,193},{193,1... | collective-permute-start | bytes 399368 | tf_op jit(solution)/shard_map/ppermute | solution.py:35
  144.8 12.4 %collective-permute-start.18 = (bf16[520,128]{1,0:T(8,128)(2,1)S(1)}, bf16[520,128]{1,0:T(8,128)(2,1)S(1)}, u32[]{:S(2)}, u32[]{:S(2)}) collective-permute-start(bf16[520,128]{1,0:T(8,128)(2,1)S(1)} %get-tuple-element.35), channel_id=1, source_target_pairs={{0,128},{64,192},{128,0},{192,64},{1,129},{65,193},{129,1},{193,65... | collective-permute-start | bytes 399368 | tf_op jit(solution)/shard_map/ppermute | solution.py:35
  148.4 4.7 %collective-permute-start.22 = (f32[128]{0:T(128)S(1)}, f32[128]{0:T(128)S(1)}, u32[]{:S(2)}, u32[]{:S(2)}) collective-permute-start(f32[128]{0:T(128)S(1)} %bitcast_maximum_fusion), channel_id=1, source_target_pairs={{0,2},{2,0},{1,3},{3,1},{4,6},{6,4},{5,7},{7,5},{8,10},{10,8},{9,1... | collective-permute-start | bytes 1544 | tf_op jit(solution)/shard_map/ppermute | solution.py:35
  (9 other events, 79.2 us)
